TPU v7x, 32 devices: a whole 2x2x4 slice. The times are simulated.
32 devices in a mesh: dp: 8 (over y, x, core), tensor: 4 (over z).
Axes of the slice: x: 2, y: 2, z: 4, core: 2. Of those that a mesh axis runs over, the one named last changes fastest.
Arguments:
- tokens: bfloat16 [8192, 2048], P(('dp', 'tensor')), may hold values from -6 to 6
- out_grad: bfloat16 [8192, 2048], P(('dp', 'tensor')), may hold values from -6 to 6
- segment_ids: int32 [8192], P('dp'), may hold values from 0 to 64, as said below
- positions: int32 [8192], P('dp'), may hold values from 0 to 1999, as said below
- norm1_gain: float32 [2048], replicated, may hold values from 0.1 to 1.9
- norm1_bias: float32 [2048], replicated, may hold values from -3 to 3
- norm2_gain: float32 [2048], replicated, may hold values from 0.1 to 1.9
- norm2_bias: float32 [2048], replicated, may hold values from -3 to 3
- qkv_weight: bfloat16 [2048, 8, 3, 256], P(None, 'tensor'), may hold values from -0.125 to 0.125
- qkv_bias: bfloat16 [8, 3, 256], P('tensor'), may hold values from -4 to 4
- out_weight: bfloat16 [8, 256, 2048], P('tensor'), may hold values from -0.75 to 0.75
- out_bias: bfloat16 [2048], replicated, may hold values from -3 to 3
- fc1_weight: bfloat16 [2048, 8192], P(None, 'tensor'), may hold values from -0.125 to 0.125
- fc1_bias: bfloat16 [8192], P('tensor'), may hold values from -3 to 3
- fc2_weight: bfloat16 [8192, 2048], P('tensor'), may hold values from -0.0625 to 0.0625
- fc2_bias: bfloat16 [2048], replicated, may hold values from -3 to 3
Outputs:
- block_out: bfloat16 [8192, 2048], P(('dp', 'tensor'))
- tokens_grad: bfloat16 [8192, 2048], P(('dp', 'tensor'))
- norm1_gain_grad: float32 [2048], replicated
- norm1_bias_grad: float32 [2048], replicated
- norm2_gain_grad: float32 [2048], replicated
- norm2_bias_grad: float32 [2048], replicated
- qkv_weight_grad: float32 [2048, 8, 3, 256], P(None, 'tensor')
- qkv_bias_grad: float32 [8, 3, 256], P('tensor')
- out_weight_grad: float32 [8, 256, 2048], P('tensor')
- out_bias_grad: float32 [2048], replicated
- fc1_weight_grad: float32 [2048, 8192], P(None, 'tensor')
- fc1_bias_grad: float32 [8192], P('tensor')
- fc2_weight_grad: float32 [8192, 2048], P('tensor')
- fc2_bias_grad: float32 [2048], replicated
Inputs may be any that keep to these rules, and one draw needn't show every extreme that they name: `segment_ids`: never falling along the tokens; the tokens of one document share one number. A document has 1 to 2000 tokens; one document of exactly 2000 tokens ends on token 4096. The last document carries the largest number. `positions`: the token's index within its document, 0 at the document's first token.
All inputs are finite; a program needn't handle non-finite values.
Results may differ from a plain program's by a relative error of at most 0.0065.
The roundings to bfloat16 on the way count: a program that leaves them out, or rounds other values in their place, can miss the bound.
Values may be sent and summed in bfloat16 or wider, within the bound.
A program may use at most 256 MiB of HBM per device.

v0:
```python
import math

import jax
import jax.numpy as jnp
from jax import lax
from jax.sharding import PartitionSpec as P

ROT = 64
MOST = 2000


epsilon = 1e-05


def shifted(x, axis, by):
    length = lax.axis_size(axis)
    pairs = [(i, i + by) for i in range(length) if 0 <= i + by < length]
    return lax.ppermute(x, axis, pairs)


def standardize(values_in):
    average = jnp.mean(values_in, -1, keepdims=True)
    centered = values_in - average
    variance = jnp.mean(centered * centered, -1, keepdims=True)
    inverse = lax.rsqrt(variance + epsilon)
    return (centered * inverse, inverse)


def layer_norm(values_in, gain, shift):
    standard, inverse = standardize(values_in)
    return standard * gain + shift


def rope_tables(position, rot_dims):
    half_rot = rot_dims // 2
    frequency = jnp.power(
        jnp.float32(10000.0), -jnp.arange(half_rot, dtype=jnp.float32) / jnp.float32(half_rot)
    )
    angles = position.astype(jnp.float32)[:, None] * frequency[None, :]
    return (jnp.cos(angles), jnp.sin(angles))


def rotate(tensor_in, cos_table, sin_table, rot_dims):
    half_rot = rot_dims // 2
    first_half = tensor_in[..., :half_rot]
    second_half = tensor_in[..., half_rot:rot_dims]
    cos_part = cos_table[:, None, :]
    sin_part = sin_table[:, None, :]
    return jnp.concatenate(
        [
            first_half * cos_part - second_half * sin_part,
            second_half * cos_part + first_half * sin_part,
            tensor_in[..., rot_dims:],
        ],
        -1,
    )


def rotate_back(grad_in, cos_table, sin_table, rot_dims):
    half_rot = rot_dims // 2
    first_grad = grad_in[..., :half_rot]
    second_grad = grad_in[..., half_rot:rot_dims]
    cos_part = cos_table[:, None, :]
    sin_part = sin_table[:, None, :]
    return jnp.concatenate(
        [
            first_grad * cos_part + second_grad * sin_part,
            second_grad * cos_part - first_grad * sin_part,
            grad_in[..., rot_dims:],
        ],
        -1,
    )


def contract_rows(first_op, second_op):
    return lax.dot_general(
        first_op, second_op, (((0,), (0,)), ((), ())), preferred_element_type=jnp.float32
    )


def contract_cols(first_op, second_op):
    return lax.dot_general(
        first_op, second_op, (((1,), (1,)), ((), ())), preferred_element_type=jnp.float32
    )


def body(
    tokens,
    out_grad,
    segment_ids,
    positions,
    norm1_gain,
    norm1_bias,
    norm2_gain,
    norm2_bias,
    qkv_weight,
    qkv_bias,
    out_weight,
    out_bias,
    fc1_weight,
    fc1_bias,
    fc2_weight,
    fc2_bias,
):
    rows_all, grads_all = (
        lax.all_gather(tokens, "tensor", axis=0, tiled=True),
        lax.all_gather(out_grad, "tensor", axis=0, tiled=True),
    )
    row_count = rows_all.shape[0]
    model_width = rows_all.shape[1]
    head_count = qkv_weight.shape[1]
    head_dim = qkv_weight.shape[3]
    score_scale = 1.0 / math.sqrt(head_dim)
    source = rows_all.astype(jnp.float32)
    standard_all, inverse_all = standardize(source)
    normed_one = (standard_all * norm1_gain + norm1_bias).astype(jnp.bfloat16)
    normed_two = (standard_all * norm2_gain + norm2_bias).astype(jnp.bfloat16)
    flat_qkv = qkv_weight.reshape(model_width, head_count * 3 * head_dim)
    projected = jnp.dot(
        normed_one, flat_qkv, preferred_element_type=jnp.float32
    ) + qkv_bias.reshape(-1).astype(jnp.float32)
    projected = projected.reshape(row_count, head_count, 3, head_dim)
    cos_table, sin_table = rope_tables(positions, ROT)
    queries = rotate(projected[:, :, 0], cos_table, sin_table, ROT).astype(jnp.bfloat16)
    key_own = rotate(projected[:, :, 1], cos_table, sin_table, ROT).astype(jnp.bfloat16)
    value_own = projected[:, :, 2].astype(jnp.bfloat16)
    reach = (MOST - 2) // row_count + 1
    key_parts = [key_own]
    value_parts = [value_own]
    for offset in range(1, reach + 1):
        got_key, got_value = shifted((key_own, value_own), "dp", offset)
        key_parts.insert(0, got_key)
        value_parts.insert(0, got_value)
    all_keys = jnp.concatenate(key_parts, 0)
    values = jnp.concatenate(value_parts, 0)
    relative = jnp.arange(-reach * row_count, row_count, dtype=jnp.int32)
    first_segment = segment_ids[0]
    first_position = positions[0]
    remote_segment = jnp.where(relative[: reach * row_count] >= -first_position, first_segment, -1)
    key_segment = jnp.concatenate([remote_segment, segment_ids], 0)
    block_rows = min(512, row_count)
    block_count = row_count // block_rows
    query_blocks = queries.reshape(block_count, block_rows, head_count, head_dim)
    segment_blocks = segment_ids.reshape(block_count, block_rows)
    index_blocks = jnp.arange(row_count, dtype=jnp.int32).reshape(block_count, block_rows)

    def masked_scores(query_block, segment_block, index_block):
        allowed = (segment_block[:, None] == key_segment[None, :]) & (
            relative[None, :] <= index_block[:, None]
        )
        raw_scores = (
            jnp.einsum("qhd,khd->hqk", query_block, all_keys, preferred_element_type=jnp.float32)
            * score_scale
        )
        return jnp.where(allowed[None], raw_scores, -1e30)

    def forward_block(inputs):
        query_block, segment_block, index_block = inputs
        scores = masked_scores(query_block, segment_block, index_block)
        row_max = jnp.max(scores, -1, keepdims=True)
        exp_scores = jnp.exp(scores - row_max)
        row_total = jnp.sum(exp_scores, -1, keepdims=True)
        weights_low = (exp_scores / row_total).astype(jnp.bfloat16)
        outcome = jnp.einsum(
            "hqk,khd->qhd", weights_low, values, preferred_element_type=jnp.float32
        )
        return (outcome, row_max + jnp.log(row_total))

    attended, log_totals = lax.map(forward_block, (query_blocks, segment_blocks, index_blocks))
    attended_low = attended.reshape(row_count, head_count * head_dim).astype(jnp.bfloat16)
    flat_out = out_weight.reshape(head_count * head_dim, model_width)
    partial_value = jnp.dot(attended_low, flat_out, preferred_element_type=jnp.float32)
    hidden = jnp.dot(normed_two, fc1_weight, preferred_element_type=jnp.float32) + fc1_bias.astype(
        jnp.float32
    )
    activated = jax.nn.gelu(hidden, approximate=False).astype(jnp.bfloat16)
    partial_value = partial_value + jnp.dot(
        activated, fc2_weight, preferred_element_type=jnp.float32
    )
    summed = lax.psum_scatter(partial_value, "tensor", scatter_dimension=0, tiled=True)
    own_rows = tokens.astype(jnp.float32)
    block_out = (
        own_rows + summed + out_bias.astype(jnp.float32) + fc2_bias.astype(jnp.float32)
    ).astype(jnp.bfloat16)
    fc2_grad = contract_rows(activated, grads_all)
    act_grad = contract_cols(grads_all, fc2_weight)
    gelu_pull = jax.vjp(lambda values_in: jax.nn.gelu(values_in, approximate=False), hidden)[1]
    hidden_grad = gelu_pull(act_grad)[0].astype(jnp.bfloat16)
    fc1_grad = contract_rows(normed_two, hidden_grad)
    fc1_bias_grad = jnp.sum(hidden_grad, 0, dtype=jnp.float32)
    normed_two_grad = contract_cols(hidden_grad, fc1_weight)
    out_weight_grad = contract_rows(attended_low, grads_all).reshape(
        head_count, head_dim, model_width
    )
    attended_grad = (
        contract_cols(grads_all, flat_out)
        .astype(jnp.bfloat16)
        .reshape(block_count, block_rows, head_count, head_dim)
    )

    def backward_block(running, inputs):
        key_total, value_total = running
        query_block, segment_block, index_block, grad_block, total_block = inputs
        scores = masked_scores(query_block, segment_block, index_block)
        softmax_out = jnp.exp(scores - total_block)
        softmax_low = softmax_out.astype(jnp.bfloat16)
        prob_grad = jnp.einsum(
            "qhd,khd->hqk", grad_block, values, preferred_element_type=jnp.float32
        )
        score_grad = (
            softmax_out * (prob_grad - jnp.sum(softmax_out * prob_grad, -1, keepdims=True))
        ).astype(jnp.bfloat16)
        query_grad = (
            jnp.einsum("hqk,khd->qhd", score_grad, all_keys, preferred_element_type=jnp.float32)
            * score_scale
        )
        key_total = (
            key_total
            + jnp.einsum(
                "hqk,qhd->khd", score_grad, query_block, preferred_element_type=jnp.float32
            )
            * score_scale
        )
        value_total = value_total + jnp.einsum(
            "hqk,qhd->khd", softmax_low, grad_block, preferred_element_type=jnp.float32
        )
        return ((key_total, value_total), query_grad)

    zero_keys = jnp.zeros(all_keys.shape, jnp.float32)
    (key_grad, value_grad), query_grad = lax.scan(
        backward_block,
        (zero_keys, zero_keys),
        (query_blocks, segment_blocks, index_blocks, attended_grad, log_totals),
    )
    own_key_grad = key_grad[reach * row_count :]
    own_value_grad = value_grad[reach * row_count :]
    for offset in range(1, reach + 1):
        low_row = (reach - offset) * row_count
        back_key, back_value = shifted(
            (key_grad[low_row : low_row + row_count], value_grad[low_row : low_row + row_count]),
            "dp",
            -offset,
        )
        own_key_grad = own_key_grad + back_key
        own_value_grad = own_value_grad + back_value
    query_grad = query_grad.reshape(row_count, head_count, head_dim)
    qkv_grad = jnp.stack(
        [
            rotate_back(query_grad, cos_table, sin_table, ROT),
            rotate_back(own_key_grad, cos_table, sin_table, ROT),
            own_value_grad,
        ],
        2,
    )
    qkv_grad = qkv_grad.astype(jnp.bfloat16).reshape(row_count, head_count * 3 * head_dim)
    qkv_weight_grad = contract_rows(normed_one, qkv_grad).reshape(
        model_width, head_count, 3, head_dim
    )
    qkv_bias_grad = jnp.sum(qkv_grad, 0, dtype=jnp.float32).reshape(head_count, 3, head_dim)
    normed_one_grad = contract_cols(qkv_grad, flat_qkv)
    qkv_weight_grad, qkv_bias_grad, out_weight_grad, fc1_grad, fc1_bias_grad, fc2_grad = lax.psum(
        (qkv_weight_grad, qkv_bias_grad, out_weight_grad, fc1_grad, fc1_bias_grad, fc2_grad), "dp"
    )
    cotangent = out_grad.astype(jnp.float32)
    one_share, two_share = (
        lax.psum_scatter(normed_one_grad, "tensor", scatter_dimension=0, tiled=True),
        lax.psum_scatter(normed_two_grad, "tensor", scatter_dimension=0, tiled=True),
    )
    pull_one = jax.vjp(layer_norm, own_rows, norm1_gain, norm1_bias)[1]
    input_one, gain_one_grad, shift_one_grad = pull_one(one_share)
    pull_two = jax.vjp(layer_norm, own_rows, norm2_gain, norm2_bias)[1]
    input_two, gain_two_grad, shift_two_grad = pull_two(two_share)
    tokens_grad = (cotangent + input_one + input_two).astype(jnp.bfloat16)
    bias_grad = jnp.sum(cotangent, 0)
    gain_one_grad, shift_one_grad, gain_two_grad, shift_two_grad, bias_grad = lax.psum(
        (gain_one_grad, shift_one_grad, gain_two_grad, shift_two_grad, bias_grad), ("dp", "tensor")
    )
    return (
        block_out,
        tokens_grad,
        gain_one_grad,
        shift_one_grad,
        gain_two_grad,
        shift_two_grad,
        qkv_weight_grad,
        qkv_bias_grad,
        out_weight_grad,
        bias_grad,
        fc1_grad,
        fc1_bias_grad,
        fc2_grad,
        bias_grad,
    )


def solution(mesh):
    placed = (
        P(("dp", "tensor"), None),
        P(("dp", "tensor"), None),
        P("dp"),
        P("dp"),
        P(),
        P(),
        P(),
        P(),
        P(None, "tensor", None, None),
        P("tensor", None, None),
        P("tensor", None, None),
        P(),
        P(None, "tensor"),
        P("tensor"),
        P("tensor", None),
        P(),
    )
    return jax.shard_map(
        body,
        mesh=mesh,
        in_specs=placed,
        out_specs=(
            P(("dp", "tensor"), None),
            P(("dp", "tensor"), None),
            P(),
            P(),
            P(),
            P(),
            P(None, "tensor", None, None),
            P("tensor", None, None),
            P("tensor", None, None),
            P(),
            P(None, "tensor"),
            P("tensor"),
            P("tensor", None),
            P(),
        ),
        check_vma=False,
    )
```

profile of v0, /device:TPU:11, one launch (start us, length us, event | category | flops | bytes accessed | tf_op | source)
XLA Modules:
  0.0 1474.8 jit_solution(14377220985656008566)
XLA Ops:
  14.4 16.4 %copy.79 = bf16[2048,2,3,256]{0,3,2,1:T(8,128)(2,1)} copy(bf16[2048,2,3,256]{3,1,2,0:T(2,128)(2,1)} %param.28) | data formatting | bytes 12582912 | tf_op args[8]
  34.7 54.2 %all-gather.3.cloned.1.call-done = bf16[1024,2048]{1,0:T(8,128)(2,1)} async-done(((bf16[256,2048]{1,0:T(8,128)(2,1)}), bf16[1024,2048]{1,0:T(8,128)(2,1)}) %all-gather.3.cloned.1.call-update) | async-done | bytes 4194320 | tf_op jit(solution)/shard_map/all_gather | solution.py:106
  93.6 11.7 convolution_add_fusion
  147.7 13.5 fusion.85
  169.7 33.5 %convert_reduce_fusion.1 = (f32[2048]{0:T(1024)}, bf16[1024,2048]{1,0:T(8,128)(2,1)S(1)}, f32[1024,2048]{1,0:T(8,128)}) fusion(f32[1024,2048]{1,0:T(8,128)} %fusion.85, f32[2048]{0:T(1024)S(1)} %convert_element_type.100, bf16[1024,2048]{1,0:T(8,128)(2,1)} %all-gather.5.cloned.1.call-done, bf16[2048,2048]{1,0:T(8,128)(2,1)} %param.34), kind=kOutput, calls=%fused_computation.65 | convolution fusion | flops 8747218944 | bytes 33570816 | tf_op jit(solution)/shard_map/dot_general | solution.py:82
  205.2 13.7 fusion.96
  243.1 30.8 %while.28 = (s32[]{:T(128)}, bf16[2,512,2,256]{3,1,2,0:T(8,128)(2,1)}, f32[2,2,512,1]{2,1,3,0:T(2,128)S(1)}, s32[2,512]{1,0:T(2,128)S(1)}, s32[3072]{0:T(1024)S(...) while((s32[]{:T(128)}, ...), condition=%wide.region_5.6_spmd.clone, body=%wide.region_2.5_spmd.clone.sunk | while | flops 3263694848 | bytes 72958168 | solution.py:169
  273.9 108.1 %while.29 = (s32[]{:T(128)}, f32[3072,2,256]{0,2,1:T(8,128)}, f32[3072,2,256]{0,2,1:T(8,128)}, f32[2,512,2,256]{3,1,0,2:T(8,128)}, bf16[2,512,2,256]{3,1,2,0:T(8...) while((s32[]{:T(128)}, f32[3072,2,256]{0,2,1:T(8,128)}, ...), condition=%wide.region_9.10_spmd.clone, body=%wide.region_7.9_spmd.clone.sunk | while | flops 8113096704 | bytes 231813472 | solution.py:230
  293.0 10.7 multiply_convert_fusion.3
  311.3 12.0 bitcast_add_fusion.5
  365.2 13.7 bitcast_add_fusion.5
  411.8 30.9 %collective-permute-done.5 = f32[1024,2,256]{2,0,1:T(8,128)} collective-permute-done((f32[1024,2,256]{2,0,1:T(8,128)}, f32[1024,2,256]{2,0,1:T(8,128)}, u32[]{:S(2)}, u32[]{:S(2)}) %collective-permute-start.5) | collective-permute-done | bytes 2097184 | tf_op jit(solution)/shard_map/ppermute | solution.py:18
  442.6 46.0 %collective-permute-done.4 = f32[1024,2,256]{2,0,1:T(8,128)} collective-permute-done((f32[1024,2,256]{2,0,1:T(8,128)}, f32[1024,2,256]{2,0,1:T(8,128)}, u32[]{:S(2)}, u32[]{:S(2)}) %collective-permute-start.4) | collective-permute-done | bytes 2097184 | tf_op jit(solution)/shard_map/ppermute | solution.py:18
  494.9 38.5 %collective-permute-done.6 = f32[1024,2,256]{2,0,1:T(8,128)S(1)} collective-permute-done((f32[1024,2,256]{2,0,1:T(8,128)S(1)}, f32[1024,2,256]{2,0,1:T(8,128)S(1)}, u32[]{:S(2)}, u32[]{:S(2)}) %collective-permute-start.6) | collective-permute-done | bytes 2097184 | tf_op jit(solution)/shard_map/ppermute | solution.py:18
  555.4 12.8 fusion.95
  575.3 15.7 %fusion.97 = f32[2048,2048]{1,0:T(8,128)} fusion(bf16[1024,2048]{1,0:T(8,128)(2,1)} %copy-done.20, bf16[1024,2048]{1,0:T(8,128)(2,1)} %all-gather.5.cloned.1.call-done), kind=kOutput, calls=%fused_computation.169 | convolution fusion | flops 8589934592 | bytes 25165824 | tf_op jit(solution)/shard_map/dot_general | solution.py:76
  591.0 12.3 fusion.83
  616.4 14.8 %fusion.53 = f32[2048,2,3,256]{3,0,2,1:T(8,128)} fusion(bf16[1024,2,3,256]{0,3,2,1:T(8,128)(2,1)} %copy.100, bf16[1024,2048]{1,0:T(8,128)(2,1)} %all-gather.3.cloned.1.call-done, f32[2048]{0:T(1024)S(1)} %copy-done.50, f32[2048]{0:T(1024)S(1)} %copy-done.33, f32[1024]{0:T(1024)S(1)} %copy-done.45, f32[1024]{0:T(1024)S(1)} %copy-done.39), kind=kOutput, calls=%fused_computation.87 | convolution fusion | flops 6455033856 | bytes 19947520 | tf_op jit(solution)/shard_map/dot_general | solution.py:76
  632.8 21.8 %all-reduce.1 = (f32[2,3,256]{2,1,0:T(4,128)S(1)}, f32[2048]{0:T(1024)}) all-reduce(f32[2,3,256]{2,1,0:T(4,128)S(1)} %get-tuple-element.365, f32[2048]{0:T(1024)S(1)} %copy-done.40), channel_id=1, replica_groups=mesh['dp'=8,'tensor'=4] {'dp'}, use_global_device_ids=true, to_apply=%region_28.29 | all-reduce | flops 3584 | bytes 28672 | tf_op jit(solution)/shard_map/psum | solution.py:261
  655.1 35.8 %reduce-scatter.6.cloned.1.call-done = f32[256,2048]{1,0:T(8,128)} async-done(((f32[1024,2048]{1,0:T(8,128)}), f32[256,2048]{1,0:T(8,128)}) %reduce-scatter.6.cloned.1.call-update) | async-done | bytes 2097168 | tf_op jit(solution)/shard_map/reduce_scatter | solution.py:266
  696.2 142.3 %reduce-scatter.4.cloned.1.call-done = f32[256,2048]{1,0:T(8,128)} async-done(((f32[1024,2048]{1,0:T(8,128)}), f32[256,2048]{1,0:T(8,128)}) %reduce-scatter.4.cloned.1.call-update) | async-done | bytes 2097168 | tf_op jit(solution)/shard_map/reduce_scatter | solution.py:180
  843.7 41.7 %all-reduce = (f32[2048]{0:T(1024)}, f32[2048]{0:T(1024)}, f32[2048]{0:T(1024)}, f32[2048]{0:T(1024)}, f32[2048]{0:T(1024)S(1)}) all-reduce(f32[2048]{0:T(1024)S(1)} %get-tuple-element.307, f32[2048]{0:T(1024)S(1)} %get-tuple-element.393, f32[2048]{0:T(1024)S(1)} %get-tuple-element.298, ...), channel_id=1, replica_groups=mesh['dp'=8,'tensor'=4] {'dp','tensor'}, use_global_device_ids=true, to_apply=%region_19.20 | all-reduce | flops 10240 | bytes 81920 | tf_op jit(solution)/shard_map/psum | solution.py:275
  885.4 539.2 %all-reduce.5.cloned.1.call-done = (f32[2048,2,3,256]{3,0,2,1:T(8,128)}, f32[2,256,2048]{2,1,0:T(8,128)}, f32[2048,2048]{1,0:T(8,128)}, f32[2048,2048]{1,0:T(8,128)}) async-done(((f32[2048,2,3,256]{3,0,2,1:T(8,128)}, f32[2,256,2048]{2,1,0:T(8,128)}, f32[2048,2048]{1,0:T(8,128)}, f32[2048,2048]{1,0:T(8,128)}), (f32[2048,2,3,256]{3,0,2,1:T(8,128)}, f32[2,256,2048]{2,1,0:T(8,128)}, f32[2048,2048]{1,0:T(8,128)}, ...) | async-done | bytes 50331664 | tf_op jit(solution)/shard_map/psum | solution.py:261
  1424.6 22.2 %copy.103 = f32[2048,2,3,256]{3,1,2,0:T(2,128)} copy(f32[2048,2,3,256]{3,0,2,1:T(8,128)} %get-tuple-element.358) | data formatting | bytes 25165824
  (285 shorter events, 305.0 us)
Async XLA Ops:
  7.2 215.2 %copy-start = (bf16[2,256,2048]{2,1,0:T(8,128)(2,1)S(1)}, bf16[2,256,2048]{2,1,0:T(8,128)(2,1)}, u32[]{:S(2)}) copy-start(bf16[2,256,2048]{2,1,0:T(8,128)(2,1)} %param.30) | copy-start | bytes 6291460
  7.2 81.7 %all-gather.3.cloned.1.call-start = ((), (), s32[]{:S(2)}) async-start(), calls=%async_computation.3 | async-start | bytes 5242880 | tf_op jit(solution)/shard_map/all_gather | solution.py:106
  7.9 161.8 %all-gather.5.cloned.1.call-start = ((), (), s32[]{:S(2)}) async-start(), calls=%async_computation.5 | async-start | bytes 5242880 | tf_op jit(solution)/shard_map/all_gather | solution.py:107
  8.7 646.5 %reduce-scatter.8.cloned.1.call-start = ((), (), s32[]{:S(2)}) async-start(), calls=%async_computation.7 | async-start | bytes 10485760 | tf_op jit(solution)/shard_map/reduce_scatter | solution.py:267
  14.4 155.3 %copy-start.35 = (f32[2048]{0:T(1024)}, f32[2048]{0:T(1024)S(1)}, u32[]{:S(2)}) copy-start(f32[2048]{0:T(1024)S(1)} %convert_element_type.100) | copy-start | bytes 24580
  30.8 62.8 %copy-start.32 = (f32[2048]{0:T(1024)S(1)}, f32[2048]{0:T(1024)}, u32[]{:S(2)}) copy-start(f32[2048]{0:T(1024)} %param.24) | copy-start | bytes 24580
  30.8 62.8 %copy-start.49 = (f32[2048]{0:T(1024)S(1)}, f32[2048]{0:T(1024)}, u32[]{:S(2)}) copy-start(f32[2048]{0:T(1024)} %param.25) | copy-start | bytes 24580
  34.6 92.8 %copy-start.13 = (f32[1024,32]{1,0:T(8,128)}, f32[1024,32]{1,0:T(8,128)S(1)}, u32[]{:S(2)}) copy-start(f32[1024,32]{1,0:T(8,128)S(1)} %get-tuple-element.401) | copy-start | bytes 393220
  34.6 92.8 %copy-start.15 = (f32[1024,32]{1,0:T(8,128)}, f32[1024,32]{1,0:T(8,128)S(1)}, u32[]{:S(2)}) copy-start(f32[1024,32]{1,0:T(8,128)S(1)} %get-tuple-element.402) | copy-start | bytes 393220
  92.3 55.3 %copy-start.38 = (f32[1024]{0:T(1024)}, f32[1024]{0:T(1024)S(1)}, u32[]{:S(2)}) copy-start(f32[1024]{0:T(1024)S(1)} %broadcast_multiply_fusion) | copy-start | bytes 12292
  133.7 104.3 %collective-permute-start.1 = (bf16[1024,2,256]{2,0,1:T(8,128)(2,1)}, bf16[1024,2,256]{2,0,1:T(8,128)(2,1)}, u32[]{:S(2)}, u32[]{:S(2)}) collective-permute-start(bf16[1024,2,256]{2,0,1:T(8,128)(2,1)} %pad_maximum_fusion.2), channel_id=1, source_target_pairs={{0,4},{4,8},{8,12},{12,16},{16,20},{20,24},{24,28},{1,5},{5,9},{9,... | collective-permute-start | bytes 3145736 | tf_op jit(solution)/shard_map/ppermute | solution.py:18
  137.5 100.5 %collective-permute-start = (bf16[1024,2,256]{2,0,1:T(8,128)(2,1)}, bf16[1024,2,256]{2,0,1:T(8,128)(2,1)}, u32[]{:S(2)}, u32[]{:S(2)}) collective-permute-start(bf16[1024,2,256]{2,0,1:T(8,128)(2,1)} %pad_maximum_fusion.2), channel_id=1, source_target_pairs={{0,8},{4,12},{8,16},{12,20},{16,24},{20,28},{1,9},{5,13},{9,17},{1... | collective-permute-start | bytes 3145736 | tf_op jit(solution)/shard_map/ppermute | solution.py:18
  143.3 86.7 %collective-permute-start.3 = (bf16[1024,2,256]{0,2,1:T(8,128)(2,1)}, bf16[1024,2,256]{0,2,1:T(8,128)(2,1)}, u32[]{:S(2)}, u32[]{:S(2)}) collective-permute-start(bf16[1024,2,256]{0,2,1:T(8,128)(2,1)} %fusion.77), channel_id=1, source_target_pairs={{0,4},{4,8},{8,12},{12,16},{16,20},{20,24},{24,28},{1,5},{5,9},{9,... | collective-permute-start | bytes 3145736 | tf_op jit(solution)/shard_map/ppermute | solution.py:18
  145.7 84.4 %collective-permute-start.2 = (bf16[1024,2,256]{0,2,1:T(8,128)(2,1)}, bf16[1024,2,256]{0,2,1:T(8,128)(2,1)}, u32[]{:S(2)}, u32[]{:S(2)}) collective-permute-start(bf16[1024,2,256]{0,2,1:T(8,128)(2,1)} %fusion.77), channel_id=1, source_target_pairs={{0,8},{4,12},{8,16},{12,20},{16,24},{20,28},{1,9},{5,13},{9,17},{1... | collective-permute-start | bytes 3145736 | tf_op jit(solution)/shard_map/ppermute | solution.py:18
  219.0 472.0 %reduce-scatter.6.cloned.1.call-start = ((), (), s32[]{:S(2)}) async-start(), calls=%async_computation.6 | async-start | bytes 10485760 | tf_op jit(solution)/shard_map/reduce_scatter | solution.py:266
  393.2 49.4 %collective-permute-start.5 = (f32[1024,2,256]{2,0,1:T(8,128)}, f32[1024,2,256]{2,0,1:T(8,128)}, u32[]{:S(2)}, u32[]{:S(2)}) collective-permute-start(f32[1024,2,256]{2,0,1:T(8,128)} %get-tuple-element.378), channel_id=1, source_target_pairs={{8,0},{12,4},{16,8},{20,12},{24,16},{28,20},{9,1},{13,5},{17,9},{2... | collective-permute-start | bytes 6291464 | tf_op jit(solution)/shard_map/ppermute | solution.py:18
  395.3 93.3 %collective-permute-start.4 = (f32[1024,2,256]{2,0,1:T(8,128)}, f32[1024,2,256]{2,0,1:T(8,128)}, u32[]{:S(2)}, u32[]{:S(2)}) collective-permute-start(f32[1024,2,256]{2,0,1:T(8,128)} %get-tuple-element.377), channel_id=1, source_target_pairs={{4,0},{8,4},{12,8},{16,12},{20,16},{24,20},{28,24},{5,1},{9,5},{13... | collective-permute-start | bytes 6291464 | tf_op jit(solution)/shard_map/ppermute | solution.py:18
  407.5 87.4 %collective-permute-start.7 = (f32[1024,2,256]{2,0,1:T(8,128)S(1)}, f32[1024,2,256]{2,0,1:T(8,128)S(1)}, u32[]{:S(2)}, u32[]{:S(2)}) collective-permute-start(f32[1024,2,256]{2,0,1:T(8,128)S(1)} %get-tuple-element.380), channel_id=1, source_target_pairs={{8,0},{12,4},{16,8},{20,12},{24,16},{28,20},{9,1},{13,5},{17,9},{2... | collective-permute-start | bytes 6291464 | tf_op jit(solution)/shard_map/ppermute | solution.py:18
  409.4 124.0 %collective-permute-start.6 = (f32[1024,2,256]{2,0,1:T(8,128)S(1)}, f32[1024,2,256]{2,0,1:T(8,128)S(1)}, u32[]{:S(2)}, u32[]{:S(2)}) collective-permute-start(f32[1024,2,256]{2,0,1:T(8,128)S(1)} %get-tuple-element.379), channel_id=1, source_target_pairs={{4,0},{8,4},{12,8},{16,12},{20,16},{24,20},{28,24},{5,1},{9,5},{13... | collective-permute-start | bytes 6291464 | tf_op jit(solution)/shard_map/ppermute | solution.py:18
  411.4 80.9 %copy-start.14 = (f32[1024,32]{1,0:T(8,128)S(1)}, f32[1024,32]{1,0:T(8,128)}, u32[]{:S(2)}) copy-start(f32[1024,32]{1,0:T(8,128)} %copy-done.13) | copy-start | bytes 393220
  411.4 80.9 %copy-start.16 = (f32[1024,32]{1,0:T(8,128)S(1)}, f32[1024,32]{1,0:T(8,128)}, u32[]{:S(2)}) copy-start(f32[1024,32]{1,0:T(8,128)} %copy-done.15) | copy-start | bytes 393220
  546.7 291.8 %reduce-scatter.4.cloned.1.call-start = ((), (), s32[]{:S(2)}) async-start(), calls=%async_computation.4 | async-start | bytes 10485760 | tf_op jit(solution)/shard_map/reduce_scatter | solution.py:180
  575.2 849.4 %all-reduce.5.cloned.1.call-start = ((), (), s32[]{:S(2)}) async-start(), calls=%async_computation.8 | async-start | bytes 100663296 | tf_op jit(solution)/shard_map/psum | solution.py:261
  885.4 561.3 %copy-start.41 = (f32[2048]{0:T(1024)}, f32[2048]{0:T(1024)S(1)}, u32[]{:S(2)}) copy-start(f32[2048]{0:T(1024)S(1)} %get-tuple-element.659) | copy-start | bytes 24580
  (64 other events, 804.6 us)
Sparse Core Ops, SparseCore 0:
  9.6 79.2 all-gather.2
  90.4 79.2 all-gather.4
  219.1 145.2 reduce-scatter.7
  546.8 144.0 reduce-scatter.5
  693.2 145.2 reduce-scatter.3
  843.7 580.8 all-reduce.4
where the time goes:
time: 1490 us; the launch traced here: 1470 us
  waiting for transfers between devices  897 us (60%)
  matrix products  250 us (17%)
  local copies, waits for them, and re-layouts  137 us (9%)
  other arithmetic  90.7 us (6%)
  blocking collectives  63.5 us (4%)
  starting transfers between devices  20.3 us (1%)
  between operations  15.7 us (1%)
    psum x1, waiting for transfers between devices, body(): lax.psum((qkv_weight_grad, qkv_bias_grad, out_weight_grad, fc1_grad, fc1_...  539 us
    reduce_scatter x1, waiting for transfers between devices, body(): lax.psum_scatter(partial_value, 'tensor', scatter_dimension=0, tiled=True)  142 us
    ppermute x8, waiting for transfers between devices, shifted(): return lax.ppermute(x, axis, pairs)  115 us
    unnamed x123, local copies, waits for them, and re-layouts  78.1 us
    dot_general x4, matrix products, contract_cols(): lax.dot_general(first_op, second_op, (((1,), (1,)), ((), ())), preferred_...  61.7 us
    all_gather x1, waiting for transfers between devices, body(): lax.all_gather(tokens, 'tensor', axis=0, tiled=True)  54.2 us
    dot_general x4, matrix products, contract_rows(): lax.dot_general(first_op, second_op, (((0,), (0,)), ((), ())), preferred_...  49.9 us
    psum x1, blocking collectives, body(): lax.psum((gain_one_grad, shift_one_grad, gain_two_grad, shift_two_grad, b...  41.7 us
  transfers between devices with their start and end apart: 14, of which 8 were waited for; matrix products, arithmetic and copies ran while one was open for 29% of the time, Pallas kernels for 0%

commit v1 on v0

v1 whole, which is shorter than its diff:
```python
import math

import jax
import jax.numpy as jnp
from jax import lax
from jax.experimental import pallas as pl
from jax.experimental.pallas import tpu as pltpu
from jax.sharding import PartitionSpec as P

ROT = 64
MOST = 2000
EPSILON = 1e-05
BF16 = jnp.bfloat16
F32 = jnp.float32
MESH = pl.DeviceIdType.MESH


def shifted(x, axis, by):
    length = lax.axis_size(axis)
    pairs = [(i, i + by) for i in range(length) if 0 <= i + by < length]
    return lax.ppermute(x, axis, pairs)


def swapped(x, axis, bit):
    length = lax.axis_size(axis)
    return lax.ppermute(x, axis, [(i, i ^ (1 << bit)) for i in range(length)])


def dot_rows(first, second):
    return lax.dot_general(first, second, (((0,), (0,)), ((), ())), preferred_element_type=F32)


def dot_cols(first, second):
    return lax.dot_general(first, second, (((1,), (1,)), ((), ())), preferred_element_type=F32)


def dot(first, second):
    return jnp.dot(first, second, preferred_element_type=F32)


def cost(flops, bytes_accessed):
    return pl.CostEstimate(flops=int(flops), bytes_accessed=int(bytes_accessed), transcendentals=0)


def params(*semantics):
    return pltpu.CompilerParams(dimension_semantics=semantics, vmem_limit_bytes=60 << 20)


def moments(values):
    average = jnp.mean(values, -1, keepdims=True)
    centered = values - average
    variance = jnp.mean(centered * centered, -1, keepdims=True)
    return average, lax.rsqrt(variance + EPSILON)


def rope_tables(position, lanes):
    half = ROT // 2
    frequency = jnp.power(F32(10000.0), -jnp.arange(half, dtype=F32) / F32(half))
    angles = position.astype(F32)[:, None] * frequency[None, :]
    cosine, sine = jnp.cos(angles), jnp.sin(angles)
    rows = position.shape[0]
    ones = jnp.ones((rows, lanes - ROT), F32)
    return (
        jnp.concatenate([cosine, cosine, ones], 1),
        jnp.concatenate([-sine, sine, 0 * ones], 1),
    )


def turn(values, cos_block, sin_block):
    lane = lax.broadcasted_iota(jnp.int32, values.shape, 1)
    half = ROT // 2
    up = pltpu.roll(values, values.shape[1] - half, 1)
    down = pltpu.roll(values, half, 1)
    return values * cos_block + jnp.where(lane < half, up, down) * sin_block


def project_kernel(
    heads, head_dim, x_ref, g1_ref, b1_ref, g2_ref, b2_ref, w_ref, bias_ref, cos_ref, sin_ref,
    n1_ref, n2_ref, q_ref, kv_ref, mean_ref, inverse_ref,
):
    x = x_ref[...].astype(F32)
    average, inverse = moments(x)
    mean_ref[...] = average
    inverse_ref[...] = inverse
    standard = (x - average) * inverse
    n1 = (standard * g1_ref[...] + b1_ref[...]).astype(BF16)
    n1_ref[...] = n1
    n2_ref[...] = (standard * g2_ref[...] + b2_ref[...]).astype(BF16)
    cos_block, sin_block = cos_ref[...], sin_ref[...]
    width = heads * head_dim
    lanes = cos_block.shape[1]
    for part in range(3):
        low = part * width
        projected = dot(n1, w_ref[:, low : low + width]) + bias_ref[:, low : low + width]
        if part == 2:
            kv_ref[:, width:] = projected.astype(BF16)
            continue
        for head in range(heads):
            at = head * head_dim
            turned = turn(projected[:, at : at + lanes], cos_block, sin_block)
            rest = projected[:, at + lanes : at + head_dim]
            if part == 0:
                scale = 1.0 / math.sqrt(head_dim)
                q_ref[:, at : at + lanes] = (turned * scale).astype(BF16)
                q_ref[:, at + lanes : at + head_dim] = (rest * scale).astype(BF16)
            else:
                kv_ref[:, at : at + lanes] = turned.astype(BF16)
                kv_ref[:, at + lanes : at + head_dim] = rest.astype(BF16)


def project(x, gain1, bias1, gain2, bias2, weight, bias, cos_table, sin_table, heads, head_dim):
    rows, depth = x.shape
    block = min(256, rows)
    width = heads * head_dim
    whole = lambda i: (0, 0)
    by_row = lambda i: (i, 0)
    return pl.pallas_call(
        lambda *refs: project_kernel(heads, head_dim, *refs),
        name="project",
        grid=(rows // block,),
        in_specs=[
            pl.BlockSpec((block, depth), by_row),
            *[pl.BlockSpec((1, depth), whole)] * 4,
            pl.BlockSpec((depth, 3 * width), whole, pipeline_mode=pl.Buffered(1)),
            pl.BlockSpec((1, 3 * width), whole),
            pl.BlockSpec((block, cos_table.shape[1]), by_row),
            pl.BlockSpec((block, cos_table.shape[1]), by_row),
        ],
        out_specs=[
            pl.BlockSpec((block, depth), by_row),
            pl.BlockSpec((block, depth), by_row),
            pl.BlockSpec((block, width), by_row),
            pl.BlockSpec((block, 2 * width), by_row),
            pl.BlockSpec((block, 1), by_row),
            pl.BlockSpec((block, 1), by_row),
        ],
        out_shape=[
            jax.ShapeDtypeStruct((rows, depth), BF16),
            jax.ShapeDtypeStruct((rows, depth), BF16),
            jax.ShapeDtypeStruct((rows, width), BF16),
            jax.ShapeDtypeStruct((rows, 2 * width), BF16),
            jax.ShapeDtypeStruct((rows, 1), F32),
            jax.ShapeDtypeStruct((rows, 1), F32),
        ],
        compiler_params=params("arbitrary"),
        cost_estimate=cost(2 * rows * depth * 3 * width, 2 * (3 * rows * depth + 3 * depth * width)),
    )(x, gain1, bias1, gain2, bias2, weight, bias, cos_table, sin_table)


def up_kernel(x_ref, w_ref, b_ref, act_ref, slope_ref):
    hidden = dot(x_ref[...], w_ref[...]) + b_ref[...]
    phi = (1.0 + lax.erf(hidden * F32(math.sqrt(0.5)))) * 0.5
    act_ref[...] = (hidden * phi).astype(BF16)
    density = jnp.exp(hidden * hidden * -0.5) * F32(1.0 / math.sqrt(2.0 * math.pi))
    slope_ref[...] = phi + hidden * density


def up(x, weight, bias):
    rows, depth = x.shape
    width = weight.shape[1]
    bm, bn = min(256, rows), min(512, width)
    return pl.pallas_call(
        up_kernel,
        name="up",
        grid=(width // bn, rows // bm),
        in_specs=[
            pl.BlockSpec((bm, depth), lambda j, i: (i, 0)),
            pl.BlockSpec((depth, bn), lambda j, i: (0, j)),
            pl.BlockSpec((1, bn), lambda j, i: (0, j)),
        ],
        out_specs=[pl.BlockSpec((bm, bn), lambda j, i: (i, j))] * 2,
        out_shape=[
            jax.ShapeDtypeStruct((rows, width), BF16),
            jax.ShapeDtypeStruct((rows, width), F32),
        ],
        compiler_params=params("arbitrary", "arbitrary"),
        cost_estimate=cost(2 * rows * depth * width, 2 * depth * width + 6 * rows * width),
    )(x, weight, bias)


def hidden_kernel(g_ref, w_ref, slope_ref, out_ref, sum_ref):
    grad = dot_cols(g_ref[...], w_ref[...])
    low = (grad * slope_ref[...]).astype(BF16)
    out_ref[...] = low
    total = jnp.sum(low.astype(F32), 0, keepdims=True)

    @pl.when(pl.program_id(1) == 0)
    def _():
        sum_ref[...] = total

    @pl.when(pl.program_id(1) > 0)
    def _():
        sum_ref[...] += total


def hidden_grads(grad, weight, slope):
    rows, depth = grad.shape
    width = weight.shape[0]
    bm, bn = min(256, rows), min(512, width)
    return pl.pallas_call(
        hidden_kernel,
        name="hidden_grads",
        grid=(width // bn, rows // bm),
        in_specs=[
            pl.BlockSpec((bm, depth), lambda j, i: (i, 0)),
            pl.BlockSpec((bn, depth), lambda j, i: (j, 0)),
            pl.BlockSpec((bm, bn), lambda j, i: (i, j)),
        ],
        out_specs=[
            pl.BlockSpec((bm, bn), lambda j, i: (i, j)),
            pl.BlockSpec((1, bn), lambda j, i: (0, j)),
        ],
        out_shape=[
            jax.ShapeDtypeStruct((rows, width), BF16),
            jax.ShapeDtypeStruct((1, width), F32),
        ],
        compiler_params=params("arbitrary", "arbitrary"),
        cost_estimate=cost(2 * rows * depth * width, 2 * depth * width + 6 * rows * width),
    )(grad, weight, slope)


def attention_kernel(heads, head_dim, parts, bk, first_ref, q_ref, do_ref, start_ref, *refs):
    kv_parts, refs = refs[:parts], refs[parts:]
    att_ref, dq_ref, refs = refs[0], refs[1], refs[2:]
    grad_parts, (kv_ref, dkv_ref, s_ref, dp_ref, o_ref, sems) = refs[:parts], refs[parts:]
    block = pl.program_id(0)
    bq = q_ref.shape[0]
    width = heads * head_dim
    rows_each = kv_ref.shape[0] // parts
    ahead = rows_each * (parts - 1)
    low = first_ref[block]
    high = (ahead + (block + 1) * bq + bk - 1) // bk
    row = ahead + block * bq + lax.broadcasted_iota(jnp.int32, (bq, 1), 0)
    start = start_ref[...]
    lane = lax.broadcasted_iota(jnp.int32, (bq, bk), 1)
    chunks = bk // 128

    @pl.when(block == 0)
    def _():
        copies = [
            pltpu.make_async_copy(
                part, kv_ref.at[pl.ds(k * rows_each, rows_each)], sems.at[k]
            )
            for k, part in enumerate(kv_parts)
        ]
        for copy in copies:
            copy.start()

        def clear(j, carry):
            dkv_ref[pl.ds(pl.multiple_of(j * 128, 128), 128), :] = jnp.zeros((128, 2 * width), F32)
            return carry

        lax.fori_loop(0, dkv_ref.shape[0] // 128, clear, 0)
        for copy in copies:
            copy.wait()

    for head in range(heads):
        at = head * head_dim
        q = q_ref[:, at : at + head_dim]
        do = do_ref[:, at : at + head_dim]

        def rows_of(j):
            return pl.ds(pl.multiple_of(j * bk, bk), bk)

        def scores(j, best):
            s = dot_cols(q, kv_ref[rows_of(j), at : at + head_dim])
            column = j * bk + lane
            s = jnp.where((column >= start) & (column <= row), s, -1e30)
            s_ref[j] = s
            for c in range(chunks):
                best = jnp.maximum(best, s[:, c * 128 : (c + 1) * 128])
            return best

        best = lax.fori_loop(low, high, scores, jnp.full((bq, 128), -1e30, F32))
        best = jnp.max(best, 1, keepdims=True)

        def weigh(j, carry):
            total, mixed = carry
            e = jnp.exp(s_ref[j] - best)
            dp = dot_cols(do, kv_ref[rows_of(j), width + at : width + at + head_dim])
            s_ref[j] = e
            dp_ref[j] = dp
            both = e * dp
            for c in range(chunks):
                total = total + e[:, c * 128 : (c + 1) * 128]
                mixed = mixed + both[:, c * 128 : (c + 1) * 128]
            return total, mixed

        zero = jnp.zeros((bq, 128), F32)
        total, mixed = lax.fori_loop(low, high, weigh, (zero, zero))
        total = jnp.sum(total, 1, keepdims=True)
        scale = 1.0 / total
        delta = jnp.sum(mixed, 1, keepdims=True) * scale
        o_ref[...] = jnp.zeros_like(o_ref)

        def spread(j, carry):
            rows = rows_of(j)
            p = s_ref[j] * scale
            p_low = p.astype(BF16)
            ds = (p * (dp_ref[j] - delta)).astype(BF16)
            k = kv_ref[rows, at : at + head_dim]
            v = kv_ref[rows, width + at : width + at + head_dim]
            o_ref[:, :head_dim] += dot(p_low, v)
            o_ref[:, head_dim:] += dot(ds, k)
            dkv_ref[rows, at : at + head_dim] += dot_rows(ds, q)
            dkv_ref[rows, width + at : width + at + head_dim] += dot_rows(p_low, do)
            return carry

        lax.fori_loop(low, high, spread, 0)
        att_ref[:, at : at + head_dim] = o_ref[:, :head_dim].astype(BF16)
        dq_ref[:, at : at + head_dim] = o_ref[:, head_dim:] * (1.0 / math.sqrt(head_dim))

    @pl.when(block == pl.num_programs(0) - 1)
    def _():
        for k, part in enumerate(grad_parts):
            part[...] = dkv_ref[k * rows_each : (k + 1) * rows_each, :].astype(part.dtype)


def attention(q, kv_parts, do, positions, heads, head_dim):
    rows, width = q.shape
    parts = len(kv_parts)
    total = rows * parts
    bq = min(256, rows)
    bk = 256
    start = jnp.arange(rows, dtype=jnp.int32) - positions + (total - rows)
    first = start[::bq] // bk
    by_row = lambda i, f: (i, 0)
    whole = lambda i, f: (0, 0)
    part_types = [BF16] + [F32] * (parts - 1)
    return pl.pallas_call(
        lambda *refs: attention_kernel(heads, head_dim, parts, bk, *refs),
        name="attention",
        grid_spec=pltpu.PrefetchScalarGridSpec(
            num_scalar_prefetch=1,
            grid=(rows // bq,),
            in_specs=[
                pl.BlockSpec((bq, width), by_row),
                pl.BlockSpec((bq, width), by_row),
                pl.BlockSpec((bq, 1), by_row),
                *[pl.BlockSpec(memory_space=pl.ANY)] * parts,
            ],
            out_specs=[
                pl.BlockSpec((bq, width), by_row),
                pl.BlockSpec((bq, width), by_row),
                *[pl.BlockSpec((rows, 2 * width), whole, pipeline_mode=pl.Buffered(1))] * parts,
            ],
            scratch_shapes=[
                pltpu.VMEM((total, 2 * width), BF16),
                pltpu.VMEM((total, 2 * width), F32),
                pltpu.VMEM((total // bk, bq, bk), F32),
                pltpu.VMEM((total // bk, bq, bk), F32),
                pltpu.VMEM((bq, 2 * head_dim), F32),
                pltpu.SemaphoreType.DMA((parts,)),
            ],
        ),
        out_shape=[
            jax.ShapeDtypeStruct((rows, width), BF16),
            jax.ShapeDtypeStruct((rows, width), F32),
            *[jax.ShapeDtypeStruct((rows, 2 * width), kind) for kind in part_types],
        ],
        compiler_params=params("arbitrary"),
        cost_estimate=cost(12 * rows * MOST * width, 8 * total * width),
    )(first, q, do, start[:, None], *kv_parts)


def turn_back_kernel(heads, head_dim, dq_ref, dkv_ref, extra_ref, cos_ref, sin_ref, out_ref, sum_ref):
    cos_block, sin_block = cos_ref[...], -sin_ref[...]
    lanes = cos_block.shape[1]
    width = heads * head_dim
    for part in range(3):
        for head in range(heads):
            at = head * head_dim
            if part == 0:
                grad = dq_ref[:, at : at + head_dim]
            else:
                low = (part - 1) * width + at
                grad = dkv_ref[:, low : low + head_dim] + extra_ref[:, low : low + head_dim].astype(F32)
            to = part * width + at
            if part < 2:
                first = turn(grad[:, :lanes], cos_block, sin_block)
                out_ref[:, to : to + lanes] = first.astype(BF16)
                out_ref[:, to + lanes : to + head_dim] = grad[:, lanes:].astype(BF16)
            else:
                out_ref[:, to : to + head_dim] = grad.astype(BF16)
    total = jnp.sum(out_ref[...].astype(F32), 0, keepdims=True)

    @pl.when(pl.program_id(0) == 0)
    def _():
        sum_ref[...] = total

    @pl.when(pl.program_id(0) > 0)
    def _():
        sum_ref[...] += total


def turn_back(dq, dkv, extra, cos_table, sin_table, heads, head_dim):
    rows, width = dq.shape
    block = min(256, rows)
    by_row = lambda i: (i, 0)
    return pl.pallas_call(
        lambda *refs: turn_back_kernel(heads, head_dim, *refs),
        name="turn_back",
        grid=(rows // block,),
        in_specs=[
            pl.BlockSpec((block, width), by_row),
            pl.BlockSpec((block, 2 * width), by_row),
            pl.BlockSpec((block, 2 * width), by_row),
            pl.BlockSpec((block, cos_table.shape[1]), by_row),
            pl.BlockSpec((block, cos_table.shape[1]), by_row),
        ],
        out_specs=[
            pl.BlockSpec((block, 3 * width), by_row),
            pl.BlockSpec((1, 3 * width), lambda i: (0, 0)),
        ],
        out_shape=[
            jax.ShapeDtypeStruct((rows, 3 * width), BF16),
            jax.ShapeDtypeStruct((1, 3 * width), F32),
        ],
        compiler_params=params("arbitrary"),
        cost_estimate=cost(0, rows * width * 20),
    )(dq, dkv, extra, cos_table, sin_table)


def input_kernel(
    dqkv_ref, w1_ref, g1_ref, hg_ref, w2_ref, g2_ref, x_ref, mean_ref, inverse_ref,
    low_ref, own_ref, sums_ref,
):
    one = dot_cols(dqkv_ref[...], w1_ref[...])
    two = dot_cols(hg_ref[...], w2_ref[...])
    combined = one * g1_ref[...] + two * g2_ref[...]
    low_ref[...] = combined.astype(BF16)

    @pl.when(pl.program_id(1) == lax.axis_index("tensor"))
    def _():
        own_ref[...] = combined

    standard = (x_ref[...].astype(F32) - mean_ref[...]) * inverse_ref[...]
    add = lambda v: jnp.sum(v, 0, keepdims=True)
    sums = jnp.concatenate([add(one * standard), add(one), add(two * standard), add(two)], 0)

    @pl.when(pl.program_id(1) == 0)
    def _():
        sums_ref[...] = sums

    @pl.when(pl.program_id(1) > 0)
    def _():
        sums_ref[...] += sums


def input_grads(dqkv, w1, gain1, hg, w2, gain2, x, mean, inverse, own_rows):
    rows, depth = x.shape
    bm, bn = own_rows, min(512, depth)
    by_row = lambda j, i: (i, 0)
    by_column = lambda j, i: (j, 0)
    tile = lambda j, i: (i, j)
    column = lambda j, i: (0, j)
    return pl.pallas_call(
        input_kernel,
        name="input_grads",
        grid=(depth // bn, rows // bm),
        in_specs=[
            pl.BlockSpec((bm, dqkv.shape[1]), by_row),
            pl.BlockSpec((bn, w1.shape[1]), by_column),
            pl.BlockSpec((1, bn), column),
            pl.BlockSpec((bm, hg.shape[1]), by_row),
            pl.BlockSpec((bn, w2.shape[1]), by_column),
            pl.BlockSpec((1, bn), column),
            pl.BlockSpec((bm, bn), tile),
            pl.BlockSpec((bm, 1), by_row),
            pl.BlockSpec((bm, 1), by_row),
        ],
        out_specs=[
            pl.BlockSpec((bm, bn), tile),
            pl.BlockSpec((bm, bn), column),
            pl.BlockSpec((4, bn), column),
        ],
        out_shape=[
            jax.ShapeDtypeStruct((rows, depth), BF16),
            jax.ShapeDtypeStruct((own_rows, depth), F32),
            jax.ShapeDtypeStruct((4, depth), F32),
        ],
        compiler_params=params("arbitrary", "arbitrary"),
        cost_estimate=cost(
            2 * rows * depth * (w1.shape[1] + w2.shape[1]),
            2 * depth * (w1.shape[1] + w2.shape[1]) + 6 * rows * depth,
        ),
    )(dqkv, w1, gain1, hg, w2, gain2, x, mean, inverse)


def spread_kernel(heads, head_dim, in_ref, out_ref):
    for head in range(heads):
        block = in_ref[head * head_dim : (head + 1) * head_dim, :].astype(F32)
        out_ref[:, 0, head, :] = block.T


def spread(stacked, heads, head_dim):
    depth = stacked.shape[1]
    block = 256
    return pl.pallas_call(
        lambda *refs: spread_kernel(heads, head_dim, *refs),
        name="spread",
        grid=(depth // block, 3),
        in_specs=[pl.BlockSpec((heads * head_dim, block), lambda i, j: (j, i))],
        out_specs=pl.BlockSpec((block, 1, heads, head_dim), lambda i, j: (i, j, 0, 0)),
        out_shape=jax.ShapeDtypeStruct((depth, 3, heads, head_dim), F32),
        compiler_params=params("arbitrary", "arbitrary"),
        cost_estimate=cost(0, 6 * stacked.size),
    )(stacked)


def reduce_kernel(plan, chunks, bits, tensor, *refs):
    refs = list(refs)
    take = lambda count: [refs.pop(0) for _ in range(count)]
    a_refs = take(len(plan))
    b_refs = take(3)
    d_ref, own_ref, vec_ref, out_ref, dsum_ref, total_ref = take(6)
    abuf, full, r0, ag = take(4)
    kept, sent, got = take(bits - 1), take(bits - 1), take(bits - 1)
    dgot, vgot, vsend, vnow = take(4)
    a_sem, o_sem, send_sem, recv_sem, d_send, d_recv, v_send, v_recv = take(8)
    index, me = lax.axis_index("dp"), lax.axis_index("tensor")
    deep, wide = full.shape[1], full.shape[2]
    slots, ring = got[0].shape[0], ag.shape[0]

    def bit_of(bit):
        return (index // (1 << bit)) % 2

    def partner(bit):
        return index + (1 << bit) * (1 - 2 * bit_of(bit))

    barrier = pltpu.get_barrier_semaphore()
    for bit in range(bits):
        pl.semaphore_signal(barrier, inc=1, device_id={"dp": partner(bit)}, device_id_type=MESH)
    for k in range(1, tensor):
        other = lax.rem(me + k, tensor)
        pl.semaphore_signal(barrier, inc=1, device_id={"tensor": other}, device_id_type=MESH)
    pl.semaphore_wait(barrier, bits + tensor - 1)

    own_rows = own_ref.shape[0]

    def d_copy(k):
        other = lax.rem(me + k, tensor)
        return pltpu.make_async_remote_copy(
            src_ref=d_ref.at[pl.ds(pl.multiple_of(other * own_rows, own_rows), own_rows)],
            dst_ref=dgot.at[k - 1],
            send_sem=d_send.at[k - 1],
            recv_sem=d_recv.at[k - 1],
            device_id={"tensor": other},
            device_id_type=MESH,
        )

    def v_copy(k, to, slot):
        return pltpu.make_async_remote_copy(
            src_ref=vec_ref,
            dst_ref=vgot.at[slot],
            send_sem=v_send.at[k - 1],
            recv_sem=v_recv.at[slot],
            device_id={"tensor": to},
            device_id_type=MESH,
        )

    def v_step(bit):
        return pltpu.make_async_remote_copy(
            src_ref=vsend.at[bit],
            dst_ref=vnow.at[bit],
            send_sem=v_send.at[tensor + bit],
            recv_sem=v_recv.at[tensor + bit],
            device_id={"dp": partner(bit)},
            device_id_type=MESH,
        )

    def fetch_copy(item, c):
        column = pl.multiple_of((c - plan[item][0]) * deep, deep)
        slot = lax.rem(c, 2)
        return pltpu.make_async_copy(
            a_refs[item].at[:, pl.ds(column, deep)], abuf.at[slot], a_sem.at[slot]
        )

    def on_items(c, act):
        for item, (first, count, _) in enumerate(plan):
            @pl.when((c >= first) & (c < first + count))
            def _():
                act(item)

    even, odd = list(range(bits)), [0, *range(2, bits), 1]

    def mixed(level, parity, of):
        first, second = of(even[level]), of(odd[level])
        return first + parity * (second - first)

    def base(level, parity):
        row = 0
        for k in range(level):
            row = row + mixed(k, parity, bit_of) * (deep >> (k + 1))
        return row

    def down_copy(level, c):
        parity = lax.rem(c, 2)
        half = deep >> (level + 1)
        if level == 0:
            row = pl.multiple_of((1 - bit_of(0)) * half, half)
            source, target = full.at[parity, pl.ds(row, half)], r0.at[parity]
        else:
            source, target = sent[level - 1].at[parity], got[level - 1].at[lax.rem(c, slots)]
        return pltpu.make_async_remote_copy(
            src_ref=source,
            dst_ref=target,
            send_sem=send_sem.at[level, lax.rem(c, ring)],
            recv_sem=recv_sem.at[level, lax.rem(c, ring)],
            device_id={"dp": mixed(level, parity, partner)},
            device_id_type=MESH,
        )

    def up_copy(level, c, incoming=False):
        parity, slot = lax.rem(c, 2), lax.rem(c, ring)
        size = deep >> (level + 1)
        row = base(level + 1, parity)
        rows = pl.ds(pl.multiple_of(row, size), size)
        return pltpu.make_async_remote_copy(
            src_ref=ag.at[slot, rows],
            dst_ref=ag.at[slot, rows],
            send_sem=send_sem.at[bits + level, slot],
            recv_sem=recv_sem.at[bits + level, slot],
            device_id={"dp": mixed(level, parity, partner)},
            device_id_type=MESH,
        )

    def out_copy(c):
        slot = lax.rem(c, ring)
        row = pl.multiple_of(c * deep, deep)
        return pltpu.make_async_copy(ag.at[slot], out_ref.at[pl.ds(row, deep)], o_sem.at[slot])

    def multiply(c):
        slot = lax.rem(c, 2)

        def with_item(item):
            fetch_copy(item, c).wait()
            left = abuf[slot].T
            right = b_refs[plan[item][2]]
            step = min(512, wide)
            for column in range(0, wide, step):
                full[slot, :, column : column + step] = dot(left, right[:, column : column + step])

        on_items(c, with_item)
        down_copy(0, c).start()

    def halve(level, c):
        parity = lax.rem(c, 2)
        down_copy(level - 1, c).wait()
        size = deep >> level
        half = size // 2
        if level < bits:
            bit = mixed(level, parity, bit_of)
            keep = pl.multiple_of(bit * half, half)
            give = pl.multiple_of((1 - bit) * half, half)
            pieces = ((keep, True), (give, False))
        else:
            pieces = ((0, True),)
            half = size
        for row, stays in pieces:
            if level == 1:
                mine = full[parity, pl.ds(pl.multiple_of(bit_of(0) * size + row, half), half)]
                value = mine + r0[parity, pl.ds(row, half)]
            else:
                mine = kept[level - 2][parity, pl.ds(row, half)]
                value = mine + got[level - 2][lax.rem(c, slots), pl.ds(row, half)].astype(F32)
            if level == bits:
                at = pl.multiple_of(base(bits, parity), size)
                ag[lax.rem(c, ring), pl.ds(at, size)] = value.astype(BF16)
            elif stays:
                kept[level - 1][parity] = value
            else:
                sent[level - 1][parity] = value.astype(BF16)
        if level < bits:
            down_copy(level, c).start()
        else:
            up_copy(bits - 1, c).start()

    def widen(level, c):
        up_copy(level, c).wait()
        up_copy(level - 1, c).start()

    def finish(c):
        up_copy(0, c).wait()
        out_copy(c).start()

    on_items(0, lambda item: fetch_copy(item, 0).start())
    for k in range(1, tensor):
        v_copy(k, lax.rem(me + k, tensor), me).start()
    for k in range(1, tensor):
        d_copy(k).start()
    vgot[me] = vec_ref[...]

    def stage(t, delay, act):
        c = t - delay

        @pl.when((c >= 0) & (c < chunks))
        def _():
            act(c)

    def iteration(t, carry):
        @pl.when(t + 1 < chunks)
        def _():
            on_items(t + 1, lambda item: fetch_copy(item, t + 1).start())

        stage(t, 2 * bits + 1, lambda c: out_copy(c).wait())
        stage(t, 2 * bits, finish)
        for level in range(1, bits):
            stage(t, 2 * bits - level, lambda c, level=level: widen(level, c))
        for level in range(bits, 0, -1):
            stage(t, level, lambda c, level=level: halve(level, c))
        stage(t, 0, multiply)

        @pl.when(t == 1)
        def _():
            for k in range(1, tensor):
                other = lax.rem(me + k, tensor)
                v_copy(k, other, me).wait_send()
                v_copy(k, other, other).wait_recv()
            lane = lax.broadcasted_iota(jnp.int32, vec_ref.shape, 0)
            both = vgot[0]
            for k in range(1, tensor):
                both = both + vgot[k]
            vsend[0] = jnp.where(lane < 5, both, vec_ref[...])
            v_step(0).start()

        for bit in range(bits):
            @pl.when(t == 2 + bit)
            def _():
                v_step(bit).wait()
                both = vsend[bit] + vnow[bit]
                if bit + 1 < bits:
                    vsend[bit + 1] = both
                    v_step(bit + 1).start()
                else:
                    total_ref[...] = both

        return carry

    lax.fori_loop(0, chunks + 2 * bits + 2, iteration, 0)
    summed_rows = own_ref[...]
    for k in range(1, tensor):
        d_copy(k).wait()
        summed_rows = summed_rows + dgot[k - 1].astype(F32)
    dsum_ref[...] = summed_rows


def reduce_grads(items, rights, d_low, d_own, vectors, bits, tensor):
    deep = 256
    rows, wide = rights[0].shape
    plan, first = [], 0
    for left, which in items:
        count = left.shape[1] // deep
        plan.append((first, count, which))
        first += count
    chunks, ring, slots = first, 8, 4
    halves_of = [deep >> (level + 1) for level in range(1, bits)]
    own_rows = d_own.shape[0]
    hbm = pl.BlockSpec(memory_space=pl.ANY)
    vmem = pl.BlockSpec(memory_space=pltpu.VMEM)
    return pl.pallas_call(
        lambda *refs: reduce_kernel(plan, chunks, bits, tensor, *refs),
        name="reduce_grads",
        in_specs=[hbm] * len(items) + [vmem] * 3 + [hbm, vmem, vmem],
        out_specs=[hbm, vmem, vmem],
        out_shape=[
            jax.ShapeDtypeStruct((chunks * deep, wide), BF16),
            jax.ShapeDtypeStruct((own_rows, wide), F32),
            jax.ShapeDtypeStruct(vectors.shape, F32),
        ],
        scratch_shapes=[
            pltpu.VMEM((2, rows, deep), BF16),
            pltpu.VMEM((2, deep, wide), F32),
            pltpu.VMEM((2, deep // 2, wide), F32),
            pltpu.VMEM((ring, deep, wide), BF16),
            *[pltpu.VMEM((2, half, wide), F32) for half in halves_of],
            *[pltpu.VMEM((2, half, wide), BF16) for half in halves_of],
            *[pltpu.VMEM((slots, half, wide), BF16) for half in halves_of],
            pltpu.VMEM((tensor - 1, own_rows, wide), BF16),
            pltpu.VMEM((tensor, *vectors.shape), F32),
            pltpu.VMEM((bits, *vectors.shape), F32),
            pltpu.VMEM((bits, *vectors.shape), F32),
            pltpu.SemaphoreType.DMA((2,)),
            pltpu.SemaphoreType.DMA((ring,)),
            pltpu.SemaphoreType.DMA((2 * bits, ring)),
            pltpu.SemaphoreType.DMA((2 * bits, ring)),
            pltpu.SemaphoreType.DMA((tensor - 1,)),
            pltpu.SemaphoreType.DMA((tensor - 1,)),
            pltpu.SemaphoreType.DMA((tensor + bits,)),
            pltpu.SemaphoreType.DMA((tensor + bits,)),
        ],
        compiler_params=pltpu.CompilerParams(
            collective_id=0, has_side_effects=True, vmem_limit_bytes=62 << 20
        ),
        cost_estimate=cost(2 * rows * chunks * deep * wide, 8 * chunks * deep * wide),
    )(*[left for left, _ in items], *rights, d_low, d_own, vectors)


def body(
    tokens, out_grad, segment_ids, positions, norm1_gain, norm1_bias, norm2_gain, norm2_bias,
    qkv_weight, qkv_bias, out_weight, out_bias, fc1_weight, fc1_bias, fc2_weight, fc2_bias,
):
    model_width, heads, _, head_dim = qkv_weight.shape
    width = heads * head_dim
    hidden_width = fc1_weight.shape[1]
    own_count = tokens.shape[0]
    tie = lax.optimization_barrier
    row = lambda v: v.reshape(1, -1).astype(F32)
    rows_all = lax.all_gather(tokens, "tensor", axis=0, tiled=True)
    grads_all = lax.all_gather(out_grad, "tensor", axis=0, tiled=True)
    row_count = rows_all.shape[0]
    flat_qkv = jnp.transpose(qkv_weight, (0, 2, 1, 3)).reshape(model_width, 3 * width)
    flat_bias = jnp.transpose(qkv_bias, (1, 0, 2)).reshape(1, 3 * width).astype(F32)
    flat_out = out_weight.reshape(width, model_width)
    cos_table, sin_table = rope_tables(positions, 128)
    normed_one, normed_two, queries, kv_own, mean, inverse = project(
        rows_all, row(norm1_gain), row(norm1_bias), row(norm2_gain), row(norm2_bias),
        flat_qkv, flat_bias, cos_table, sin_table, heads, head_dim,
    )
    reach = (MOST - 2) // row_count + 1
    kv_parts = [kv_own]
    for _ in range(reach):
        kv_parts.insert(0, shifted(kv_parts[0], "dp", 1))
    activated, slope = up(normed_two, fc1_weight, row(fc1_bias))
    forward = dot(activated, fc2_weight)
    grads_all, activated, slope, forward = tie((grads_all, activated, slope, forward))

    attended_grad = dot_cols(grads_all, flat_out).astype(BF16)
    attended, query_grad, *kv_grads = attention(
        queries, kv_parts, attended_grad, positions, heads, head_dim
    )
    grads_all, attended, query_grad, *kv_grads = tie((grads_all, attended, query_grad, *kv_grads))
    partial = dot(attended, flat_out) + forward
    branch = lax.psum_scatter(partial, "tensor", scatter_dimension=0, tiled=True)
    hidden_grad, fc1_bias_grad = hidden_grads(grads_all, fc2_weight, slope)
    extra = None
    for part in kv_grads[:-1]:
        if extra is not None:
            part = (part + extra.astype(F32)).astype(BF16)
        extra = shifted(part, "dp", -1)
        extra, hidden_grad = tie((extra, hidden_grad))
    qkv_grad, qkv_bias_grad = turn_back(
        query_grad, kv_grads[-1], extra, cos_table, sin_table, heads, head_dim
    )
    d_low, d_own, sums = input_grads(
        qkv_grad, flat_qkv, row(norm1_gain), hidden_grad, fc1_weight, row(norm2_gain),
        rows_all, mean, inverse, own_count,
    )
    wide = lambda v: jnp.pad(v, ((0, 0), (0, model_width - v.shape[1])))
    own_grad = out_grad.astype(F32)
    vectors = jnp.concatenate(
        [
            sums, jnp.sum(own_grad, 0, keepdims=True), wide(fc1_bias_grad), wide(qkv_bias_grad),
            jnp.zeros((1, model_width), F32),
        ],
        0,
    )
    bits = (lax.axis_size("dp") - 1).bit_length()
    natural = hidden_width == model_width
    fc1_pair = (normed_two, hidden_grad) if natural else (hidden_grad, normed_two)
    stacked, d_sum, vectors = reduce_grads(
        [(activated, 0), (attended, 0), (fc1_pair[0], 1), (qkv_grad, 2)],
        [grads_all, fc1_pair[1], normed_one],
        d_low, d_own, vectors, bits, lax.axis_size("tensor"),
    )
    fc2_grad = stacked[:hidden_width].astype(F32)
    at = hidden_width
    out_weight_grad = stacked[at : at + width].astype(F32).reshape(heads, head_dim, model_width)
    at += width
    fc1_grad = stacked[at : at + fc1_pair[0].shape[1]].astype(F32)
    at += fc1_pair[0].shape[1]
    if not natural:
        fc1_grad = fc1_grad.T
    qkv_weight_grad = jnp.transpose(spread(stacked[at:], heads, head_dim), (0, 2, 1, 3))
    fc1_bias_grad = vectors[5, :hidden_width]
    qkv_bias_grad = vectors[6, : 3 * width].reshape(3, heads, head_dim)
    qkv_bias_grad = jnp.transpose(qkv_bias_grad, (1, 0, 2))
    own_rows = tokens.astype(F32)
    block_out = own_rows + branch + out_bias.astype(F32) + fc2_bias.astype(F32)
    own_mean, own_inverse = moments(own_rows)
    standard = (own_rows - own_mean) * own_inverse
    tokens_grad = own_grad + own_inverse * (
        d_sum
        - jnp.mean(d_sum, -1, keepdims=True)
        - standard * jnp.mean(d_sum * standard, -1, keepdims=True)
    )
    return (
        block_out.astype(BF16), tokens_grad.astype(BF16),
        vectors[0], vectors[1], vectors[2], vectors[3],
        qkv_weight_grad, qkv_bias_grad, out_weight_grad, vectors[4],
        fc1_grad, fc1_bias_grad, fc2_grad, vectors[4],
    )


def solution(mesh):
    rows = P(("dp", "tensor"), None)
    return jax.shard_map(
        body,
        mesh=mesh,
        in_specs=(
            rows, rows, P("dp"), P("dp"), P(), P(), P(), P(),
            P(None, "tensor", None, None), P("tensor", None, None), P("tensor", None, None), P(),
            P(None, "tensor"), P("tensor"), P("tensor", None), P(),
        ),
        out_specs=(
            rows, rows, P(), P(), P(), P(),
            P(None, "tensor", None, None), P("tensor", None, None), P("tensor", None, None), P(),
            P(None, "tensor"), P("tensor"), P("tensor", None), P(),
        ),
        check_vma=False,
    )
```

time: 1490 us -> 681 us (0.46)
  waiting for transfers between devices: 897 us -> 112 us
  Pallas kernels: 0 us -> 445 us
  matrix products: 250 us -> 29.5 us
  local copies, waits for them, and re-layouts: 137 us -> 31.6 us
  blocking collectives: 63.5 us -> 0 us
  other arithmetic: 90.7 us -> 35.1 us
    psum x1 -> x0, waiting for transfers between devices: 539 us -> none  [body(): lax.psum((qkv_weight_grad, qkv_bias_grad, out_weight_grad, fc1_grad, fc1_...]
    pallas_call x0 -> x8, Pallas kernels: none -> 445 us  [the longest x1 273 us: reduce_grads(): pl.pallas_call(lambda *refs: reduce_kernel(plan, chunks, bits, tensor, *r...]
    dot_general x26 -> x3, matrix products: 250 us -> 29.5 us  [the longest x2 24 us: dot(): return jnp.dot(first, second, preferred_element_type=F32)]
    reduce_scatter x3 -> x1, waiting for transfers between devices: 178 us -> 0.01 us  [body(): lax.psum_scatter(partial, 'tensor', scatter_dimension=0, tiled=True)]
    ppermute x8 -> x4, waiting for transfers between devices: 115 us -> 29.4 us  [shifted(): return lax.ppermute(x, axis, pairs)]
    unnamed x123 -> x29, local copies, waits for them, and re-layouts: 78.1 us -> 1.97 us
    psum x2 -> x0, blocking collectives: 63.5 us -> none  [the longest x1 41.7 us: body(): lax.psum((gain_one_grad, shift_one_grad, gain_two_grad, shift_two_grad, b...]
    reduce_sum x9 -> x4, other arithmetic: 22.7 us -> 1.37 us  [the longest x1 0.56 us: body(): jnp.mean(d_sum, -1, keepdims=True)]
  transfers between devices with their start and end apart: 14 -> 7, of which waited for: 8 -> 4; matrix products, arithmetic and copies ran while one was open for 29% -> 12% of each run, Pallas kernels for 0% -> 58%
where the time goes in v1:
time: 681 us; the launch traced here: 677 us
  Pallas kernels  445 us (65%)
  waiting for transfers between devices  112 us (16%)
  other arithmetic  35.1 us (5%)
  local copies, waits for them, and re-layouts  31.6 us (5%)
  matrix products  29.5 us (4%)
  between operations  14 us (2%)
  starting transfers between devices  10.2 us (1%)
    pallas_call x1, Pallas kernels, reduce_grads(): pl.pallas_call(lambda *refs: reduce_kernel(plan, chunks, bits, tensor, *r...  273 us
    all_gather x1, waiting for transfers between devices, body(): rows_all = lax.all_gather(tokens, 'tensor', axis=0, tiled=True)  61.6 us
    pallas_call x1, Pallas kernels, attention(): pl.pallas_call(lambda *refs: attention_kernel(heads, head_dim, parts, bk,...  54.2 us
    pallas_call x1, Pallas kernels, input_grads(): pl.pallas_call(input_kernel, name='input_grads', grid=(depth // bn, rows...  33 us
    ppermute x4, waiting for transfers between devices, shifted(): return lax.ppermute(x, axis, pairs)  29.4 us
    pallas_call x1, Pallas kernels, up(): pl.pallas_call(up_kernel, name='up', grid=(width // bn, rows // bm), in_s...  24.3 us
    dot_general x2, matrix products, dot(): return jnp.dot(first, second, preferred_element_type=F32)  24 us
    pallas_call x1, Pallas kernels, hidden_grads(): pl.pallas_call(hidden_kernel, name='hidden_grads', grid=(width // bn, row...  22.4 us
  transfers between devices with their start and end apart: 7, of which 4 were waited for; matrix products, arithmetic and copies ran while one was open for 12% of the time, Pallas kernels for 58%

profile of v1, /device:TPU:11, one launch (start us, length us, event | category | flops | bytes accessed | tf_op | source)
XLA Modules:
  0.0 677.2 jit_solution(7245719162989311957)
XLA Ops:
  8.7 14.5 %reshape.105.refs_5_.w1_ref = bf16[2048,1536]{1,0:T(8,128)(2,1)} reshape(bf16[2048,3,2,256]{3,2,1,0:T(2,128)(2,1)} %bitcast.29) | data formatting | bytes 12582912 | tf_op jit(solution)/shard_map/reshape | solution.py:812
  27.3 61.6 %all-gather.5.cloned.1.call-done.refs_0_.x_ref = bf16[1024,2048]{1,0:T(8,128)(2,1)} async-done(((bf16[256,2048]{1,0:T(8,128)(2,1)}), bf16[1024,2048]{1,0:T(8,128)(2,1)}) %all-gather.5.cloned.1.call-update) | async-done | bytes 4194320 | tf_op jit(solution)/shard_map/all_gather | solution.py:809
  88.8 13.8 %project.1 = (bf16[1024,2048]{1,0:T(8,128)(2,1)}, bf16[1024,2048]{1,0:T(8,128)(2,1)}, bf16[1024,512]{1,0:T(8,128)(2,1)}, bf16[1024,1024]{1,0:T(8,128)(2,1)}, f32[1024,1]{1,0:T(8,128)}, /*index=5*/f32[1024,1]{1,0:T(8,128)}) custom-call(bf16[1024,2048]{1,0:T(8,128)(2,1)} %all-gather.5.cloned.1.call-done.refs_0_.x_ref, f32[1,2048]{1,0:T(1,128)} %bitcast.45, ...), custom_call_target="tpu_custom_call" | custom-call | flops 6442450944 | bytes 18874368 | tf_op jit(solution)/shard_map/project/pallas_call | solution.py:117
  102.7 3.8 collective-permute-start
  108.8 24.3 %up.1 = (bf16[1024,2048]{1,0:T(8,128)(2,1)}, f32[1024,2048]{1,0:T(8,128)}) custom-call(bf16[1024,2048]{1,0:T(8,128)(2,1)} %get-tuple-element.51.x_ref.refs_2_, bf16[2048,2048]{1,0:T(8,128)(2,1)} %w2_ref.1, f32[1,2048]{1,0:T(1,128)} %bitcast.41), custom_call_target="tpu_custom_call" | custom-call | flops 8589934592 | bytes 20971520 | tf_op jit(solution)/shard_map/up/pallas_call | solution.py:162
  133.1 2.2 collective-permute-start.1
  135.3 14.7 %fusion.15 = f32[1024,2048]{1,0:T(8,128)} fusion(bf16[1024,2048]{1,0:T(8,128)(2,1)} %get-tuple-element.64.refs_0_, bf16[2048,2048]{1,0:T(8,128)(2,1)} %w_ref.3), kind=kOutput, calls=%fused_computation.41 | convolution fusion | flops 8589934592 | bytes 20971520 | tf_op jit(solution)/shard_map/dot_general | solution.py:38
  150.0 19.7 %all-gather.3.cloned.1.call-done.g_ref.refs_4_ = bf16[1024,2048]{1,0:T(8,128)(2,1)} async-done(((bf16[256,2048]{1,0:T(8,128)(2,1)}), bf16[1024,2048]{1,0:T(8,128)(2,1)}) %all-gather.3.cloned.1.call-update) | async-done | bytes 4194320 | tf_op jit(solution)/shard_map/all_gather | solution.py:810
  169.7 5.5 convolution_convert_fusion.refs_2_
  175.2 54.2 %attention.1 = (bf16[1024,512]{1,0:T(8,128)(2,1)}, f32[1024,512]{1,0:T(8,128)}, bf16[1024,1024]{1,0:T(8,128)(2,1)}, f32[1024,1024]{1,0:T(8,128)}, f32[1024,1024]{1,0:T(8,128)}) custom-call(s32[4]{0:T(128)} %and_select_fusion.refs_0_, bf16[1024,512]{1,0:T(8,128)(2,1)} %get-tuple-element.55.refs_1_, bf16[1024,512]{1,0:T(8,128)(2,1)} %convolution_convert_fusion.refs_2_, ...), custom_call_target="tpu_custom_call" | custom-call | flops 12582912000 | bytes 12582912 | tf_op jit(solution)/shard_map/attention/pallas_call | solution.py:330
  229.4 9.3 %convolution_add_fusion = f32[1024,2048]{1,0:T(8,128)} fusion(f32[1024,2048]{1,0:T(8,128)} %fusion.15, bf16[1024,512]{1,0:T(8,128)(2,1)} %get-tuple-element.62.refs_1_, bf16[512,2048]{1,0:T(8,128)(2,1)S(1)} %bitcast.31), kind=kOutput, calls=%fused_computation.3 | convolution fusion | flops 2149580800 | bytes 19922944 | tf_op jit(solution)/shard_map/dot_general | solution.py:38
  240.7 22.4 %hidden_grads.1 = (bf16[1024,2048]{1,0:T(8,128)(2,1)}, f32[1,2048]{1,0:T(1,128)}) custom-call(bf16[1024,2048]{1,0:T(8,128)(2,1)} %all-gather.3.cloned.1.call-done.g_ref.refs_4_, bf16[2048,2048]{1,0:T(8,128)(2,1)} %w_ref.3, f32[1024,2048]{1,0:T(8,128)} %get-tuple-element.70.slope_ref), custom_call_target="tpu_custom_call" | custom-call | flops 8589934592 | bytes 20971520 | tf_op jit(solution)/shard_map/hidden_grads/pallas_call | solution.py:200
  263.0 4.2 collective-permute-done.2
  267.3 3.1 add_convert_fusion
  273.4 25.2 %collective-permute-done.3.refs_2_ = bf16[1024,1024]{1,0:T(8,128)(2,1)S(1)} collective-permute-done((bf16[1024,1024]{1,0:T(8,128)(2,1)S(1)}, bf16[1024,1024]{1,0:T(8,128)(2,1)S(1)}, u32[]{:S(2)}, u32[]{:S(2)}) %collective-permute-start.3) | collective-permute-done | bytes 2097184 | tf_op jit(solution)/shard_map/ppermute | solution.py:21
  299.9 6.6 turn_back.1
  307.3 33.0 %input_grads.1 = (bf16[1024,2048]{1,0:T(8,128)(2,1)}, f32[256,2048]{1,0:T(8,128)}, f32[4,2048]{1,0:T(4,128)}) custom-call(bf16[1024,1536]{1,0:T(8,128)(2,1)} %get-tuple-element.75.dqkv_ref.refs_3_, bf16[2048,1536]{1,0:T(8,128)(2,1)} %reshape.105.refs_5_.w1_ref, f32[1,2048]{1,0:T(1,128)} %bitcast.46, bf16[1024,2048]{1,0:T(8,128)(2,1)} %get-tuple-element.76.hg_ref.refs_5_, ...), custom_call_target="tpu_custom_call" | custom-call | flops 15032385536 | bytes 27262976 | tf_op jit(solution)/shard_map/input_grads/pallas_call | solution.py:457
  341.7 272.5 %reduce_grads.1 = (bf16[6144,2048]{1,0:T(8,128)(2,1)}, f32[256,2048]{1,0:T(8,128)}, f32[8,2048]{1,0:T(8,128)}) custom-call(bf16[1024,2048]{1,0:T(8,128)(2,1)} %get-tuple-element.64.refs_0_, bf16[1024,512]{1,0:T(8,128)(2,1)} %get-tuple-element.62.refs_1_, bf16[1024,2048]{1,0:T(8,128)(2,1)} %get-tuple-element.51.x_ref.refs_2_, ...), custom_call_target="tpu_custom_call" | custom-call | flops 25769803776 | bytes 100663296 | tf_op jit(solution)/shard_map/reduce_grads/pallas_call | solution.py:761
  614.3 6.6 slice.42.refs_0_
  620.9 3.2 slice.44
  624.0 17.9 %spread.1 = f32[2048,3,2,256]{3,2,1,0:T(2,128)} custom-call(bf16[1536,2048]{1,0:T(8,128)(2,1)} %slice.42.refs_0_), custom_call_target="tpu_custom_call" | custom-call | bytes 18874368 | tf_op jit(solution)/shard_map/spread/pallas_call | solution.py:499
  642.6 4.3 convert.4
  648.1 17.1 %slice_convert_fusion = (f32[2048,2048]{1,0:T(8,128)}, f32[2048,2048]{1,0:T(8,128)}) fusion(bf16[6144,2048]{1,0:T(8,128)(2,1)} %get-tuple-element.87), kind=kLoop, calls=%fused_computation | loop fusion | flops 8388608 | bytes 50331648 | tf_op jit(solution)/shard_map/convert_element_type | solution.py:866
  665.3 4.7 fusion.8
  (70 shorter events, 18.6 us)
Async XLA Ops:
  7.2 81.7 %all-gather.5.cloned.1.call-start = ((), (), s32[]{:S(2)}) async-start(), calls=%async_computation.2 | async-start | bytes 5242880 | tf_op jit(solution)/shard_map/all_gather | solution.py:809
  7.9 161.8 %all-gather.3.cloned.1.call-start = ((), (), s32[]{:S(2)}) async-start(), calls=%async_computation.1 | async-start | bytes 5242880 | tf_op jit(solution)/shard_map/all_gather | solution.py:810
  8.7 656.6 %reduce-scatter.2.cloned.1.call-start = ((), (), s32[]{:S(2)}) async-start(), calls=%async_computation.3 | async-start | bytes 10485760 | tf_op jit(solution)/shard_map/reduce_scatter | solution.py:834
  8.7 14.5 %copy-start.13 = (bf16[2,3,256]{2,0,1:T(2,128)(2,1)S(1)}, bf16[2,3,256]{2,0,1:T(2,128)(2,1)}, u32[]{:S(2)}) copy-start(bf16[2,3,256]{2,0,1:T(2,128)(2,1)} %param.24) | copy-start | bytes 9220
  8.7 15.3 %copy-start.9 = (s32[1024]{0:T(1024)S(1)}, s32[1024]{0:T(1024)}, u32[]{:S(2)}) copy-start(s32[1024]{0:T(1024)} %param.18) | copy-start | bytes 12292
  88.8 17.7 %copy-start.10 = (bf16[2048]{0:T(1024)(128)(2,1)S(1)}, bf16[2048]{0:T(1024)(128)(2,1)}, u32[]{:S(2)}) copy-start(bf16[2048]{0:T(1024)(128)(2,1)} %param.28) | copy-start | bytes 12292
  102.7 30.4 %collective-permute-start = (bf16[1024,1024]{1,0:T(8,128)(2,1)}, bf16[1024,1024]{1,0:T(8,128)(2,1)}, u32[]{:S(2)}, u32[]{:S(2)}) collective-permute-start(bf16[1024,1024]{1,0:T(8,128)(2,1)} %get-tuple-element.56.refs_6_), channel_id=1, source_target_pairs={{0,4},{4,8},{8,12},{12,16},{16,20},{20,24},{24,28},{1,5},{5,9},{9,... | collective-permute-start | bytes 6291464 | tf_op jit(solution)/shard_map/ppermute | solution.py:21
  133.1 42.1 %collective-permute-start.1 = (bf16[1024,1024]{1,0:T(8,128)(2,1)}, bf16[1024,1024]{1,0:T(8,128)(2,1)}, u32[]{:S(2)}, u32[]{:S(2)}) collective-permute-start(bf16[1024,1024]{1,0:T(8,128)(2,1)} %collective-permute-done.refs_5_), channel_id=1, source_target_pairs={{0,4},{4,8},{8,12},{12,16},{16,20},{20,24},{24,28},{1,5},{5,9},{9,... | collective-permute-start | bytes 6291464 | tf_op jit(solution)/shard_map/ppermute | solution.py:21
  135.3 34.4 %copy-start.4 = (bf16[2,256,2048]{2,1,0:T(8,128)(2,1)S(1)}, bf16[2,256,2048]{2,1,0:T(8,128)(2,1)}, u32[]{:S(2)}) copy-start(bf16[2,256,2048]{2,1,0:T(8,128)(2,1)} %param.25) | copy-start | bytes 6291460
  238.7 28.5 %collective-permute-start.2 = (bf16[1024,1024]{1,0:T(8,128)(2,1)}, bf16[1024,1024]{1,0:T(8,128)(2,1)S(1)}, u32[]{:S(2)}, u32[]{:S(2)}) collective-permute-start(bf16[1024,1024]{1,0:T(8,128)(2,1)} %get-tuple-element.68), channel_id=1, source_target_pairs={{4,0},{8,4},{12,8},{16,12},{20,16},{24,20},{28,24},{5,1},{9,5},{13... | collective-permute-start | bytes 6291464 | tf_op jit(solution)/shard_map/ppermute | solution.py:21
  267.2 5.3 copy-start.11
  267.2 5.3 copy-start.12
  267.3 5.3 copy-start.1
  267.3 5.5 copy-start
  270.4 28.3 %collective-permute-start.3 = (bf16[1024,1024]{1,0:T(8,128)(2,1)S(1)}, bf16[1024,1024]{1,0:T(8,128)(2,1)S(1)}, u32[]{:S(2)}, u32[]{:S(2)}) collective-permute-start(bf16[1024,1024]{1,0:T(8,128)(2,1)S(1)} %add_convert_fusion), channel_id=1, source_target_pairs={{4,0},{8,4},{12,8},{16,12},{20,16},{24,20},{28,24},{5,1},{9,5},{13... | collective-permute-start | bytes 6291464 | tf_op jit(solution)/shard_map/ppermute | solution.py:21
  298.6 1.3 copy-start.5
  307.3 33.0 %copy-start.8 = (f32[1,2048]{1,0:T(1,128)S(1)}, f32[1,2048]{1,0:T(1,128)}, u32[]{:S(2)}) copy-start(f32[1,2048]{1,0:T(1,128)} %get-tuple-element.83) | copy-start | bytes 24580
  624.0 17.9 %copy-start.6 = (f32[8,2048]{1,0:T(8,128)S(1)}, f32[8,2048]{1,0:T(8,128)}, u32[]{:S(2)}) copy-start(f32[8,2048]{1,0:T(8,128)} %get-tuple-element.86) | copy-start | bytes 196612
  642.6 4.9 copy-start.3
  647.5 22.5 %copy-start.7 = (f32[1,2048]{1,0:T(1,128)}, f32[1,2048]{1,0:T(1,128)S(1)}, u32[]{:S(2)}) copy-start(f32[1,2048]{1,0:T(1,128)S(1)} %get-tuple-element.95) | copy-start | bytes 24580
  648.1 17.2 %copy-start.2 = (bf16[256,2048]{1,0:T(8,128)(2,1)S(1)}, bf16[256,2048]{1,0:T(8,128)(2,1)}, u32[]{:S(2)}) copy-start(bf16[256,2048]{1,0:T(8,128)(2,1)} %param.17) | copy-start | bytes 3145732
Sparse Core Ops, SparseCore 0:
  9.6 79.2 all-gather.4
  90.4 79.2 all-gather.2
  238.8 206.1 reduce-scatter.1

commit v2 on v1

--- a/solution.py
+++ b/solution.py
@@ -421,81 +421,34 @@
     )(dq, dkv, extra, cos_table, sin_table)
 
 
-def input_kernel(
-    dqkv_ref, w1_ref, g1_ref, hg_ref, w2_ref, g2_ref, x_ref, mean_ref, inverse_ref,
-    low_ref, own_ref, sums_ref,
-):
-    one = dot_cols(dqkv_ref[...], w1_ref[...])
-    two = dot_cols(hg_ref[...], w2_ref[...])
-    combined = one * g1_ref[...] + two * g2_ref[...]
-    low_ref[...] = combined.astype(BF16)
-
-    @pl.when(pl.program_id(1) == lax.axis_index("tensor"))
-    def _():
-        own_ref[...] = combined
-
-    standard = (x_ref[...].astype(F32) - mean_ref[...]) * inverse_ref[...]
-    add = lambda v: jnp.sum(v, 0, keepdims=True)
-    sums = jnp.concatenate([add(one * standard), add(one), add(two * standard), add(two)], 0)
-
-    @pl.when(pl.program_id(1) == 0)
-    def _():
-        sums_ref[...] = sums
-
-    @pl.when(pl.program_id(1) > 0)
-    def _():
-        sums_ref[...] += sums
-
-
-def input_grads(dqkv, w1, gain1, hg, w2, gain2, x, mean, inverse, own_rows):
+def widen_kernel(in_ref, out_ref):
+    out_ref[...] = in_ref[...].astype(F32)
+
+
+def widened(x):
     rows, depth = x.shape
-    bm, bn = own_rows, min(512, depth)
-    by_row = lambda j, i: (i, 0)
-    by_column = lambda j, i: (j, 0)
-    tile = lambda j, i: (i, j)
-    column = lambda j, i: (0, j)
+    block = min(512, rows)
     return pl.pallas_call(
-        input_kernel,
-        name="input_grads",
-        grid=(depth // bn, rows // bm),
-        in_specs=[
-            pl.BlockSpec((bm, dqkv.shape[1]), by_row),
-            pl.BlockSpec((bn, w1.shape[1]), by_column),
-            pl.BlockSpec((1, bn), column),
-            pl.BlockSpec((bm, hg.shape[1]), by_row),
-            pl.BlockSpec((bn, w2.shape[1]), by_column),
-            pl.BlockSpec((1, bn), column),
-            pl.BlockSpec((bm, bn), tile),
-            pl.BlockSpec((bm, 1), by_row),
-            pl.BlockSpec((bm, 1), by_row),
-        ],
-        out_specs=[
-            pl.BlockSpec((bm, bn), tile),
-            pl.BlockSpec((bm, bn), column),
-            pl.BlockSpec((4, bn), column),
-        ],
-        out_shape=[
-            jax.ShapeDtypeStruct((rows, depth), BF16),
-            jax.ShapeDtypeStruct((own_rows, depth), F32),
-            jax.ShapeDtypeStruct((4, depth), F32),
-        ],
-        compiler_params=params("arbitrary", "arbitrary"),
-        cost_estimate=cost(
-            2 * rows * depth * (w1.shape[1] + w2.shape[1]),
-            2 * depth * (w1.shape[1] + w2.shape[1]) + 6 * rows * depth,
-        ),
-    )(dqkv, w1, gain1, hg, w2, gain2, x, mean, inverse)
+        widen_kernel,
+        name="widened",
+        grid=(rows // block,),
+        in_specs=[pl.BlockSpec((block, depth), lambda i: (i, 0))],
+        out_specs=pl.BlockSpec((block, depth), lambda i: (i, 0)),
+        out_shape=jax.ShapeDtypeStruct(x.shape, F32),
+        compiler_params=params("arbitrary"),
+        cost_estimate=cost(0, 6 * x.size),
+    )(x)
 
 
 def spread_kernel(heads, head_dim, in_ref, out_ref):
     for head in range(heads):
-        block = in_ref[head * head_dim : (head + 1) * head_dim, :].astype(F32)
-        out_ref[:, 0, head, :] = block.T
+        block = in_ref[head * head_dim : (head + 1) * head_dim, :]
+        out_ref[:, 0, head, :] = block.T.astype(F32)
 
 
 def spread(stacked, heads, head_dim):
     depth = stacked.shape[1]
-    block = 256
+    block = min(1024, depth)
     return pl.pallas_call(
         lambda *refs: spread_kernel(heads, head_dim, *refs),
         name="spread",
@@ -513,14 +466,18 @@
     take = lambda count: [refs.pop(0) for _ in range(count)]
     a_refs = take(len(plan))
     b_refs = take(3)
-    d_ref, own_ref, vec_ref, out_ref, dsum_ref, total_ref = take(6)
+    vec_ref, dqkv_ref, hg_ref, gain1_ref, gain2_ref, mean_ref, inverse_ref = take(7)
+    w1_ref, w2_ref, x_ref = take(3)
+    out_refs = take(len(plan))
+    dsum_ref, total_ref = take(2)
     abuf, full, r0, ag = take(4)
+    w1buf, w2buf, xbuf, zsend, mine_ref, w_sem = take(6)
     kept, sent, got = take(bits - 1), take(bits - 1), take(bits - 1)
     dgot, vgot, vsend, vnow = take(4)
     a_sem, o_sem, send_sem, recv_sem, d_send, d_recv, v_send, v_recv = take(8)
     index, me = lax.axis_index("dp"), lax.axis_index("tensor")
     deep, wide = full.shape[1], full.shape[2]
-    slots, ring = got[0].shape[0], ag.shape[0]
+    slots, ring, lag = r0.shape[0], ag.shape[0], 2
 
     def bit_of(bit):
         return (index // (1 << bit)) % 2
@@ -536,22 +493,79 @@
         pl.semaphore_signal(barrier, inc=1, device_id={"tensor": other}, device_id_type=MESH)
     pl.semaphore_wait(barrier, bits + tensor - 1)
 
-    own_rows = own_ref.shape[0]
-
-    def d_copy(k):
+    own_rows = dsum_ref.shape[0]
+    units = wide // deep
+    zslots = zsend.shape[0]
+    begin = max(chunks // 2, 1)
+
+    def columns_of(u):
+        return pl.ds(pl.multiple_of(u * deep, deep), deep)
+
+    def d_copy(k, u):
         other = lax.rem(me + k, tensor)
+        rows = pl.ds(pl.multiple_of(other * own_rows, own_rows), own_rows)
         return pltpu.make_async_remote_copy(
-            src_ref=d_ref.at[pl.ds(pl.multiple_of(other * own_rows, own_rows), own_rows)],
-            dst_ref=dgot.at[k - 1],
-            send_sem=d_send.at[k - 1],
-            recv_sem=d_recv.at[k - 1],
+            src_ref=zsend.at[lax.rem(u, zslots), rows],
+            dst_ref=dgot.at[k - 1, :, columns_of(u)],
+            send_sem=d_send.at[k - 1, u],
+            recv_sem=d_recv.at[k - 1, u],
             device_id={"tensor": other},
             device_id_type=MESH,
         )
 
+    def unit_copies(u):
+        slot = lax.rem(u, 2)
+        return [
+            pltpu.make_async_copy(w1_ref.at[columns_of(u)], w1buf.at[slot], w_sem.at[0, slot]),
+            pltpu.make_async_copy(w2_ref.at[columns_of(u)], w2buf.at[slot], w_sem.at[1, slot]),
+            pltpu.make_async_copy(x_ref.at[:, columns_of(u)], xbuf.at[slot], w_sem.at[2, slot]),
+        ]
+
+    def unit(u):
+        slot, zslot = lax.rem(u, 2), lax.rem(u, zslots)
+        columns = columns_of(u)
+
+        @pl.when(u + 1 < units)
+        def _():
+            for copy in unit_copies(u + 1):
+                copy.start()
+
+        for copy in unit_copies(u):
+            copy.wait()
+
+        @pl.when(u >= zslots)
+        def _():
+            for k in range(1, tensor):
+                d_copy(k, u - zslots).wait_send()
+
+        gain1, gain2 = gain1_ref[:, columns], gain2_ref[:, columns]
+        mine_ref[0:4, columns] = jnp.zeros((4, deep), F32)
+
+        def row_block(i, carry):
+            rows = pl.ds(pl.multiple_of(i * own_rows, own_rows), own_rows)
+            one = dot_cols(dqkv_ref[rows, :], w1buf[slot])
+            two = dot_cols(hg_ref[rows, :], w2buf[slot])
+            both = one * gain1 + two * gain2
+            zsend[zslot, rows] = both.astype(BF16)
+
+            @pl.when(i == me)
+            def _():
+                dsum_ref[:, columns] = both
+
+            standard = (xbuf[slot, rows].astype(F32) - mean_ref[rows, :]) * inverse_ref[rows, :]
+            add = lambda v: jnp.sum(v, 0, keepdims=True)
+            mine_ref[0:4, columns] += jnp.concatenate(
+                [add(one * standard), add(one), add(two * standard), add(two)], 0
+            )
+            return carry
+
+        lax.fori_loop(0, tensor, row_block, 0)
+        for k in range(1, tensor):
+            d_copy(k, u).start()
+
     def v_copy(k, to, slot):
         return pltpu.make_async_remote_copy(
-            src_ref=vec_ref,
+            src_ref=mine_ref,
             dst_ref=vgot.at[slot],
             send_sem=v_send.at[k - 1],
             recv_sem=v_recv.at[slot],
@@ -595,13 +609,13 @@
         return row
 
     def down_copy(level, c):
-        parity = lax.rem(c, 2)
+        parity, slot = lax.rem(c, 2), lax.rem(c, slots)
         half = deep >> (level + 1)
         if level == 0:
             row = pl.multiple_of((1 - bit_of(0)) * half, half)
-            source, target = full.at[parity, pl.ds(row, half)], r0.at[parity]
+            source, target = full.at[lax.rem(c, 3), pl.ds(row, half)], r0.at[slot]
         else:
-            source, target = sent[level - 1].at[parity], got[level - 1].at[lax.rem(c, slots)]
+            source, target = sent[level - 1].at[slot], got[level - 1].at[slot]
         return pltpu.make_async_remote_copy(
             src_ref=source,
             dst_ref=target,
@@ -611,7 +625,7 @@
             device_id_type=MESH,
         )
 
-    def up_copy(level, c, incoming=False):
+    def up_copy(level, c):
         parity, slot = lax.rem(c, 2), lax.rem(c, ring)
         size = deep >> (level + 1)
         row = base(level + 1, parity)
@@ -625,17 +639,19 @@
             device_id_type=MESH,
         )
 
-    def out_copy(c):
+    def out_copy(item, c):
         slot = lax.rem(c, ring)
-        row = pl.multiple_of(c * deep, deep)
-        return pltpu.make_async_copy(ag.at[slot], out_ref.at[pl.ds(row, deep)], o_sem.at[slot])
+        row = pl.multiple_of((c - plan[item][0]) * deep, deep)
+        return pltpu.make_async_copy(
+            ag.at[slot], out_refs[item].at[pl.ds(row, deep)], o_sem.at[slot]
+        )
 
     def multiply(c):
-        slot = lax.rem(c, 2)
+        slot = lax.rem(c, 3)
 
         def with_item(item):
             fetch_copy(item, c).wait()
-            left = abuf[slot].T
+            left = abuf[lax.rem(c, 2)].T
             right = b_refs[plan[item][2]]
             step = min(512, wide)
             for column in range(0, wide, step):
@@ -645,7 +661,7 @@
         down_copy(0, c).start()
 
     def halve(level, c):
-        parity = lax.rem(c, 2)
+        parity, slot = lax.rem(c, 2), lax.rem(c, slots)
         down_copy(level - 1, c).wait()
         size = deep >> level
         half = size // 2
@@ -659,18 +675,20 @@
             half = size
         for row, stays in pieces:
             if level == 1:
-                mine = full[parity, pl.ds(pl.multiple_of(bit_of(0) * size + row, half), half)]
-                value = mine + r0[parity, pl.ds(row, half)]
+                mine = full[
+                    lax.rem(c, 3), pl.ds(pl.multiple_of(bit_of(0) * size + row, half), half)
+                ]
+                value = mine + r0[slot, pl.ds(row, half)]
             else:
-                mine = kept[level - 2][parity, pl.ds(row, half)]
-                value = mine + got[level - 2][lax.rem(c, slots), pl.ds(row, half)].astype(F32)
+                mine = kept[level - 2][slot, pl.ds(row, half)]
+                value = mine + got[level - 2][slot, pl.ds(row, half)].astype(F32)
             if level == bits:
                 at = pl.multiple_of(base(bits, parity), size)
                 ag[lax.rem(c, ring), pl.ds(at, size)] = value.astype(BF16)
             elif stays:
-                kept[level - 1][parity] = value
+                kept[level - 1][slot] = value
             else:
-                sent[level - 1][parity] = value.astype(BF16)
+                sent[level - 1][slot] = value.astype(BF16)
         if level < bits:
             down_copy(level, c).start()
         else:
@@ -682,14 +700,12 @@
 
     def finish(c):
         up_copy(0, c).wait()
-        out_copy(c).start()
+        on_items(c, lambda item: out_copy(item, c).start())
 
     on_items(0, lambda item: fetch_copy(item, 0).start())
-    for k in range(1, tensor):
-        v_copy(k, lax.rem(me + k, tensor), me).start()
-    for k in range(1, tensor):
-        d_copy(k).start()
-    vgot[me] = vec_ref[...]
+    for copy in unit_copies(0):
+        copy.start()
+    mine_ref[...] = vec_ref[...]
 
     def stage(t, delay, act):
         c = t - delay
@@ -697,35 +713,51 @@
         @pl.when((c >= 0) & (c < chunks))
         def _():
             act(c)
+
+    def stage_of(t, first, count, act):
+        @pl.when((t >= first) & (t < first + count))
+        def _():
+            act(t - first)
 
     def iteration(t, carry):
         @pl.when(t + 1 < chunks)
         def _():
             on_items(t + 1, lambda item: fetch_copy(item, t + 1).start())
 
-        stage(t, 2 * bits + 1, lambda c: out_copy(c).wait())
-        stage(t, 2 * bits, finish)
+        stage(
+            t, 2 * bits * lag + 1,
+            lambda c: on_items(c, lambda item: out_copy(item, c).wait()),
+        )
+        stage(t, 2 * bits * lag, finish)
         for level in range(1, bits):
-            stage(t, 2 * bits - level, lambda c, level=level: widen(level, c))
+            stage(t, (2 * bits - level) * lag, lambda c, level=level: widen(level, c))
         for level in range(bits, 0, -1):
-            stage(t, level, lambda c, level=level: halve(level, c))
+            stage(t, level * lag, lambda c, level=level: halve(level, c))
         stage(t, 0, multiply)
 
-        @pl.when(t == 1)
+        stage_of(t, begin, units, unit)
+
+        @pl.when(t == begin + units)
+        def _():
+            for k in range(1, tensor):
+                v_copy(k, lax.rem(me + k, tensor), me).start()
+            vgot[me] = mine_ref[...]
+
+        @pl.when(t == begin + units + 2)
         def _():
             for k in range(1, tensor):
                 other = lax.rem(me + k, tensor)
                 v_copy(k, other, me).wait_send()
                 v_copy(k, other, other).wait_recv()
-            lane = lax.broadcasted_iota(jnp.int32, vec_ref.shape, 0)
+            line = lax.broadcasted_iota(jnp.int32, mine_ref.shape, 0)
             both = vgot[0]
             for k in range(1, tensor):
                 both = both + vgot[k]
-            vsend[0] = jnp.where(lane < 5, both, vec_ref[...])
+            vsend[0] = jnp.where(line < 5, both, mine_ref[...])
             v_step(0).start()
 
         for bit in range(bits):
-            @pl.when(t == 2 + bit)
+            @pl.when(t == begin + units + 4 + 2 * bit)
             def _():
                 v_step(bit).wait()
                 both = vsend[bit] + vnow[bit]
@@ -737,15 +769,24 @@
 
         return carry
 
-    lax.fori_loop(0, chunks + 2 * bits + 2, iteration, 0)
-    summed_rows = own_ref[...]
+    lax.fori_loop(0, max(chunks + 2 * bits * lag + 1, begin + units + 3 + 2 * bits), iteration, 0)
+
+    def gather(u, carry):
+        for k in range(1, tensor):
+            d_copy(k, u).wait_recv()
+        return carry
+
+    lax.fori_loop(0, units, gather, 0)
+    for u in range(max(units - zslots, 0), units):
+        for k in range(1, tensor):
+            d_copy(k, u).wait_send()
+    rest = dsum_ref[...]
     for k in range(1, tensor):
-        d_copy(k).wait()
-        summed_rows = summed_rows + dgot[k - 1].astype(F32)
-    dsum_ref[...] = summed_rows
-
-
-def reduce_grads(items, rights, d_low, d_own, vectors, bits, tensor):
+        rest = rest + dgot[k - 1].astype(F32)
+    dsum_ref[...] = rest
+
+
+def reduce_grads(items, rights, vectors, moments_of, pair_one, pair_two, x, bits, tensor):
     deep = 256
     rows, wide = rights[0].shape
     plan, first = [], 0
@@ -753,28 +794,36 @@
         count = left.shape[1] // deep
         plan.append((first, count, which))
         first += count
-    chunks, ring, slots = first, 8, 4
+    chunks, ring, slots = first, 4 * bits - 2, 4
     halves_of = [deep >> (level + 1) for level in range(1, bits)]
-    own_rows = d_own.shape[0]
+    own_rows = rows // tensor
+    (dqkv, w1, gain1), (hg, w2, gain2), (mean, inverse) = pair_one, pair_two, moments_of
+    units, zslots = wide // deep, 3
     hbm = pl.BlockSpec(memory_space=pl.ANY)
     vmem = pl.BlockSpec(memory_space=pltpu.VMEM)
     return pl.pallas_call(
         lambda *refs: reduce_kernel(plan, chunks, bits, tensor, *refs),
         name="reduce_grads",
-        in_specs=[hbm] * len(items) + [vmem] * 3 + [hbm, vmem, vmem],
-        out_specs=[hbm, vmem, vmem],
+        in_specs=[hbm] * len(items) + [vmem] * 10 + [hbm] * 3,
+        out_specs=[hbm] * len(items) + [vmem, vmem],
         out_shape=[
-            jax.ShapeDtypeStruct((chunks * deep, wide), BF16),
+            *[jax.ShapeDtypeStruct((left.shape[1], wide), BF16) for left, _ in items],
             jax.ShapeDtypeStruct((own_rows, wide), F32),
             jax.ShapeDtypeStruct(vectors.shape, F32),
         ],
         scratch_shapes=[
             pltpu.VMEM((2, rows, deep), BF16),
-            pltpu.VMEM((2, deep, wide), F32),
-            pltpu.VMEM((2, deep // 2, wide), F32),
+            pltpu.VMEM((3, deep, wide), F32),
+            pltpu.VMEM((slots, deep // 2, wide), F32),
             pltpu.VMEM((ring, deep, wide), BF16),
-            *[pltpu.VMEM((2, half, wide), F32) for half in halves_of],
-            *[pltpu.VMEM((2, half, wide), BF16) for half in halves_of],
+            pltpu.VMEM((2, deep, w1.shape[1]), BF16),
+            pltpu.VMEM((2, deep, w2.shape[1]), BF16),
+            pltpu.VMEM((2, rows, deep), BF16),
+            pltpu.VMEM((zslots, rows, deep), BF16),
+            pltpu.VMEM(vectors.shape, F32),
+            pltpu.SemaphoreType.DMA((3, 2)),
+            *[pltpu.VMEM((slots, half, wide), F32) for half in halves_of],
+            *[pltpu.VMEM((slots, half, wide), BF16) for half in halves_of],
             *[pltpu.VMEM((slots, half, wide), BF16) for half in halves_of],
             pltpu.VMEM((tensor - 1, own_rows, wide), BF16),
             pltpu.VMEM((tensor, *vectors.shape), F32),
@@ -784,8 +833,8 @@
             pltpu.SemaphoreType.DMA((ring,)),
             pltpu.SemaphoreType.DMA((2 * bits, ring)),
             pltpu.SemaphoreType.DMA((2 * bits, ring)),
-            pltpu.SemaphoreType.DMA((tensor - 1,)),
-            pltpu.SemaphoreType.DMA((tensor - 1,)),
+            pltpu.SemaphoreType.DMA((tensor - 1, units)),
+            pltpu.SemaphoreType.DMA((tensor - 1, units)),
             pltpu.SemaphoreType.DMA((tensor + bits,)),
             pltpu.SemaphoreType.DMA((tensor + bits,)),
         ],
@@ -793,7 +842,10 @@
             collective_id=0, has_side_effects=True, vmem_limit_bytes=62 << 20
         ),
         cost_estimate=cost(2 * rows * chunks * deep * wide, 8 * chunks * deep * wide),
-    )(*[left for left, _ in items], *rights, d_low, d_own, vectors)
+    )(
+        *[left for left, _ in items], *rights, vectors, dqkv, hg, gain1, gain2, mean, inverse,
+        w1, w2, x,
+    )
 
 
 def body(
@@ -842,15 +894,11 @@
     qkv_grad, qkv_bias_grad = turn_back(
         query_grad, kv_grads[-1], extra, cos_table, sin_table, heads, head_dim
     )
-    d_low, d_own, sums = input_grads(
-        qkv_grad, flat_qkv, row(norm1_gain), hidden_grad, fc1_weight, row(norm2_gain),
-        rows_all, mean, inverse, own_count,
-    )
     wide = lambda v: jnp.pad(v, ((0, 0), (0, model_width - v.shape[1])))
     own_grad = out_grad.astype(F32)
     vectors = jnp.concatenate(
         [
-            sums, jnp.sum(own_grad, 0, keepdims=True), wide(fc1_bias_grad), wide(qkv_bias_grad),
+            jnp.zeros((4, model_width), F32), jnp.sum(own_grad, 0, keepdims=True), wide(fc1_bias_grad), wide(qkv_bias_grad),
             jnp.zeros((1, model_width), F32),
         ],
         0,
@@ -858,20 +906,16 @@
     bits = (lax.axis_size("dp") - 1).bit_length()
     natural = hidden_width == model_width
     fc1_pair = (normed_two, hidden_grad) if natural else (hidden_grad, normed_two)
-    stacked, d_sum, vectors = reduce_grads(
+    fc2_grad, out_weight_grad, fc1_grad, qkv_weight_grad, d_sum, vectors = reduce_grads(
         [(activated, 0), (attended, 0), (fc1_pair[0], 1), (qkv_grad, 2)],
         [grads_all, fc1_pair[1], normed_one],
-        d_low, d_own, vectors, bits, lax.axis_size("tensor"),
+        vectors, (mean, inverse), (qkv_grad, flat_qkv, row(norm1_gain)),
+        (hidden_grad, fc1_weight, row(norm2_gain)), rows_all, bits, lax.axis_size("tensor"),
     )
-    fc2_grad = stacked[:hidden_width].astype(F32)
-    at = hidden_width
-    out_weight_grad = stacked[at : at + width].astype(F32).reshape(heads, head_dim, model_width)
-    at += width
-    fc1_grad = stacked[at : at + fc1_pair[0].shape[1]].astype(F32)
-    at += fc1_pair[0].shape[1]
-    if not natural:
-        fc1_grad = fc1_grad.T
-    qkv_weight_grad = jnp.transpose(spread(stacked[at:], heads, head_dim), (0, 2, 1, 3))
+    fc2_grad = widened(fc2_grad)
+    out_weight_grad = out_weight_grad.astype(F32).reshape(heads, head_dim, model_width)
+    fc1_grad = widened(fc1_grad) if natural else fc1_grad.T.astype(F32)
+    qkv_weight_grad = jnp.transpose(spread(qkv_weight_grad, heads, head_dim), (0, 2, 1, 3))
     fc1_bias_grad = vectors[5, :hidden_width]
     qkv_bias_grad = vectors[6, : 3 * width].reshape(3, heads, head_dim)
     qkv_bias_grad = jnp.transpose(qkv_bias_grad, (1, 0, 2))

time: 681 us -> 606 us (0.89)
  Pallas kernels: 445 us -> 397 us
  other arithmetic: 35.1 us -> 19.4 us
  local copies, waits for them, and re-layouts: 31.6 us -> 22.9 us
    pallas_call x1, Pallas kernels: 273 us -> 246 us  [reduce_grads(): pl.pallas_call(lambda *refs: reduce_kernel(plan, chunks, bits, tensor, *r...]
    convert_element_type x1 -> x0, other arithmetic: 17.1 us -> none  [body(): fc2_grad = stacked[:hidden_width].astype(F32)]
    pallas_call x1 -> x2, Pallas kernels: 33 us -> 19 us  [widened(): pl.pallas_call(widen_kernel, name='widened', grid=(rows // block,), in_sp...]
    slice x2 -> x0, local copies, waits for them, and re-layouts: 9.77 us -> none  [the longest x1 6.61 us: body(): stacked[at:]]
    pallas_call x1, Pallas kernels: 17.9 us -> 10.2 us  [spread(): pl.pallas_call(lambda *refs: spread_kernel(heads, head_dim, *refs), name=...]
  transfers between devices with their start and end apart: 7 -> 7, of which waited for: 4 -> 4; matrix products, arithmetic and copies ran while one was open for 12% -> 9% of each run, Pallas kernels for 58% -> 57%
where the time goes in v2:
time: 606 us; the launch traced here: 605 us
  Pallas kernels  397 us (66%)
  waiting for transfers between devices  112 us (18%)
  matrix products  29.5 us (5%)
  local copies, waits for them, and re-layouts  22.9 us (4%)
  other arithmetic  19.4 us (3%)
  between operations  14 us (2%)
  starting transfers between devices  10.2 us (2%)
    pallas_call x1, Pallas kernels, reduce_grads(): pl.pallas_call(lambda *refs: reduce_kernel(plan, chunks, bits, tensor, *r...  246 us
    all_gather x1, waiting for transfers between devices, body(): rows_all = lax.all_gather(tokens, 'tensor', axis=0, tiled=True)  61.6 us
    pallas_call x1, Pallas kernels, attention(): pl.pallas_call(lambda *refs: attention_kernel(heads, head_dim, parts, bk,...  54.1 us
    ppermute x4, waiting for transfers between devices, shifted(): return lax.ppermute(x, axis, pairs)  29.4 us
    pallas_call x1, Pallas kernels, up(): pl.pallas_call(up_kernel, name='up', grid=(width // bn, rows // bm), in_s...  24.4 us
    dot_general x2, matrix products, dot(): return jnp.dot(first, second, preferred_element_type=F32)  24 us
    pallas_call x1, Pallas kernels, hidden_grads(): pl.pallas_call(hidden_kernel, name='hidden_grads', grid=(width // bn, row...  22.4 us
    all_gather x1, waiting for transfers between devices, body(): grads_all = lax.all_gather(out_grad, 'tensor', axis=0, tiled=True)  19.7 us
  transfers between devices with their start and end apart: 7, of which 4 were waited for; matrix products, arithmetic and copies ran while one was open for 9% of the time, Pallas kernels for 57%

profile of v2, /device:TPU:11, one launch (start us, length us, event | category | flops | bytes accessed | tf_op | source)
XLA Modules:
  0.0 604.7 jit_solution(13094544890658277684)
XLA Ops:
  9.5 14.5 %reshape.105.refs_5_.refs_14_ = bf16[2048,1536]{1,0:T(8,128)(2,1)} reshape(bf16[2048,3,2,256]{3,2,1,0:T(2,128)(2,1)} %bitcast.28) | data formatting | bytes 12582912 | tf_op jit(solution)/shard_map/reshape | solution.py:864
  27.3 61.6 %all-gather.5.cloned.1.call-done.refs_0_.refs_16_ = bf16[1024,2048]{1,0:T(8,128)(2,1)} async-done(((bf16[256,2048]{1,0:T(8,128)(2,1)}), bf16[1024,2048]{1,0:T(8,128)(2,1)}) %all-gather.5.cloned.1.call-update) | async-done | bytes 4194320 | tf_op jit(solution)/shard_map/all_gather | solution.py:861
  88.9 13.8 %project.1 = (bf16[1024,2048]{1,0:T(8,128)(2,1)}, bf16[1024,2048]{1,0:T(8,128)(2,1)}, bf16[1024,512]{1,0:T(8,128)(2,1)}, bf16[1024,1024]{1,0:T(8,128)(2,1)}, f32[1024,1]{1,0:T(8,128)}, /*index=5*/f32[1024,1]{1,0:T(8,128)}) custom-call(bf16[1024,2048]{1,0:T(8,128)(2,1)} %all-gather.5.cloned.1.call-done.refs_0_.refs_16_, f32[1,2048]{1,0:T(1,128)} %bitcast.45, ...), custom_call_target="tpu_custom_call" | custom-call | flops 6442450944 | bytes 18874368 | tf_op jit(solution)/shard_map/project/pallas_call | solution.py:117
  102.7 3.8 collective-permute-start
  108.8 24.4 %up.1 = (bf16[1024,2048]{1,0:T(8,128)(2,1)}, f32[1024,2048]{1,0:T(8,128)}) custom-call(bf16[1024,2048]{1,0:T(8,128)(2,1)} %get-tuple-element.51.x_ref.refs_2_, bf16[2048,2048]{1,0:T(8,128)(2,1)} %refs_15_.1, f32[1,2048]{1,0:T(1,128)} %bitcast.41), custom_call_target="tpu_custom_call" | custom-call | flops 8589934592 | bytes 20971520 | tf_op jit(solution)/shard_map/up/pallas_call | solution.py:162
  133.1 2.2 collective-permute-start.1
  135.3 14.7 %fusion.15 = f32[1024,2048]{1,0:T(8,128)} fusion(bf16[1024,2048]{1,0:T(8,128)(2,1)} %get-tuple-element.64.refs_0_, bf16[2048,2048]{1,0:T(8,128)(2,1)} %w_ref.3), kind=kOutput, calls=%fused_computation.39 | convolution fusion | flops 8589934592 | bytes 20971520 | tf_op jit(solution)/shard_map/dot_general | solution.py:38
  150.0 19.7 %all-gather.3.cloned.1.call-done.g_ref.refs_4_ = bf16[1024,2048]{1,0:T(8,128)(2,1)} async-done(((bf16[256,2048]{1,0:T(8,128)(2,1)}), bf16[1024,2048]{1,0:T(8,128)(2,1)}) %all-gather.3.cloned.1.call-update) | async-done | bytes 4194320 | tf_op jit(solution)/shard_map/all_gather | solution.py:862
  169.7 5.5 convolution_convert_fusion.refs_2_
  175.2 54.1 %attention.1 = (bf16[1024,512]{1,0:T(8,128)(2,1)}, f32[1024,512]{1,0:T(8,128)}, bf16[1024,1024]{1,0:T(8,128)(2,1)}, f32[1024,1024]{1,0:T(8,128)}, f32[1024,1024]{1,0:T(8,128)}) custom-call(s32[4]{0:T(128)} %and_select_fusion.refs_0_, bf16[1024,512]{1,0:T(8,128)(2,1)} %get-tuple-element.55.refs_1_, bf16[1024,512]{1,0:T(8,128)(2,1)} %convolution_convert_fusion.refs_2_, ...), custom_call_target="tpu_custom_call" | custom-call | flops 12582912000 | bytes 12582912 | tf_op jit(solution)/shard_map/attention/pallas_call | solution.py:330
  229.4 9.3 %convolution_add_fusion = f32[1024,2048]{1,0:T(8,128)} fusion(f32[1024,2048]{1,0:T(8,128)} %fusion.15, bf16[1024,512]{1,0:T(8,128)(2,1)} %get-tuple-element.62.refs_1_, bf16[512,2048]{1,0:T(8,128)(2,1)S(1)} %bitcast.30), kind=kOutput, calls=%fused_computation.1 | convolution fusion | flops 2149580800 | bytes 19922944 | tf_op jit(solution)/shard_map/dot_general | solution.py:38
  240.6 22.4 %hidden_grads.1 = (bf16[1024,2048]{1,0:T(8,128)(2,1)}, f32[1,2048]{1,0:T(1,128)}) custom-call(bf16[1024,2048]{1,0:T(8,128)(2,1)} %all-gather.3.cloned.1.call-done.g_ref.refs_4_, bf16[2048,2048]{1,0:T(8,128)(2,1)} %w_ref.3, f32[1024,2048]{1,0:T(8,128)} %get-tuple-element.70.slope_ref), custom_call_target="tpu_custom_call" | custom-call | flops 8589934592 | bytes 20971520 | tf_op jit(solution)/shard_map/hidden_grads/pallas_call | solution.py:200
  263.0 4.2 collective-permute-done.2
  267.2 3.1 add_convert_fusion
  270.3 2.1 collective-permute-start.3
  273.4 25.2 %collective-permute-done.3.refs_2_ = bf16[1024,1024]{1,0:T(8,128)(2,1)S(1)} collective-permute-done((bf16[1024,1024]{1,0:T(8,128)(2,1)S(1)}, bf16[1024,1024]{1,0:T(8,128)(2,1)S(1)}, u32[]{:S(2)}, u32[]{:S(2)}) %collective-permute-start.3) | collective-permute-done | bytes 2097184 | tf_op jit(solution)/shard_map/ppermute | solution.py:21
  299.9 6.6 %turn_back.1 = (bf16[1024,1536]{1,0:T(8,128)(2,1)}, f32[1,1536]{1,0:T(1,128)}) custom-call(f32[1024,512]{1,0:T(8,128)} %get-tuple-element.65.refs_0_, f32[1024,1024]{1,0:T(8,128)} %get-tuple-element.66.refs_1_, bf16[1024,1024]{1,0:T(8,128)(2,1)} %copy-done.4, f32[1024,128]{1,0:T(8,128)} %get-tuple-element.103.refs_7_.refs_3_, ...), custom_call_target="tpu_custom_call" | custom-call | bytes 10485760 | tf_op jit(solution)/shard_map/turn_back/pallas_call | solution.py:400
  307.9 246.0 %reduce_grads.1 = (bf16[2048,2048]{1,0:T(8,128)(2,1)}, bf16[512,2048]{1,0:T(8,128)(2,1)}, bf16[2048,2048]{1,0:T(8,128)(2,1)}, bf16[1536,2048]{1,0:T(8,128)(2,1)}...) custom-call(bf16[1024,2048]{1,0:T(8,128)(2,1)} %get-tuple-element.64.refs_0_, bf16[1024,512]{1,0:T(8,128)(2,1)} %get-tuple-element.62.refs_1_, ...), custom_call_target="tpu_custom_call" | custom-call | flops 25769803776 | bytes 100663296 | tf_op jit(solution)/shard_map/reduce_grads/pallas_call | solution.py:804
  557.1 4.1 convert.4
  561.3 10.2 %spread.1 = f32[2048,3,2,256]{3,2,1,0:T(2,128)} custom-call(bf16[1536,2048]{1,0:T(8,128)(2,1)} %get-tuple-element.84.refs_0_), custom_call_target="tpu_custom_call" | custom-call | bytes 18874368 | tf_op jit(solution)/shard_map/spread/pallas_call | solution.py:452
  571.5 9.5 %widened.2 = f32[2048,2048]{1,0:T(8,128)} custom-call(bf16[2048,2048]{1,0:T(8,128)(2,1)} %get-tuple-element.86.in_ref), custom_call_target="tpu_custom_call" | custom-call | bytes 25165824 | tf_op jit(solution)/shard_map/widened/pallas_call | solution.py:431
  581.0 9.5 %widened.3 = f32[2048,2048]{1,0:T(8,128)} custom-call(bf16[2048,2048]{1,0:T(8,128)(2,1)} %get-tuple-element.87.in_ref), custom_call_target="tpu_custom_call" | custom-call | bytes 25165824 | tf_op jit(solution)/shard_map/widened/pallas_call | solution.py:431
  590.6 2.2 fusion.13
  592.8 4.7 fusion.8
  (65 shorter events, 17.1 us)
Async XLA Ops:
  7.2 1.7 copy-start.11
  7.2 81.7 %all-gather.5.cloned.1.call-start = ((), (), s32[]{:S(2)}) async-start(), calls=%async_computation.2 | async-start | bytes 5242880 | tf_op jit(solution)/shard_map/all_gather | solution.py:861
  7.9 161.8 %all-gather.3.cloned.1.call-start = ((), (), s32[]{:S(2)}) async-start(), calls=%async_computation.1 | async-start | bytes 5242880 | tf_op jit(solution)/shard_map/all_gather | solution.py:862
  8.7 584.1 %reduce-scatter.2.cloned.1.call-start = ((), (), s32[]{:S(2)}) async-start(), calls=%async_computation.3 | async-start | bytes 10485760 | tf_op jit(solution)/shard_map/reduce_scatter | solution.py:886
  9.5 14.5 %copy-start.7 = (s32[1024]{0:T(1024)S(1)}, s32[1024]{0:T(1024)}, u32[]{:S(2)}) copy-start(s32[1024]{0:T(1024)} %param.18) | copy-start | bytes 12292
  88.9 17.7 %copy-start.8 = (bf16[2048]{0:T(1024)(128)(2,1)S(1)}, bf16[2048]{0:T(1024)(128)(2,1)}, u32[]{:S(2)}) copy-start(bf16[2048]{0:T(1024)(128)(2,1)} %param.28) | copy-start | bytes 12292
  102.7 30.4 %collective-permute-start = (bf16[1024,1024]{1,0:T(8,128)(2,1)}, bf16[1024,1024]{1,0:T(8,128)(2,1)}, u32[]{:S(2)}, u32[]{:S(2)}) collective-permute-start(bf16[1024,1024]{1,0:T(8,128)(2,1)} %get-tuple-element.56.refs_6_), channel_id=1, source_target_pairs={{0,4},{4,8},{8,12},{12,16},{16,20},{20,24},{24,28},{1,5},{5,9},{9,... | collective-permute-start | bytes 6291464 | tf_op jit(solution)/shard_map/ppermute | solution.py:21
  133.1 42.1 %collective-permute-start.1 = (bf16[1024,1024]{1,0:T(8,128)(2,1)}, bf16[1024,1024]{1,0:T(8,128)(2,1)}, u32[]{:S(2)}, u32[]{:S(2)}) collective-permute-start(bf16[1024,1024]{1,0:T(8,128)(2,1)} %collective-permute-done.refs_5_), channel_id=1, source_target_pairs={{0,4},{4,8},{8,12},{12,16},{16,20},{20,24},{24,28},{1,5},{5,9},{9,... | collective-permute-start | bytes 6291464 | tf_op jit(solution)/shard_map/ppermute | solution.py:21
  135.3 34.4 %copy-start.3 = (bf16[2,256,2048]{2,1,0:T(8,128)(2,1)S(1)}, bf16[2,256,2048]{2,1,0:T(8,128)(2,1)}, u32[]{:S(2)}) copy-start(bf16[2,256,2048]{2,1,0:T(8,128)(2,1)} %param.25) | copy-start | bytes 6291460
  238.7 28.5 %collective-permute-start.2 = (bf16[1024,1024]{1,0:T(8,128)(2,1)}, bf16[1024,1024]{1,0:T(8,128)(2,1)S(1)}, u32[]{:S(2)}, u32[]{:S(2)}) collective-permute-start(bf16[1024,1024]{1,0:T(8,128)(2,1)} %get-tuple-element.68), channel_id=1, source_target_pairs={{4,0},{8,4},{12,8},{16,12},{20,16},{24,20},{28,24},{5,1},{9,5},{13... | collective-permute-start | bytes 6291464 | tf_op jit(solution)/shard_map/ppermute | solution.py:21
  267.2 5.3 copy-start.9
  267.2 5.3 copy-start.10
  267.2 5.3 copy-start
  267.2 5.5 copy-start.1
  270.3 28.3 %collective-permute-start.3 = (bf16[1024,1024]{1,0:T(8,128)(2,1)S(1)}, bf16[1024,1024]{1,0:T(8,128)(2,1)S(1)}, u32[]{:S(2)}, u32[]{:S(2)}) collective-permute-start(bf16[1024,1024]{1,0:T(8,128)(2,1)S(1)} %add_convert_fusion), channel_id=1, source_target_pairs={{4,0},{8,4},{12,8},{16,12},{20,16},{24,20},{28,24},{5,1},{9,5},{13... | collective-permute-start | bytes 6291464 | tf_op jit(solution)/shard_map/ppermute | solution.py:21
  273.4 33.9 %copy-start.6 = (f32[1,2048]{1,0:T(1,128)S(1)}, f32[1,2048]{1,0:T(1,128)}, u32[]{:S(2)}) copy-start(f32[1,2048]{1,0:T(1,128)} %get-tuple-element.78) | copy-start | bytes 24580
  298.6 1.3 copy-start.4
  557.1 40.4 %copy-start.5 = (f32[1,2048]{1,0:T(1,128)}, f32[1,2048]{1,0:T(1,128)S(1)}, u32[]{:S(2)}) copy-start(f32[1,2048]{1,0:T(1,128)S(1)} %get-tuple-element.93) | copy-start | bytes 24580
  590.6 2.3 copy-start.2
Sparse Core Ops, SparseCore 0:
  9.6 79.2 all-gather.4
  90.4 79.2 all-gather.2
  238.8 143.8 reduce-scatter.1

commit v3 on v2

--- a/solution.py
+++ b/solution.py
@@ -176,47 +176,6 @@
         compiler_params=params("arbitrary", "arbitrary"),
         cost_estimate=cost(2 * rows * depth * width, 2 * depth * width + 6 * rows * width),
     )(x, weight, bias)
-
-
-def hidden_kernel(g_ref, w_ref, slope_ref, out_ref, sum_ref):
-    grad = dot_cols(g_ref[...], w_ref[...])
-    low = (grad * slope_ref[...]).astype(BF16)
-    out_ref[...] = low
-    total = jnp.sum(low.astype(F32), 0, keepdims=True)
-
-    @pl.when(pl.program_id(1) == 0)
-    def _():
-        sum_ref[...] = total
-
-    @pl.when(pl.program_id(1) > 0)
-    def _():
-        sum_ref[...] += total
-
-
-def hidden_grads(grad, weight, slope):
-    rows, depth = grad.shape
-    width = weight.shape[0]
-    bm, bn = min(256, rows), min(512, width)
-    return pl.pallas_call(
-        hidden_kernel,
-        name="hidden_grads",
-        grid=(width // bn, rows // bm),
-        in_specs=[
-            pl.BlockSpec((bm, depth), lambda j, i: (i, 0)),
-            pl.BlockSpec((bn, depth), lambda j, i: (j, 0)),
-            pl.BlockSpec((bm, bn), lambda j, i: (i, j)),
-        ],
-        out_specs=[
-            pl.BlockSpec((bm, bn), lambda j, i: (i, j)),
-            pl.BlockSpec((1, bn), lambda j, i: (0, j)),
-        ],
-        out_shape=[
-            jax.ShapeDtypeStruct((rows, width), BF16),
-            jax.ShapeDtypeStruct((1, width), F32),
-        ],
-        compiler_params=params("arbitrary", "arbitrary"),
-        cost_estimate=cost(2 * rows * depth * width, 2 * depth * width + 6 * rows * width),
-    )(grad, weight, slope)
 
 
 def attention_kernel(heads, head_dim, parts, bk, first_ref, q_ref, do_ref, start_ref, *refs):
@@ -363,64 +322,6 @@
     )(first, q, do, start[:, None], *kv_parts)
 
 
-def turn_back_kernel(heads, head_dim, dq_ref, dkv_ref, extra_ref, cos_ref, sin_ref, out_ref, sum_ref):
-    cos_block, sin_block = cos_ref[...], -sin_ref[...]
-    lanes = cos_block.shape[1]
-    width = heads * head_dim
-    for part in range(3):
-        for head in range(heads):
-            at = head * head_dim
-            if part == 0:
-                grad = dq_ref[:, at : at + head_dim]
-            else:
-                low = (part - 1) * width + at
-                grad = dkv_ref[:, low : low + head_dim] + extra_ref[:, low : low + head_dim].astype(F32)
-            to = part * width + at
-            if part < 2:
-                first = turn(grad[:, :lanes], cos_block, sin_block)
-                out_ref[:, to : to + lanes] = first.astype(BF16)
-                out_ref[:, to + lanes : to + head_dim] = grad[:, lanes:].astype(BF16)
-            else:
-                out_ref[:, to : to + head_dim] = grad.astype(BF16)
-    total = jnp.sum(out_ref[...].astype(F32), 0, keepdims=True)
-
-    @pl.when(pl.program_id(0) == 0)
-    def _():
-        sum_ref[...] = total
-
-    @pl.when(pl.program_id(0) > 0)
-    def _():
-        sum_ref[...] += total
-
-
-def turn_back(dq, dkv, extra, cos_table, sin_table, heads, head_dim):
-    rows, width = dq.shape
-    block = min(256, rows)
-    by_row = lambda i: (i, 0)
-    return pl.pallas_call(
-        lambda *refs: turn_back_kernel(heads, head_dim, *refs),
-        name="turn_back",
-        grid=(rows // block,),
-        in_specs=[
-            pl.BlockSpec((block, width), by_row),
-            pl.BlockSpec((block, 2 * width), by_row),
-            pl.BlockSpec((block, 2 * width), by_row),
-            pl.BlockSpec((block, cos_table.shape[1]), by_row),
-            pl.BlockSpec((block, cos_table.shape[1]), by_row),
-        ],
-        out_specs=[
-            pl.BlockSpec((block, 3 * width), by_row),
-            pl.BlockSpec((1, 3 * width), lambda i: (0, 0)),
-        ],
-        out_shape=[
-            jax.ShapeDtypeStruct((rows, 3 * width), BF16),
-            jax.ShapeDtypeStruct((1, 3 * width), F32),
-        ],
-        compiler_params=params("arbitrary"),
-        cost_estimate=cost(0, rows * width * 20),
-    )(dq, dkv, extra, cos_table, sin_table)
-
-
 def widen_kernel(in_ref, out_ref):
     out_ref[...] = in_ref[...].astype(F32)
 
@@ -461,22 +362,28 @@
     )(stacked)
 
 
-def reduce_kernel(plan, chunks, bits, tensor, *refs):
+def reduce_kernel(plan, dims, *refs):
+    chunks, bits, tensor, heads, head_dim, blocks, wide_b = dims
     refs = list(refs)
     take = lambda count: [refs.pop(0) for _ in range(count)]
-    a_refs = take(len(plan))
-    b_refs = take(3)
-    vec_ref, dqkv_ref, hg_ref, gain1_ref, gain2_ref, mean_ref, inverse_ref = take(7)
-    w1_ref, w2_ref, x_ref = take(3)
+    g_ref, n1_ref, slope_ref, up_ref, down_ref, w1_ref, x_ref, wout_ref, forward_ref = take(9)
+    far_ref, near_ref, own_ref, dq_ref = take(4)
+    extra_refs = take(wide_b)
+    lefts = take(sum(1 for item in plan if item[3]))
+    att_ref, vec_ref, gain1_ref, gain2_ref, mean_ref, inverse_ref, cos_ref, sin_ref = take(8)
     out_refs = take(len(plan))
-    dsum_ref, total_ref = take(2)
-    abuf, full, r0, ag = take(4)
-    w1buf, w2buf, xbuf, zsend, mine_ref, w_sem = take(6)
+    down_own, dgot, branch_own, bgot, total_ref = take(5)
+    abuf, full, r0, ag, gbuf, hg, dqkv = take(7)
     kept, sent, got = take(bits - 1), take(bits - 1), take(bits - 1)
-    dgot, vgot, vsend, vnow = take(4)
+    w1buf, w2buf, xbuf, sbuf, wobuf, fbuf, zsend, zown, mine_ref = take(9)
+    near_buf, own_buf, dq_buf, hop_send, far_got, near_got = take(6)
+    vgot, vsend, vnow = take(3)
     a_sem, o_sem, send_sem, recv_sem, d_send, d_recv, v_send, v_recv = take(8)
+    w_sem, b_sem, h_sem, hop_sems, z_sem = take(5)
     index, me = lax.axis_index("dp"), lax.axis_index("tensor")
+    last = (1 << bits) - 1
     deep, wide = full.shape[1], full.shape[2]
+    rows_all = gbuf.shape[0]
     slots, ring, lag = r0.shape[0], ag.shape[0], 2
 
     def bit_of(bit):
@@ -486,43 +393,242 @@
         return index + (1 << bit) * (1 - 2 * bit_of(bit))
 
     barrier = pltpu.get_barrier_semaphore()
+
+    def greet(axis, to):
+        pl.semaphore_signal(barrier, inc=1, device_id={axis: to}, device_id_type=MESH)
+
     for bit in range(bits):
-        pl.semaphore_signal(barrier, inc=1, device_id={"dp": partner(bit)}, device_id_type=MESH)
+        greet("dp", partner(bit))
     for k in range(1, tensor):
-        other = lax.rem(me + k, tensor)
-        pl.semaphore_signal(barrier, inc=1, device_id={"tensor": other}, device_id_type=MESH)
-    pl.semaphore_wait(barrier, bits + tensor - 1)
-
-    own_rows = dsum_ref.shape[0]
+        greet("tensor", lax.rem(me + k, tensor))
+
+    @pl.when(index > 0)
+    def _():
+        greet("dp", index - 1)
+
+    @pl.when(index < last)
+    def _():
+        greet("dp", index + 1)
+
+    inner = jnp.where(index > 0, 1, 0) + jnp.where(index < last, 1, 0)
+    pl.semaphore_wait(barrier, bits + tensor - 1 + inner)
+
+    hidden_units = hg.shape[1] // deep
+
+    def columns_of(u):
+        return pl.ds(pl.multiple_of(u * deep, deep), deep)
+
+    def hidden_copies(u):
+        slot = lax.rem(u, 2)
+        return [
+            pltpu.make_async_copy(down_ref.at[columns_of(u)], w2buf.at[slot], w_sem.at[1, slot]),
+            pltpu.make_async_copy(slope_ref.at[:, columns_of(u)], sbuf.at[slot], w_sem.at[3, slot]),
+        ]
+
+    row_step = min(256, rows_all)
+
+    def hidden_unit(u):
+        slot, columns = lax.rem(u, 2), columns_of(u)
+
+        @pl.when(u + 1 < hidden_units)
+        def _():
+            for copy in hidden_copies(u + 1):
+                copy.start()
+
+        for copy in hidden_copies(u):
+            copy.wait()
+
+        def row_block(i, total):
+            rows = pl.ds(pl.multiple_of(i * row_step, row_step), row_step)
+            grad = dot_cols(gbuf[rows, :], w2buf[slot])
+            low = (grad * sbuf[slot, rows, :]).astype(BF16)
+            hg[rows, columns] = low
+            return total + jnp.sum(low.astype(F32), 0, keepdims=True)
+
+        total = lax.fori_loop(0, rows_all // row_step, row_block, jnp.zeros((1, deep), F32))
+        mine_ref[5:6, columns] = total
+
+    block = rows_all // blocks
+    width = heads * head_dim
+
+    def block_of(p):
+        return pl.ds(pl.multiple_of(p * block, block), block)
+
+    def far_copy(p):
+        return pltpu.make_async_remote_copy(
+            src_ref=far_ref.at[block_of(p)],
+            dst_ref=far_got.at[block_of(p)],
+            send_sem=hop_sems.at[0, p],
+            recv_sem=hop_sems.at[1, p],
+            device_id={"dp": jnp.maximum(index - 1, 0)},
+            device_id_type=MESH,
+        )
+
+    def near_copy(p):
+        return pltpu.make_async_remote_copy(
+            src_ref=hop_send.at[lax.rem(p, 4)],
+            dst_ref=near_got.at[block_of(p)],
+            send_sem=hop_sems.at[2, p],
+            recv_sem=hop_sems.at[3, p],
+            device_id={"dp": jnp.maximum(index - 1, 0)},
+            device_id_type=MESH,
+        )
+
+    def near_load(p):
+        slot = lax.rem(p, 2)
+        return pltpu.make_async_copy(near_ref.at[block_of(p)], near_buf.at[slot], h_sem.at[0, slot])
+
+    def own_loads(p):
+        slot = lax.rem(p, 2)
+        return [
+            pltpu.make_async_copy(own_ref.at[block_of(p)], own_buf.at[slot], h_sem.at[1, slot]),
+            pltpu.make_async_copy(dq_ref.at[block_of(p)], dq_buf.at[slot], h_sem.at[2, slot]),
+        ]
+
+    def far_start(p):
+        @pl.when(index > 0)
+        def _():
+            far_copy(p).start()
+
+    def relay(p):
+        slot = lax.rem(p, 2)
+
+        @pl.when(index > 0)
+        def _():
+            far_copy(p).wait_send()
+
+        near_load(p).wait()
+
+        @pl.when(index < last)
+        def _():
+            far_copy(p).wait_recv()
+            near_buf[slot] += far_got[block_of(p)].astype(F32)
+
+        @pl.when(index > 0)
+        def _():
+            hop_send[lax.rem(p, 4)] = near_buf[slot].astype(BF16)
+            near_copy(p).start()
+
+    def turn_block(p):
+        slot, rows = lax.rem(p, 2), block_of(p)
+
+        @pl.when(index > 0)
+        def _():
+            near_copy(p).wait_send()
+
+        for copy in own_loads(p):
+            copy.wait()
+
+        @pl.when(index < last)
+        def _():
+            near_copy(p).wait_recv()
+            own_buf[slot] += near_got[rows].astype(F32)
+
+        cos_block, sin_block = cos_ref[rows, :], -sin_ref[rows, :]
+        lanes = cos_block.shape[1]
+        for part in range(3):
+            for head in range(heads):
+                at = head * head_dim
+                to = part * width + at
+                if part == 0:
+                    grad = dq_buf[slot, :, at : at + head_dim]
+                else:
+                    low = (part - 1) * width + at
+                    grad = own_buf[slot, :, low : low + head_dim]
+                if part < 2:
+                    first = turn(grad[:, :lanes], cos_block, sin_block)
+                    grad = jnp.concatenate([first, grad[:, lanes:]], 1)
+                low_grad = grad.astype(BF16)
+                dqkv[rows, to : to + head_dim] = low_grad
+                mine_ref[6:7, to : to + head_dim] += jnp.sum(
+                    low_grad.astype(F32), 0, keepdims=True
+                )
+
+    own_rows = down_own.shape[0]
     units = wide // deep
     zslots = zsend.shape[0]
-    begin = max(chunks // 2, 1)
-
-    def columns_of(u):
-        return pl.ds(pl.multiple_of(u * deep, deep), deep)
-
-    def d_copy(k, u):
+    begin = max(chunks // 2, blocks + 4)
+
+    def z_copy(k, v, target):
         other = lax.rem(me + k, tensor)
         rows = pl.ds(pl.multiple_of(other * own_rows, own_rows), own_rows)
         return pltpu.make_async_remote_copy(
-            src_ref=zsend.at[lax.rem(u, zslots), rows],
-            dst_ref=dgot.at[k - 1, :, columns_of(u)],
-            send_sem=d_send.at[k - 1, u],
-            recv_sem=d_recv.at[k - 1, u],
+            src_ref=zsend.at[lax.rem(v, zslots), rows],
+            dst_ref=target.at[k - 1, :, columns_of(lax.rem(v, units))],
+            send_sem=d_send.at[k - 1, v],
+            recv_sem=d_recv.at[k - 1, v],
             device_id={"tensor": other},
             device_id_type=MESH,
         )
+
+    def own_copy(v, target):
+        slot = lax.rem(v, 2)
+        return pltpu.make_async_copy(
+            zown.at[slot], target.at[:, columns_of(lax.rem(v, units))], z_sem.at[slot]
+        )
+
+    def z_clear(v):
+        @pl.when(v >= zslots)
+        def _():
+            for k in range(1, tensor):
+                z_copy(k, v - zslots, dgot).wait_send()
+
+        @pl.when(v >= 2)
+        def _():
+            own_copy(v - 2, down_own).wait()
+
+    def z_put(v, i, rows, value):
+        zsend[lax.rem(v, zslots), rows] = value.astype(BF16)
+
+        @pl.when(i == me)
+        def _():
+            zown[lax.rem(v, 2)] = value
+
+    def z_start(v, target, own_target):
+        for k in range(1, tensor):
+            z_copy(k, v, target).start()
+        own_copy(v, own_target).start()
+
+    def branch_copies(u):
+        slot = lax.rem(u, 2)
+        return [
+            pltpu.make_async_copy(wout_ref.at[:, columns_of(u)], wobuf.at[slot], w_sem.at[4, slot]),
+            pltpu.make_async_copy(forward_ref.at[:, columns_of(u)], fbuf.at[slot], w_sem.at[5, slot]),
+        ]
+
+    def branch_unit(u):
+        slot = lax.rem(u, 2)
+
+        @pl.when(u + 1 < units)
+        def _():
+            for copy in branch_copies(u + 1):
+                copy.start()
+
+        for copy in branch_copies(u):
+            copy.wait()
+
+        z_clear(u)
+
+        def row_block(i, carry):
+            rows = pl.ds(pl.multiple_of(i * own_rows, own_rows), own_rows)
+            z_put(u, i, rows, dot(att_ref[rows, :], wobuf[slot]) + fbuf[slot, rows, :])
+            return carry
+
+        lax.fori_loop(0, tensor, row_block, 0)
+        z_start(u, bgot, branch_own)
 
     def unit_copies(u):
         slot = lax.rem(u, 2)
         return [
             pltpu.make_async_copy(w1_ref.at[columns_of(u)], w1buf.at[slot], w_sem.at[0, slot]),
-            pltpu.make_async_copy(w2_ref.at[columns_of(u)], w2buf.at[slot], w_sem.at[1, slot]),
+            pltpu.make_async_copy(
+                up_ref.at[columns_of(u)], w2buf.at[slot, :, pl.ds(0, hg.shape[1])], w_sem.at[1, slot]
+            ),
             pltpu.make_async_copy(x_ref.at[:, columns_of(u)], xbuf.at[slot], w_sem.at[2, slot]),
         ]
 
     def unit(u):
-        slot, zslot = lax.rem(u, 2), lax.rem(u, zslots)
+        slot, v = lax.rem(u, 2), units + u
         columns = columns_of(u)
 
         @pl.when(u + 1 < units)
@@ -533,25 +639,16 @@
         for copy in unit_copies(u):
             copy.wait()
 
-        @pl.when(u >= zslots)
-        def _():
-            for k in range(1, tensor):
-                d_copy(k, u - zslots).wait_send()
-
+        z_clear(v)
         gain1, gain2 = gain1_ref[:, columns], gain2_ref[:, columns]
         mine_ref[0:4, columns] = jnp.zeros((4, deep), F32)
 
         def row_block(i, carry):
             rows = pl.ds(pl.multiple_of(i * own_rows, own_rows), own_rows)
-            one = dot_cols(dqkv_ref[rows, :], w1buf[slot])
-            two = dot_cols(hg_ref[rows, :], w2buf[slot])
+            one = dot_cols(dqkv[rows, :], w1buf[slot])
+            two = dot_cols(hg[rows, :], w2buf[slot, :, : hg.shape[1]])
             both = one * gain1 + two * gain2
-            zsend[zslot, rows] = both.astype(BF16)
-
-            @pl.when(i == me)
-            def _():
-                dsum_ref[:, columns] = both
-
+            z_put(v, i, rows, both)
             standard = (xbuf[slot, rows].astype(F32) - mean_ref[rows, :]) * inverse_ref[rows, :]
             add = lambda v: jnp.sum(v, 0, keepdims=True)
             mine_ref[0:4, columns] += jnp.concatenate(
@@ -560,8 +657,7 @@
             return carry
 
         lax.fori_loop(0, tensor, row_block, 0)
-        for k in range(1, tensor):
-            d_copy(k, u).start()
+        z_start(v, dgot, down_own)
 
     def v_copy(k, to, slot):
         return pltpu.make_async_remote_copy(
@@ -583,15 +679,33 @@
             device_id_type=MESH,
         )
 
+    left_at = {}
+    for item, entry in enumerate(plan):
+        if entry[3]:
+            left_at[item] = lefts[len(left_at)]
+
     def fetch_copy(item, c):
         column = pl.multiple_of((c - plan[item][0]) * deep, deep)
         slot = lax.rem(c, 2)
         return pltpu.make_async_copy(
-            a_refs[item].at[:, pl.ds(column, deep)], abuf.at[slot], a_sem.at[slot]
+            left_at[item].at[:, pl.ds(column, deep)], abuf.at[slot], a_sem.at[slot]
         )
 
+    def fetch(c):
+        def start(item):
+            if item in left_at:
+                fetch_copy(item, c).start()
+
+        on_items(c, start)
+
+    def g_copy():
+        return pltpu.make_async_copy(g_ref, gbuf, b_sem.at[0])
+
+    def n1_copy():
+        return pltpu.make_async_copy(n1_ref, gbuf, b_sem.at[1])
+
     def on_items(c, act):
-        for item, (first, count, _) in enumerate(plan):
+        for item, (first, count, _, _, _) in enumerate(plan):
             @pl.when((c >= first) & (c < first + count))
             def _():
                 act(item)
@@ -650,9 +764,15 @@
         slot = lax.rem(c, 3)
 
         def with_item(item):
-            fetch_copy(item, c).wait()
-            left = abuf[lax.rem(c, 2)].T
-            right = b_refs[plan[item][2]]
+            _, _, right, _, local = plan[item]
+            right = gbuf if right is None else hg if right == "hidden" else extra_refs[right]
+            if item in left_at:
+                fetch_copy(item, c).wait()
+                left = abuf[lax.rem(c, 2)].T
+            else:
+                column = pl.multiple_of((c - plan[item][0]) * deep, deep)
+                held = {"hidden": hg, "projected": dqkv, "attended": att_ref}[local]
+                left = held[:, pl.ds(column, deep)].T
             step = min(512, wide)
             for column in range(0, wide, step):
                 full[slot, :, column : column + step] = dot(left, right[:, column : column + step])
@@ -702,10 +822,12 @@
         up_copy(0, c).wait()
         on_items(c, lambda item: out_copy(item, c).start())
 
-    on_items(0, lambda item: fetch_copy(item, 0).start())
-    for copy in unit_copies(0):
+    fetch(0)
+    g_copy().start()
+    for copy in hidden_copies(0) + branch_copies(0):
         copy.start()
     mine_ref[...] = vec_ref[...]
+    g_copy().wait()
 
     def stage(t, delay, act):
         c = t - delay
@@ -722,8 +844,22 @@
     def iteration(t, carry):
         @pl.when(t + 1 < chunks)
         def _():
-            on_items(t + 1, lambda item: fetch_copy(item, t + 1).start())
-
+            fetch(t + 1)
+
+        @pl.when(t == plan[2][0])
+        def _():
+            n1_copy().start()
+
+        @pl.when(t == plan[3][0])
+        def _():
+            n1_copy().wait()
+
+        @pl.when(t == begin - 1)
+        def _():
+            for copy in unit_copies(0):
+                copy.start()
+
+        stage_of(t, 0, blocks, far_start)
         stage(
             t, 2 * bits * lag + 1,
             lambda c: on_items(c, lambda item: out_copy(item, c).wait()),
@@ -735,6 +871,12 @@
             stage(t, level * lag, lambda c, level=level: halve(level, c))
         stage(t, 0, multiply)
 
+        stage_of(t, 1, blocks, lambda p: near_load(p).start())
+        stage_of(t, 2, blocks, relay)
+        stage_of(t, 3, blocks, lambda p: [copy.start() for copy in own_loads(p)])
+        stage_of(t, 4, blocks, turn_block)
+        stage_of(t, 0, hidden_units, hidden_unit)
+        stage_of(t, 0, units, branch_unit)
         stage_of(t, begin, units, unit)
 
         @pl.when(t == begin + units)
@@ -773,42 +915,58 @@
 
     def gather(u, carry):
         for k in range(1, tensor):
-            d_copy(k, u).wait_recv()
+            z_copy(k, u, bgot).wait_recv()
+            z_copy(k, units + u, dgot).wait_recv()
         return carry
 
     lax.fori_loop(0, units, gather, 0)
-    for u in range(max(units - zslots, 0), units):
+    for v in range(2 * units - zslots, 2 * units):
         for k in range(1, tensor):
-            d_copy(k, u).wait_send()
-    rest = dsum_ref[...]
-    for k in range(1, tensor):
-        rest = rest + dgot[k - 1].astype(F32)
-    dsum_ref[...] = rest
-
-
-def reduce_grads(items, rights, vectors, moments_of, pair_one, pair_two, x, bits, tensor):
+            z_copy(k, v, dgot).wait_send()
+    for v in range(2 * units - 2, 2 * units):
+        own_copy(v, down_own).wait()
+
+
+def reduce_grads(pairs, kv_grads, dq, vectors, tables, moments_of, gains, weights, x, sizes):
+    act, att, n2, grads, n1, slope, forward = pairs
+    bits, tensor, heads, head_dim = sizes
+    fc1_weight, fc2_weight, w1, flat_out = weights
     deep = 256
-    rows, wide = rights[0].shape
+    rows, wide = grads.shape
+    hidden_width, width = act.shape[1], heads * head_dim
+    natural = hidden_width == wide
+    shapes = [
+        (hidden_width, None, True, None),
+        (width, None, False, "attended"),
+        (wide, "hidden", True, None) if natural else (hidden_width, 0, False, "hidden"),
+        (3 * width, None, False, "projected"),
+    ]
     plan, first = [], 0
-    for left, which in items:
-        count = left.shape[1] // deep
-        plan.append((first, count, which))
-        first += count
-    chunks, ring, slots = first, 4 * bits - 2, 4
+    for size, right, fetched, local in shapes:
+        plan.append((first, size // deep, right, fetched, local))
+        first += size // deep
+    chunks, ring, slots, zslots = first, 4 * bits - 2, 4, 3
+    blocks = 8 if chunks >= 20 else 4
+    block = rows // blocks
+    own_rows, units = rows // tensor, wide // deep
     halves_of = [deep >> (level + 1) for level in range(1, bits)]
-    own_rows = rows // tensor
-    (dqkv, w1, gain1), (hg, w2, gain2), (mean, inverse) = pair_one, pair_two, moments_of
-    units, zslots = wide // deep, 3
     hbm = pl.BlockSpec(memory_space=pl.ANY)
     vmem = pl.BlockSpec(memory_space=pltpu.VMEM)
+    lefts = [act, n2] if natural else [act]
+    extra = [] if natural else [n2]
+    dims = (chunks, bits, tensor, heads, head_dim, blocks, len(extra))
     return pl.pallas_call(
-        lambda *refs: reduce_kernel(plan, chunks, bits, tensor, *refs),
+        lambda *refs: reduce_kernel(plan, dims, *refs),
         name="reduce_grads",
-        in_specs=[hbm] * len(items) + [vmem] * 10 + [hbm] * 3,
-        out_specs=[hbm] * len(items) + [vmem, vmem],
+        in_specs=[hbm] * 13 + [vmem] * len(extra) + [hbm] * len(lefts) + [vmem] * 8,
+        out_specs=[hbm] * 8 + [vmem],
         out_shape=[
-            *[jax.ShapeDtypeStruct((left.shape[1], wide), BF16) for left, _ in items],
-            jax.ShapeDtypeStruct((own_rows, wide), F32),
+            *[jax.ShapeDtypeStruct((item[0], wide), BF16) for item in shapes],
+            *[
+                jax.ShapeDtypeStruct((own_rows, wide), F32),
+                jax.ShapeDtypeStruct((tensor - 1, own_rows, wide), BF16),
+            ]
+            * 2,
             jax.ShapeDtypeStruct(vectors.shape, F32),
         ],
         scratch_shapes=[
@@ -816,16 +974,27 @@
             pltpu.VMEM((3, deep, wide), F32),
             pltpu.VMEM((slots, deep // 2, wide), F32),
             pltpu.VMEM((ring, deep, wide), BF16),
-            pltpu.VMEM((2, deep, w1.shape[1]), BF16),
-            pltpu.VMEM((2, deep, w2.shape[1]), BF16),
-            pltpu.VMEM((2, rows, deep), BF16),
-            pltpu.VMEM((zslots, rows, deep), BF16),
-            pltpu.VMEM(vectors.shape, F32),
-            pltpu.SemaphoreType.DMA((3, 2)),
+            pltpu.VMEM((rows, wide), BF16),
+            pltpu.VMEM((rows, hidden_width), BF16),
+            pltpu.VMEM((rows, 3 * width), BF16),
             *[pltpu.VMEM((slots, half, wide), F32) for half in halves_of],
             *[pltpu.VMEM((slots, half, wide), BF16) for half in halves_of],
             *[pltpu.VMEM((slots, half, wide), BF16) for half in halves_of],
-            pltpu.VMEM((tensor - 1, own_rows, wide), BF16),
+            pltpu.VMEM((2, deep, 3 * width), BF16),
+            pltpu.VMEM((2, deep, wide), BF16),
+            pltpu.VMEM((2, rows, deep), BF16),
+            pltpu.VMEM((2, rows, deep), F32),
+            pltpu.VMEM((2, width, deep), BF16),
+            pltpu.VMEM((2, rows, deep), F32),
+            pltpu.VMEM((zslots, rows, deep), BF16),
+            pltpu.VMEM((2, own_rows, deep), F32),
+            pltpu.VMEM(vectors.shape, F32),
+            pltpu.VMEM((2, block, 2 * width), F32),
+            pltpu.VMEM((2, block, 2 * width), F32),
+            pltpu.VMEM((2, block, width), F32),
+            pltpu.VMEM((4, block, 2 * width), BF16),
+            pltpu.VMEM((rows, 2 * width), BF16),
+            pltpu.VMEM((rows, 2 * width), BF16),
             pltpu.VMEM((tensor, *vectors.shape), F32),
             pltpu.VMEM((bits, *vectors.shape), F32),
             pltpu.VMEM((bits, *vectors.shape), F32),
@@ -833,18 +1002,25 @@
             pltpu.SemaphoreType.DMA((ring,)),
             pltpu.SemaphoreType.DMA((2 * bits, ring)),
             pltpu.SemaphoreType.DMA((2 * bits, ring)),
-            pltpu.SemaphoreType.DMA((tensor - 1, units)),
-            pltpu.SemaphoreType.DMA((tensor - 1, units)),
+            pltpu.SemaphoreType.DMA((tensor - 1, 2 * units)),
+            pltpu.SemaphoreType.DMA((tensor - 1, 2 * units)),
             pltpu.SemaphoreType.DMA((tensor + bits,)),
             pltpu.SemaphoreType.DMA((tensor + bits,)),
+            pltpu.SemaphoreType.DMA((6, 2)),
+            pltpu.SemaphoreType.DMA((2,)),
+            pltpu.SemaphoreType.DMA((3, 2)),
+            pltpu.SemaphoreType.DMA((4, blocks)),
+            pltpu.SemaphoreType.DMA((2,)),
         ],
         compiler_params=pltpu.CompilerParams(
-            collective_id=0, has_side_effects=True, vmem_limit_bytes=62 << 20
+            collective_id=0, has_side_effects=True, vmem_limit_bytes=63 << 20
         ),
-        cost_estimate=cost(2 * rows * chunks * deep * wide, 8 * chunks * deep * wide),
+        cost_estimate=cost(
+            2 * rows * wide * (chunks * deep + 2 * hidden_width + 3 * width), 8 * chunks * deep * wide
+        ),
     )(
-        *[left for left, _ in items], *rights, vectors, dqkv, hg, gain1, gain2, mean, inverse,
-        w1, w2, x,
+        grads, n1, slope, fc1_weight, fc2_weight, w1, x, flat_out, forward, *kv_grads, dq,
+        *extra, *lefts, att, vectors, *gains, *moments_of, *tables,
     )
 
 
@@ -881,37 +1057,20 @@
     attended, query_grad, *kv_grads = attention(
         queries, kv_parts, attended_grad, positions, heads, head_dim
     )
-    grads_all, attended, query_grad, *kv_grads = tie((grads_all, attended, query_grad, *kv_grads))
-    partial = dot(attended, flat_out) + forward
-    branch = lax.psum_scatter(partial, "tensor", scatter_dimension=0, tiled=True)
-    hidden_grad, fc1_bias_grad = hidden_grads(grads_all, fc2_weight, slope)
-    extra = None
-    for part in kv_grads[:-1]:
-        if extra is not None:
-            part = (part + extra.astype(F32)).astype(BF16)
-        extra = shifted(part, "dp", -1)
-        extra, hidden_grad = tie((extra, hidden_grad))
-    qkv_grad, qkv_bias_grad = turn_back(
-        query_grad, kv_grads[-1], extra, cos_table, sin_table, heads, head_dim
+    own_grad = out_grad.astype(F32)
+    vectors = jnp.pad(jnp.sum(own_grad, 0, keepdims=True), ((4, 3), (0, 0)))
+    bits = (lax.axis_size("dp") - 1).bit_length()
+    *stacked, d_sum, d_got, branch, b_got, vectors = reduce_grads(
+        (activated, attended, normed_two, grads_all, normed_one, slope, forward), kv_grads, query_grad,
+        vectors, (cos_table, sin_table), (mean, inverse), (row(norm1_gain), row(norm2_gain)),
+        (fc1_weight, fc2_weight, flat_qkv, flat_out), rows_all,
+        (bits, lax.axis_size("tensor"), heads, head_dim),
     )
-    wide = lambda v: jnp.pad(v, ((0, 0), (0, model_width - v.shape[1])))
-    own_grad = out_grad.astype(F32)
-    vectors = jnp.concatenate(
-        [
-            jnp.zeros((4, model_width), F32), jnp.sum(own_grad, 0, keepdims=True), wide(fc1_bias_grad), wide(qkv_bias_grad),
-            jnp.zeros((1, model_width), F32),
-        ],
-        0,
-    )
-    bits = (lax.axis_size("dp") - 1).bit_length()
+    for k in range(d_got.shape[0]):
+        d_sum = d_sum + d_got[k].astype(F32)
+        branch = branch + b_got[k].astype(F32)
+    fc2_grad, out_weight_grad, fc1_grad, qkv_weight_grad = stacked
     natural = hidden_width == model_width
-    fc1_pair = (normed_two, hidden_grad) if natural else (hidden_grad, normed_two)
-    fc2_grad, out_weight_grad, fc1_grad, qkv_weight_grad, d_sum, vectors = reduce_grads(
-        [(activated, 0), (attended, 0), (fc1_pair[0], 1), (qkv_grad, 2)],
-        [grads_all, fc1_pair[1], normed_one],
-        vectors, (mean, inverse), (qkv_grad, flat_qkv, row(norm1_gain)),
-        (hidden_grad, fc1_weight, row(norm2_gain)), rows_all, bits, lax.axis_size("tensor"),
-    )
     fc2_grad = widened(fc2_grad)
     out_weight_grad = out_weight_grad.astype(F32).reshape(heads, head_dim, model_width)
     fc1_grad = widened(fc1_grad) if natural else fc1_grad.T.astype(F32)

time: 606 us -> 579 us (0.955)
  waiting for transfers between devices: 112 us -> 81.1 us
  Pallas kernels: 397 us -> 416 us
  matrix products: 29.5 us -> 20.1 us
    ppermute x4 -> x2, waiting for transfers between devices: 29.4 us -> 0.01 us  [shifted(): return lax.ppermute(x, axis, pairs)]
    pallas_call x3 -> x1, Pallas kernels: 275 us -> 295 us  [reduce_grads(): pl.pallas_call(lambda *refs: reduce_kernel(plan, dims, *refs), name='redu...]
    dot_general x2 -> x1, matrix products: 24 us -> 14.6 us  [dot(): return jnp.dot(first, second, preferred_element_type=F32)]
  transfers between devices with their start and end apart: 7 -> 4, of which waited for: 4 -> 2; matrix products, arithmetic and copies ran while one was open for 9% -> 7% of each run, Pallas kernels for 57% -> 7%
where the time goes in v3:
time: 579 us; the launch traced here: 576 us
  Pallas kernels  416 us (72%)
  waiting for transfers between devices  81.1 us (14%)
  local copies, waits for them, and re-layouts  21.1 us (4%)
  matrix products  20.1 us (3%)
  other arithmetic  16.9 us (3%)
  between operations  14.2 us (2%)
  starting transfers between devices  6.2 us (1%)
    pallas_call x1, Pallas kernels, reduce_grads(): pl.pallas_call(lambda *refs: reduce_kernel(plan, dims, *refs), name='redu...  295 us
    all_gather x1, waiting for transfers between devices, body(): rows_all = lax.all_gather(tokens, 'tensor', axis=0, tiled=True)  61.6 us
    pallas_call x1, Pallas kernels, attention(): pl.pallas_call(lambda *refs: attention_kernel(heads, head_dim, parts, bk,...  54.2 us
    pallas_call x1, Pallas kernels, up(): pl.pallas_call(up_kernel, name='up', grid=(width // bn, rows // bm), in_s...  24.3 us
    pallas_call x2, Pallas kernels, widened(): pl.pallas_call(widen_kernel, name='widened', grid=(rows // block,), in_sp...  19.1 us
    all_gather x1, waiting for transfers between devices, body(): grads_all = lax.all_gather(out_grad, 'tensor', axis=0, tiled=True)  18.1 us
    dot_general x1, matrix products, dot(): return jnp.dot(first, second, preferred_element_type=F32)  14.6 us
    reshape x1, local copies, waits for them, and re-layouts, body(): jnp.transpose(qkv_weight, (0, 2, 1, 3)).reshape(model_width, 3 * width)  14.5 us
  transfers between devices with their start and end apart: 4, of which 2 were waited for; matrix products, arithmetic and copies ran while one was open for 7% of the time, Pallas kernels for 7%

profile of v3, /device:TPU:11, one launch (start us, length us, event | category | flops | bytes accessed | tf_op | source)
XLA Modules:
  0.0 576.0 jit_solution(1597573824840894239)
XLA Ops:
  7.2 0.7 all-gather.5.cloned.1.call-update
  8.0 0.7 all-gather.3.cloned.1.call-update
  8.8 14.5 %reshape.117.refs_5_ = bf16[2048,1536]{1,0:T(8,128)(2,1)} reshape(bf16[2048,3,2,256]{3,2,1,0:T(2,128)(2,1)} %bitcast.47) | data formatting | bytes 12582912 | tf_op jit(solution)/shard_map/reshape | solution.py:1040
  24.0 1.9 fusion.12
  25.9 1.3 maximum_maximum_fusion
  27.2 61.6 %all-gather.5.cloned.1.call-done.refs_0_.refs_6_ = bf16[1024,2048]{1,0:T(8,128)(2,1)} async-done(((bf16[256,2048]{1,0:T(8,128)(2,1)}), bf16[1024,2048]{1,0:T(8,128)(2,1)}) %all-gather.5.cloned.1.call-update) | async-done | bytes 4194320 | tf_op jit(solution)/shard_map/all_gather | solution.py:1037
  88.9 13.9 %project.1 = (bf16[1024,2048]{1,0:T(8,128)(2,1)}, bf16[1024,2048]{1,0:T(8,128)(2,1)}, bf16[1024,512]{1,0:T(8,128)(2,1)}, bf16[1024,1024]{1,0:T(8,128)(2,1)}, f32[1024,1]{1,0:T(8,128)}, /*index=5*/f32[1024,1]{1,0:T(8,128)}) custom-call(bf16[1024,2048]{1,0:T(8,128)(2,1)} %all-gather.5.cloned.1.call-done.refs_0_.refs_6_, f32[1,2048]{1,0:T(1,128)} %bitcast.64, ...), custom_call_target="tpu_custom_call" | custom-call | flops 6442450944 | bytes 18874368 | tf_op jit(solution)/shard_map/project/pallas_call | solution.py:117
  102.8 4.0 collective-permute-start
  107.4 1.0 copy.31.refs_3_
  110.5 24.3 %up.1 = (bf16[1024,2048]{1,0:T(8,128)(2,1)}, f32[1024,2048]{1,0:T(8,128)}) custom-call(bf16[1024,2048]{1,0:T(8,128)(2,1)} %get-tuple-element.40.x_ref.refs_14_, bf16[2048,2048]{1,0:T(8,128)(2,1)} %refs_3_.1, f32[1,2048]{1,0:T(1,128)} %bitcast.58), custom_call_target="tpu_custom_call" | custom-call | flops 8589934592 | bytes 20971520 | tf_op jit(solution)/shard_map/up/pallas_call | solution.py:162
  134.8 2.2 collective-permute-start.1
  137.0 14.6 %fusion.15.refs_8_ = f32[1024,2048]{1,0:T(8,128)} fusion(bf16[1024,2048]{1,0:T(8,128)(2,1)} %get-tuple-element.53.refs_13_, bf16[2048,2048]{1,0:T(8,128)(2,1)} %refs_4_.1), kind=kOutput, calls=%fused_computation.43 | convolution fusion | flops 8589934592 | bytes 20971520 | tf_op jit(solution)/shard_map/dot_general | solution.py:38
  151.6 18.1 %all-gather.3.cloned.1.call-done.refs_0_ = bf16[1024,2048]{1,0:T(8,128)(2,1)} async-done(((bf16[256,2048]{1,0:T(8,128)(2,1)}), bf16[1024,2048]{1,0:T(8,128)(2,1)}) %all-gather.3.cloned.1.call-update) | async-done | bytes 4194320 | tf_op jit(solution)/shard_map/all_gather | solution.py:1038
  169.7 5.5 convolution_convert_fusion.refs_2_
  175.2 54.2 %attention.1 = (bf16[1024,512]{1,0:T(8,128)(2,1)}, f32[1024,512]{1,0:T(8,128)}, bf16[1024,1024]{1,0:T(8,128)(2,1)}, f32[1024,1024]{1,0:T(8,128)}, f32[1024,1024]{1,0:T(8,128)}) custom-call(s32[4]{0:T(128)} %and_select_fusion.refs_0_, bf16[1024,512]{1,0:T(8,128)(2,1)} %get-tuple-element.47.refs_1_, bf16[1024,512]{1,0:T(8,128)(2,1)} %convolution_convert_fusion.refs_2_, ...), custom_call_target="tpu_custom_call" | custom-call | flops 12582912000 | bytes 12582912 | tf_op jit(solution)/shard_map/attention/pallas_call | solution.py:289
  229.4 294.5 %reduce_grads.1 = (bf16[2048,2048]{1,0:T(8,128)(2,1)}, bf16[512,2048]{1,0:T(8,128)(2,1)}, bf16[2048,2048]{1,0:T(8,128)(2,1)}, bf16[1536,2048]{1,0:T(8,128)(2,1)}...) custom-call(bf16[1024,2048]{1,0:T(8,128)(2,1)} %all-gather.3.cloned., ...), custom_call_target="tpu_custom_call" | custom-call | flops 49392123904 | bytes 100663296 | tf_op jit(solution)/shard_map/reduce_grads/pallas_call | solution.py:958
  523.9 2.0 fusion.14
  525.9 0.8 slice_reduce_fusion
  526.7 9.5 %widened.2 = f32[2048,2048]{1,0:T(8,128)} custom-call(bf16[2048,2048]{1,0:T(8,128)(2,1)} %get-tuple-element.64.in_ref), custom_call_target="tpu_custom_call" | custom-call | bytes 25165824 | tf_op jit(solution)/shard_map/widened/pallas_call | solution.py:332
  536.3 9.5 %widened.3 = f32[2048,2048]{1,0:T(8,128)} custom-call(bf16[2048,2048]{1,0:T(8,128)(2,1)} %get-tuple-element.65.in_ref), custom_call_target="tpu_custom_call" | custom-call | bytes 25165824 | tf_op jit(solution)/shard_map/widened/pallas_call | solution.py:332
  545.8 10.4 %spread.1 = f32[2048,3,2,256]{3,2,1,0:T(2,128)} custom-call(bf16[1536,2048]{1,0:T(8,128)(2,1)} %get-tuple-element.62.refs_0_), custom_call_target="tpu_custom_call" | custom-call | bytes 18874368 | tf_op jit(solution)/shard_map/spread/pallas_call | solution.py:353
  556.2 4.1 fusion.13
  560.3 2.5 convert.16
  563.5 5.0 fusion.8
  (53 shorter events, 4.8 us)
Async XLA Ops:
  7.2 81.7 %all-gather.5.cloned.1.call-start = ((), (), s32[]{:S(2)}) async-start(), calls=%async_computation.1 | async-start | bytes 5242880 | tf_op jit(solution)/shard_map/all_gather | solution.py:1037
  7.9 161.8 %all-gather.3.cloned.1.call-start = ((), (), s32[]{:S(2)}) async-start(), calls=%async_computation | async-start | bytes 5242880 | tf_op jit(solution)/shard_map/all_gather | solution.py:1038
  8.8 14.5 %copy-start.11 = (bf16[2,3,256]{2,0,1:T(2,128)(2,1)S(1)}, bf16[2,3,256]{2,0,1:T(2,128)(2,1)}, u32[]{:S(2)}) copy-start(bf16[2,3,256]{2,0,1:T(2,128)(2,1)} %param.24) | copy-start | bytes 9220
  8.8 15.2 %copy-start.7 = (s32[1024]{0:T(1024)S(1)}, s32[1024]{0:T(1024)}, u32[]{:S(2)}) copy-start(s32[1024]{0:T(1024)} %param.18) | copy-start | bytes 12292
  88.8 17.9 %copy-start.8 = (bf16[2048]{0:T(1024)(128)(2,1)S(1)}, bf16[2048]{0:T(1024)(128)(2,1)}, u32[]{:S(2)}) copy-start(bf16[2048]{0:T(1024)(128)(2,1)} %param.28) | copy-start | bytes 12292
  88.8 19.6 %copy-start.2 = (bf16[256,2048]{1,0:T(8,128)(2,1)S(1)}, bf16[256,2048]{1,0:T(8,128)(2,1)}, u32[]{:S(2)}) copy-start(bf16[256,2048]{1,0:T(8,128)(2,1)} %param.17) | copy-start | bytes 3145732
  88.8 20.4 %copy-start.9 = (bf16[2048]{0:T(1024)(128)(2,1)S(1)}, bf16[2048]{0:T(1024)(128)(2,1)}, u32[]{:S(2)}) copy-start(bf16[2048]{0:T(1024)(128)(2,1)} %param.26) | copy-start | bytes 12292
  88.9 20.4 %copy-start.10 = (bf16[2048]{0:T(1024)(128)(2,1)S(1)}, bf16[2048]{0:T(1024)(128)(2,1)}, u32[]{:S(2)}) copy-start(bf16[2048]{0:T(1024)(128)(2,1)} %param.30) | copy-start | bytes 12292
  102.7 6.5 %copy-start = (bf16[256,2048]{1,0:T(8,128)(2,1)S(1)}, bf16[256,2048]{1,0:T(8,128)(2,1)}, u32[]{:S(2)}) copy-start(bf16[256,2048]{1,0:T(8,128)(2,1)} %param.16) | copy-start | bytes 3145732
  102.8 32.0 %collective-permute-start = (bf16[1024,1024]{1,0:T(8,128)(2,1)}, bf16[1024,1024]{1,0:T(8,128)(2,1)}, u32[]{:S(2)}, u32[]{:S(2)}) collective-permute-start(bf16[1024,1024]{1,0:T(8,128)(2,1)} %get-tuple-element.48.refs_6_), channel_id=1, source_target_pairs={{0,4},{4,8},{8,12},{12,16},{16,20},{20,24},{24,28},{1,5},{5,9},{9,... | collective-permute-start | bytes 6291464 | tf_op jit(solution)/shard_map/ppermute | solution.py:21
  134.8 40.4 %collective-permute-start.1 = (bf16[1024,1024]{1,0:T(8,128)(2,1)}, bf16[1024,1024]{1,0:T(8,128)(2,1)}, u32[]{:S(2)}, u32[]{:S(2)}) collective-permute-start(bf16[1024,1024]{1,0:T(8,128)(2,1)} %collective-permute-done.refs_5_), channel_id=1, source_target_pairs={{0,4},{4,8},{8,12},{12,16},{16,20},{20,24},{24,28},{1,5},{5,9},{9,... | collective-permute-start | bytes 6291464 | tf_op jit(solution)/shard_map/ppermute | solution.py:21
  136.9 32.7 %copy-start.12 = (bf16[2,256,2048]{2,1,0:T(8,128)(2,1)S(1)}, bf16[2,256,2048]{2,1,0:T(8,128)(2,1)}, u32[]{:S(2)}) copy-start(bf16[2,256,2048]{2,1,0:T(8,128)(2,1)} %param.25) | copy-start | bytes 6291460
  525.9 42.6 %copy-start.6 = (f32[1,2048]{1,0:T(1,128)}, f32[1,2048]{1,0:T(1,128)S(1)}, u32[]{:S(2)}) copy-start(f32[1,2048]{1,0:T(1,128)S(1)} %get-tuple-element.72) | copy-start | bytes 24580
  545.8 10.4 %copy-start.1 = (bf16[256,2048]{1,0:T(8,128)(2,1)S(1)}, bf16[256,2048]{1,0:T(8,128)(2,1)}, u32[]{:S(2)}) copy-start(bf16[256,2048]{1,0:T(8,128)(2,1)} %param.16) | copy-start | bytes 3145732
  545.8 10.4 %copy-start.5 = (f32[256,2048]{1,0:T(8,128)S(1)}, f32[256,2048]{1,0:T(8,128)}, u32[]{:S(2)}) copy-start(f32[256,2048]{1,0:T(8,128)} %get-tuple-element.59) | copy-start | bytes 6291460
  556.2 4.1 copy-start.4
  560.3 3.2 copy-start.3
Sparse Core Ops, SparseCore 0:
  9.6 79.2 all-gather.4
  90.4 79.2 all-gather.2

commit v4 on v3

--- a/solution.py
+++ b/solution.py
@@ -13,17 +13,6 @@
 BF16 = jnp.bfloat16
 F32 = jnp.float32
 MESH = pl.DeviceIdType.MESH
-
-
-def shifted(x, axis, by):
-    length = lax.axis_size(axis)
-    pairs = [(i, i + by) for i in range(length) if 0 <= i + by < length]
-    return lax.ppermute(x, axis, pairs)
-
-
-def swapped(x, axis, bit):
-    length = lax.axis_size(axis)
-    return lax.ppermute(x, axis, [(i, i ^ (1 << bit)) for i in range(length)])
 
 
 def dot_rows(first, second):
@@ -74,108 +63,402 @@
     return values * cos_block + jnp.where(lane < half, up, down) * sin_block
 
 
-def project_kernel(
-    heads, head_dim, x_ref, g1_ref, b1_ref, g2_ref, b2_ref, w_ref, bias_ref, cos_ref, sin_ref,
-    n1_ref, n2_ref, q_ref, kv_ref, mean_ref, inverse_ref,
-):
-    x = x_ref[...].astype(F32)
-    average, inverse = moments(x)
-    mean_ref[...] = average
-    inverse_ref[...] = inverse
-    standard = (x - average) * inverse
-    n1 = (standard * g1_ref[...] + b1_ref[...]).astype(BF16)
-    n1_ref[...] = n1
-    n2_ref[...] = (standard * g2_ref[...] + b2_ref[...]).astype(BF16)
-    cos_block, sin_block = cos_ref[...], sin_ref[...]
-    width = heads * head_dim
-    lanes = cos_block.shape[1]
-    for part in range(3):
-        low = part * width
-        projected = dot(n1, w_ref[:, low : low + width]) + bias_ref[:, low : low + width]
-        if part == 2:
-            kv_ref[:, width:] = projected.astype(BF16)
-            continue
-        for head in range(heads):
-            at = head * head_dim
-            turned = turn(projected[:, at : at + lanes], cos_block, sin_block)
-            rest = projected[:, at + lanes : at + head_dim]
-            if part == 0:
-                scale = 1.0 / math.sqrt(head_dim)
-                q_ref[:, at : at + lanes] = (turned * scale).astype(BF16)
-                q_ref[:, at + lanes : at + head_dim] = (rest * scale).astype(BF16)
-            else:
-                kv_ref[:, at : at + lanes] = turned.astype(BF16)
-                kv_ref[:, at + lanes : at + head_dim] = rest.astype(BF16)
-
-
-def project(x, gain1, bias1, gain2, bias2, weight, bias, cos_table, sin_table, heads, head_dim):
-    rows, depth = x.shape
-    block = min(256, rows)
-    width = heads * head_dim
-    whole = lambda i: (0, 0)
-    by_row = lambda i: (i, 0)
+PIECES = 4
+
+
+def front_kernel(dims, *refs):
+    tensor, last, heads, head_dim = dims
+    refs = list(refs)
+    take = lambda count: [refs.pop(0) for _ in range(count)]
+    tokens_ref, grads_ref, w4_ref, up_ref, down_ref, out_ref = take(6)
+    g1_ref, b1_ref, g2_ref, b2_ref, qb_ref, ub_ref, cos_ref, sin_ref = take(8)
+    rows_out, grads_out, flat_out, n1_out, n2_out, q_out, kv_own, kv_near, kv_far = take(9)
+    act_out, slope_out, forward_out, agrad_out, mean_ref, inverse_ref = take(6)
+    both, wq, w_up, w_down, w_out, wstage = take(6)
+    n1s, n2s, qs, kvs, acts, slopes, forwards, agrads = take(8)
+    own_sem, w_sem, q_sem, send_sem, recv_sem, kv_sems, s_sem = take(7)
+    index, me = lax.axis_index("dp"), lax.axis_index("tensor")
+    own = tokens_ref.shape[0]
+    piece = own // PIECES
+    width, depth = heads * head_dim, tokens_ref.shape[1]
+    hidden_width = act_out.shape[1]
+    span = tensor * PIECES
+
+    barrier = pltpu.get_barrier_semaphore()
+
+    def greet(axis, to):
+        pl.semaphore_signal(barrier, inc=1, device_id={axis: to}, device_id_type=MESH)
+
+    sides = [
+        (me < tensor - 1, "tensor", me + 1),
+        (me > 0, "tensor", me - 1),
+        (index < last, "dp", index + 1),
+        (index > 0, "dp", index - 1),
+    ]
+    for there, axis, to in sides:
+        @pl.when(there)
+        def _():
+            greet(axis, to)
+
+    pl.semaphore_wait(barrier, sum(jnp.where(there, 1, 0) for there, _, _ in sides))
+
+    def rows_of(shard):
+        return pl.ds(pl.multiple_of(shard * own, own), own)
+
+    own_copies = [
+        pltpu.make_async_copy(source, both.at[a, rows_of(me)], own_sem.at[a])
+        for a, source in enumerate((tokens_ref, grads_ref))
+    ]
+    weight_copies = [
+        pltpu.make_async_copy(up_ref, w_up, w_sem.at[0]),
+        pltpu.make_async_copy(down_ref, w_down, w_sem.at[1]),
+        pltpu.make_async_copy(out_ref, w_out, w_sem.at[2]),
+    ]
+    wrows = wstage.shape[1]
+
+    def wq_copy(b):
+        return pltpu.make_async_copy(
+            w4_ref.at[pl.ds(pl.multiple_of(b * wrows, wrows), wrows)],
+            wstage.at[lax.rem(b, 2)], q_sem.at[lax.rem(b, 2)],
+        )
+
+    flat_copy = pltpu.make_async_copy(wq, flat_out, w_sem.at[3])
+    for copy in own_copies:
+        copy.start()
+    wq_copy(0).start()
+    wq_copy(1).start()
+    for copy in weight_copies:
+        copy.start()
+    for copy in own_copies:
+        copy.wait()
+
+    def hop(t, shard, p, direction):
+        rows = pl.ds(pl.multiple_of(shard * own + p * piece, piece), piece)
+        here = both.at[t // span, rows]
+        to = me + 1 if direction == 0 else me - 1
+        return pltpu.make_async_remote_copy(
+            src_ref=here,
+            dst_ref=here,
+            send_sem=send_sem.at[direction, t],
+            recv_sem=recv_sem.at[direction, t],
+            device_id={"tensor": jnp.clip(to, 0, tensor - 1)},
+            device_id_type=MESH,
+        )
+
+    def passing(t):
+        k, p = lax.rem(t // PIECES, tensor), lax.rem(t, PIECES)
+        return k, p, ((me - k, me - k >= 0, me < tensor - 1), (me + k, me + k < tensor, me > 0))
+
+    def relay(t):
+        k, p, ways = passing(t)
+        for direction, (shard, held, onward) in enumerate(ways):
+            @pl.when(held & (k > 0))
+            def _():
+                hop(t - PIECES, shard, p, direction).wait_recv()
+
+            @pl.when(held & onward)
+            def _():
+                hop(t, shard, p, direction).start()
+
+    def drain(t, carry):
+        k, p, ways = passing(t)
+        for direction, (shard, held, onward) in enumerate(ways):
+            @pl.when(held & onward)
+            def _():
+                hop(t, shard, p, direction).wait_send()
+
+        return carry
+
+    tables = []
+    for m in range(tensor):
+        near = sorted(range(tensor), key=lambda shard: (abs(shard - m), shard))
+        tables.append(near)
+
+    def shard_at(j):
+        found = 0
+        for m in range(tensor):
+            for place in range(tensor):
+                hit = (me == m) & (j == place)
+                found = found + jnp.where(hit, tables[m][place], 0)
+        return found
+
+    def outs_project(shard):
+        rows = rows_of(shard)
+        return [
+            pltpu.make_async_copy(both.at[0, rows], rows_out.at[rows], s_sem.at[0]),
+            pltpu.make_async_copy(n1s, n1_out.at[rows], s_sem.at[1]),
+            pltpu.make_async_copy(n2s, n2_out.at[rows], s_sem.at[2]),
+            pltpu.make_async_copy(qs, q_out.at[rows], s_sem.at[3]),
+            pltpu.make_async_copy(kvs, kv_own.at[rows], s_sem.at[4]),
+        ]
+
+    def outs_up(shard):
+        rows = rows_of(shard)
+        return [
+            pltpu.make_async_copy(acts, act_out.at[rows], s_sem.at[5]),
+            pltpu.make_async_copy(slopes, slope_out.at[rows], s_sem.at[6]),
+        ]
+
+    def out_forward(shard):
+        return pltpu.make_async_copy(forwards, forward_out.at[rows_of(shard)], s_sem.at[7])
+
+    def outs_agrad(shard):
+        rows = rows_of(shard)
+        return [
+            pltpu.make_async_copy(both.at[1, rows], grads_out.at[rows], s_sem.at[8]),
+            pltpu.make_async_copy(agrads, agrad_out.at[rows], s_sem.at[9]),
+        ]
+
+    def near_copy(j):
+        rows = rows_of(shard_at(j))
+        return pltpu.make_async_remote_copy(
+            src_ref=kvs,
+            dst_ref=kv_near.at[rows],
+            send_sem=kv_sems.at[0, j],
+            recv_sem=kv_sems.at[1, j],
+            device_id={"dp": jnp.minimum(index + 1, last)},
+            device_id_type=MESH,
+        )
+
+    def far_copy(j):
+        rows = rows_of(shard_at(j))
+        return pltpu.make_async_remote_copy(
+            src_ref=kv_near.at[rows],
+            dst_ref=kv_far.at[rows],
+            send_sem=kv_sems.at[2, j],
+            recv_sem=kv_sems.at[3, j],
+            device_id={"dp": jnp.minimum(index + 1, last)},
+            device_id_type=MESH,
+        )
+
+    def project_shard(j):
+        shard = shard_at(j)
+        rows = rows_of(shard)
+
+        @pl.when(j > 0)
+        def _():
+            for copy in outs_project(shard_at(j - 1)):
+                copy.wait()
+
+            @pl.when(index < last)
+            def _():
+                near_copy(j - 1).wait_send()
+
+        x = both[0, rows].astype(F32)
+        average, inverse = moments(x)
+        mean_ref[rows, :] = average
+        inverse_ref[rows, :] = inverse
+        standard = (x - average) * inverse
+        n1s[...] = (standard * g1_ref[...] + b1_ref[...]).astype(BF16)
+        n2s[...] = (standard * g2_ref[...] + b2_ref[...]).astype(BF16)
+        cos_block, sin_block = cos_ref[rows, :], sin_ref[rows, :]
+        lanes = cos_block.shape[1]
+        scale = 1.0 / math.sqrt(head_dim)
+        for part in range(3):
+            low = part * width
+            projected = dot(n1s[...], wq[:, low : low + width]) + qb_ref[:, low : low + width]
+            if part == 2:
+                kvs[:, width:] = projected.astype(BF16)
+                continue
+            for head in range(heads):
+                at = head * head_dim
+                turned = turn(projected[:, at : at + lanes], cos_block, sin_block)
+                other = projected[:, at + lanes : at + head_dim]
+                if part == 0:
+                    qs[:, at : at + lanes] = (turned * scale).astype(BF16)
+                    qs[:, at + lanes : at + head_dim] = (other * scale).astype(BF16)
+                else:
+                    kvs[:, at : at + lanes] = turned.astype(BF16)
+                    kvs[:, at + lanes : at + head_dim] = other.astype(BF16)
+        for copy in outs_project(shard):
+            copy.start()
+
+        @pl.when(index < last)
+        def _():
+            near_copy(j).start()
+
+    def up_half(j, half):
+        if half == 0:
+            @pl.when(j > 0)
+            def _():
+                for copy in outs_up(shard_at(j - 1)):
+                    copy.wait()
+
+        size = hidden_width // 2
+        step = min(512, size)
+        for column in range(half * size, (half + 1) * size, step):
+            part = slice(column, column + step)
+            hidden = dot(n2s[...], w_up[:, part]) + ub_ref[:, part]
+            phi = (1.0 + lax.erf(hidden * F32(math.sqrt(0.5)))) * 0.5
+            acts[:, part] = (hidden * phi).astype(BF16)
+            density = jnp.exp(hidden * hidden * -0.5) * F32(1.0 / math.sqrt(2.0 * math.pi))
+            slopes[:, part] = phi + hidden * density
+        if half == 1:
+            for copy in outs_up(shard_at(j)):
+                copy.start()
+
+    def forward_shard(j):
+        @pl.when(j > 0)
+        def _():
+            out_forward(shard_at(j - 1)).wait()
+
+        step = min(512, depth)
+        for column in range(0, depth, step):
+            part = slice(column, column + step)
+            forwards[:, part] = dot(acts[...], w_down[:, part])
+        out_forward(shard_at(j)).start()
+
+    def pass_kv(j):
+        @pl.when(index > 0)
+        def _():
+            near_copy(j).wait_recv()
+
+            @pl.when(index < last)
+            def _():
+                far_copy(j).start()
+
+    def agrad_shard(j):
+        @pl.when(j > 0)
+        def _():
+            for copy in outs_agrad(shard_at(j - 1)):
+                copy.wait()
+
+        shard = shard_at(j)
+        agrads[...] = dot_cols(both[1, rows_of(shard)], w_out[...]).astype(BF16)
+        for copy in outs_agrad(shard):
+            copy.start()
+
+    def on(condition, act):
+        @pl.when(condition)
+        def _():
+            act()
+
+    def slot(t, carry):
+        on(t < 2 * span, lambda: relay(t))
+
+        @pl.when(t == 2)
+        def _():
+            for b in range(depth // wrows):
+                wq_copy(b).wait()
+                for part in range(3):
+                    wq[b * wrows : (b + 1) * wrows, part * width : (part + 1) * width] = wstage[
+                        b % 2, :, part
+                    ].reshape(wrows, width)
+                if b + 2 < depth // wrows:
+                    wq_copy(b + 2).start()
+            flat_copy.start()
+
+        j, sub = t // PIECES - 1, lax.rem(t, PIECES)
+        working = (j >= 0) & (j < tensor)
+        on(working & (sub == 0), lambda: project_shard(j))
+
+        @pl.when(t == PIECES + 1)
+        def _():
+            weight_copies[0].wait()
+
+        on(working & (sub == 1), lambda: up_half(j, 0))
+        on(working & (sub == 2), lambda: up_half(j, 1))
+
+        @pl.when(t == PIECES + 3)
+        def _():
+            weight_copies[1].wait()
+
+        on(working & (sub == 3), lambda: forward_shard(j))
+        before = j - 1
+        on((before >= 0) & (before < tensor) & (sub == 1), lambda: pass_kv(before))
+
+        @pl.when(t == span + PIECES)
+        def _():
+            weight_copies[2].wait()
+
+        late = j - tensor
+        on((late >= 0) & (late < tensor) & (sub == 0), lambda: agrad_shard(late))
+        return carry
+
+    lax.fori_loop(0, 2 * span + 1, slot, 0)
+    final = shard_at(tensor - 1)
+    for copy in outs_project(final) + outs_up(final) + [out_forward(final)] + outs_agrad(final):
+        copy.wait()
+    flat_copy.wait()
+
+    @pl.when(index < last)
+    def _():
+        near_copy(tensor - 1).wait_send()
+
+    def kv_drain(j, carry):
+        @pl.when((index > 0) & (index < last))
+        def _():
+            far_copy(j).wait_send()
+
+        @pl.when(index > 1)
+        def _():
+            far_copy(j).wait_recv()
+
+        return carry
+
+    lax.fori_loop(0, tensor, kv_drain, 0)
+    lax.fori_loop(0, 2 * span, drain, 0)
+
+
+def front(tokens, grads, w4, fc1_weight, fc2_weight, flat_out, small, tables, sizes):
+    tensor, last, heads, head_dim = sizes
+    own, depth = tokens.shape
+    rows, width, hidden_width = own * tensor, heads * head_dim, fc1_weight.shape[1]
+    span, wrows = tensor * PIECES, 256
+    hbm = pl.BlockSpec(memory_space=pl.ANY)
+    vmem = pl.BlockSpec(memory_space=pltpu.VMEM)
+    shape = jax.ShapeDtypeStruct
     return pl.pallas_call(
-        lambda *refs: project_kernel(heads, head_dim, *refs),
-        name="project",
-        grid=(rows // block,),
-        in_specs=[
-            pl.BlockSpec((block, depth), by_row),
-            *[pl.BlockSpec((1, depth), whole)] * 4,
-            pl.BlockSpec((depth, 3 * width), whole, pipeline_mode=pl.Buffered(1)),
-            pl.BlockSpec((1, 3 * width), whole),
-            pl.BlockSpec((block, cos_table.shape[1]), by_row),
-            pl.BlockSpec((block, cos_table.shape[1]), by_row),
+        lambda *refs: front_kernel(sizes, *refs),
+        name="front",
+        in_specs=[hbm] * 6 + [vmem] * 8,
+        out_specs=[hbm] * 13 + [vmem] * 2,
+        out_shape=[
+            shape((rows, depth), BF16),
+            shape((rows, depth), BF16),
+            shape((depth, 3 * width), BF16),
+            shape((rows, depth), BF16),
+            shape((rows, depth), BF16),
+            shape((rows, width), BF16),
+            *[shape((rows, 2 * width), BF16)] * 3,
+            shape((rows, hidden_width), BF16),
+            shape((rows, hidden_width), F32),
+            shape((rows, depth), F32),
+            shape((rows, width), BF16),
+            shape((rows, 1), F32),
+            shape((rows, 1), F32),
         ],
-        out_specs=[
-            pl.BlockSpec((block, depth), by_row),
-            pl.BlockSpec((block, depth), by_row),
-            pl.BlockSpec((block, width), by_row),
-            pl.BlockSpec((block, 2 * width), by_row),
-            pl.BlockSpec((block, 1), by_row),
-            pl.BlockSpec((block, 1), by_row),
+        scratch_shapes=[
+            pltpu.VMEM((2, rows, depth), BF16),
+            pltpu.VMEM((depth, 3 * width), BF16),
+            pltpu.VMEM((depth, hidden_width), BF16),
+            pltpu.VMEM((hidden_width, depth), BF16),
+            pltpu.VMEM((width, depth), BF16),
+            pltpu.VMEM((2, wrows, 3, heads, head_dim), BF16),
+            pltpu.VMEM((own, depth), BF16),
+            pltpu.VMEM((own, depth), BF16),
+            pltpu.VMEM((own, width), BF16),
+            pltpu.VMEM((own, 2 * width), BF16),
+            pltpu.VMEM((own, hidden_width), BF16),
+            pltpu.VMEM((own, hidden_width), F32),
+            pltpu.VMEM((own, depth), F32),
+            pltpu.VMEM((own, width), BF16),
+            pltpu.SemaphoreType.DMA((2,)),
+            pltpu.SemaphoreType.DMA((4,)),
+            pltpu.SemaphoreType.DMA((2,)),
+            pltpu.SemaphoreType.DMA((2, 2 * span)),
+            pltpu.SemaphoreType.DMA((2, 2 * span)),
+            pltpu.SemaphoreType.DMA((4, tensor)),
+            pltpu.SemaphoreType.DMA((10,)),
         ],
-        out_shape=[
-            jax.ShapeDtypeStruct((rows, depth), BF16),
-            jax.ShapeDtypeStruct((rows, depth), BF16),
-            jax.ShapeDtypeStruct((rows, width), BF16),
-            jax.ShapeDtypeStruct((rows, 2 * width), BF16),
-            jax.ShapeDtypeStruct((rows, 1), F32),
-            jax.ShapeDtypeStruct((rows, 1), F32),
-        ],
-        compiler_params=params("arbitrary"),
-        cost_estimate=cost(2 * rows * depth * 3 * width, 2 * (3 * rows * depth + 3 * depth * width)),
-    )(x, gain1, bias1, gain2, bias2, weight, bias, cos_table, sin_table)
-
-
-def up_kernel(x_ref, w_ref, b_ref, act_ref, slope_ref):
-    hidden = dot(x_ref[...], w_ref[...]) + b_ref[...]
-    phi = (1.0 + lax.erf(hidden * F32(math.sqrt(0.5)))) * 0.5
-    act_ref[...] = (hidden * phi).astype(BF16)
-    density = jnp.exp(hidden * hidden * -0.5) * F32(1.0 / math.sqrt(2.0 * math.pi))
-    slope_ref[...] = phi + hidden * density
-
-
-def up(x, weight, bias):
-    rows, depth = x.shape
-    width = weight.shape[1]
-    bm, bn = min(256, rows), min(512, width)
-    return pl.pallas_call(
-        up_kernel,
-        name="up",
-        grid=(width // bn, rows // bm),
-        in_specs=[
-            pl.BlockSpec((bm, depth), lambda j, i: (i, 0)),
-            pl.BlockSpec((depth, bn), lambda j, i: (0, j)),
-            pl.BlockSpec((1, bn), lambda j, i: (0, j)),
-        ],
-        out_specs=[pl.BlockSpec((bm, bn), lambda j, i: (i, j))] * 2,
-        out_shape=[
-            jax.ShapeDtypeStruct((rows, width), BF16),
-            jax.ShapeDtypeStruct((rows, width), F32),
-        ],
-        compiler_params=params("arbitrary", "arbitrary"),
-        cost_estimate=cost(2 * rows * depth * width, 2 * depth * width + 6 * rows * width),
-    )(x, weight, bias)
+        compiler_params=pltpu.CompilerParams(
+            collective_id=1, has_side_effects=True, vmem_limit_bytes=62 << 20
+        ),
+        cost_estimate=cost(
+            2 * rows * depth * (3 * width + 2 * hidden_width + width),
+            2 * rows * (6 * depth + 4 * hidden_width),
+        ),
+    )(tokens, grads, w4, fc1_weight, fc2_weight, flat_out, *small, *tables)
 
 
 def attention_kernel(heads, head_dim, parts, bk, first_ref, q_ref, do_ref, start_ref, *refs):
@@ -1031,40 +1314,34 @@
     model_width, heads, _, head_dim = qkv_weight.shape
     width = heads * head_dim
     hidden_width = fc1_weight.shape[1]
-    own_count = tokens.shape[0]
-    tie = lax.optimization_barrier
     row = lambda v: v.reshape(1, -1).astype(F32)
-    rows_all = lax.all_gather(tokens, "tensor", axis=0, tiled=True)
-    grads_all = lax.all_gather(out_grad, "tensor", axis=0, tiled=True)
-    row_count = rows_all.shape[0]
-    flat_qkv = jnp.transpose(qkv_weight, (0, 2, 1, 3)).reshape(model_width, 3 * width)
+    w4 = jnp.transpose(qkv_weight, (0, 2, 1, 3))
     flat_bias = jnp.transpose(qkv_bias, (1, 0, 2)).reshape(1, 3 * width).astype(F32)
     flat_out = out_weight.reshape(width, model_width)
-    cos_table, sin_table = rope_tables(positions, 128)
-    normed_one, normed_two, queries, kv_own, mean, inverse = project(
-        rows_all, row(norm1_gain), row(norm1_bias), row(norm2_gain), row(norm2_bias),
-        flat_qkv, flat_bias, cos_table, sin_table, heads, head_dim,
+    tables = rope_tables(positions, 128)
+    small = [
+        row(norm1_gain), row(norm1_bias), row(norm2_gain), row(norm2_bias), flat_bias, row(fc1_bias)
+    ]
+    tensor, last = lax.axis_size("tensor"), lax.axis_size("dp") - 1
+    (
+        rows_all, grads_all, flat_qkv, normed_one, normed_two, queries, kv_own, kv_near, kv_far,
+        activated, slope, forward, attended_grad, mean, inverse,
+    ) = front(
+        tokens, out_grad, w4, fc1_weight, fc2_weight, flat_out, small, tables,
+        (tensor, last, heads, head_dim),
     )
-    reach = (MOST - 2) // row_count + 1
-    kv_parts = [kv_own]
-    for _ in range(reach):
-        kv_parts.insert(0, shifted(kv_parts[0], "dp", 1))
-    activated, slope = up(normed_two, fc1_weight, row(fc1_bias))
-    forward = dot(activated, fc2_weight)
-    grads_all, activated, slope, forward = tie((grads_all, activated, slope, forward))
-
-    attended_grad = dot_cols(grads_all, flat_out).astype(BF16)
+    assert MOST - 2 < 2 * rows_all.shape[0]
     attended, query_grad, *kv_grads = attention(
-        queries, kv_parts, attended_grad, positions, heads, head_dim
+        queries, [kv_far, kv_near, kv_own], attended_grad, positions, heads, head_dim
     )
     own_grad = out_grad.astype(F32)
     vectors = jnp.pad(jnp.sum(own_grad, 0, keepdims=True), ((4, 3), (0, 0)))
-    bits = (lax.axis_size("dp") - 1).bit_length()
+    bits = last.bit_length()
     *stacked, d_sum, d_got, branch, b_got, vectors = reduce_grads(
         (activated, attended, normed_two, grads_all, normed_one, slope, forward), kv_grads, query_grad,
-        vectors, (cos_table, sin_table), (mean, inverse), (row(norm1_gain), row(norm2_gain)),
+        vectors, tables, (mean, inverse), (row(norm1_gain), row(norm2_gain)),
         (fc1_weight, fc2_weight, flat_qkv, flat_out), rows_all,
-        (bits, lax.axis_size("tensor"), heads, head_dim),
+        (bits, tensor, heads, head_dim),
     )
     for k in range(d_got.shape[0]):
         d_sum = d_sum + d_got[k].astype(F32)

time: 579 us -> 546 us (0.943)
  Pallas kernels: 416 us -> 527 us
  waiting for transfers between devices: 81.1 us -> 0 us
  matrix products: 20.1 us -> 0 us
  local copies, waits for them, and re-layouts: 21.1 us -> 6.23 us
  between operations: 14.2 us -> 0.8 us
  starting transfers between devices: 6.2 us -> 0 us
    pallas_call x2 -> x1, Pallas kernels: 38.2 us -> 147 us  [front(): pl.pallas_call(lambda *refs: front_kernel(sizes, *refs), name='front', in...]
    all_gather x2 -> x0, waiting for transfers between devices: 79.7 us -> none  [the longest x1 61.6 us: body(): rows_all = lax.all_gather(tokens, 'tensor', axis=0, tiled=True)]
    dot_general x2 -> x0, matrix products: 20.1 us -> none  [the longest x1 14.6 us: dot(): return jnp.dot(first, second, preferred_element_type=F32)]
    reshape x1 -> x0, local copies, waits for them, and re-layouts: 14.5 us -> none  [body(): jnp.transpose(qkv_weight, (0, 2, 1, 3)).reshape(model_width, 3 * width)]
    ppermute x2 -> x0, starting transfers between devices: 6.12 us -> none  [shifted(): return lax.ppermute(x, axis, pairs)]
  transfers between devices with their start and end apart: 4 -> 0, of which waited for: 2 -> 0; matrix products, arithmetic and copies ran while one was open for 7% -> 0% of each run, Pallas kernels for 7% -> 0%
where the time goes in v4:
time: 546 us; the launch traced here: 549 us
  Pallas kernels  527 us (97%)
  other arithmetic  14.1 us (3%)
  local copies, waits for them, and re-layouts  6.23 us (1%)
    pallas_call x1, Pallas kernels, reduce_grads(): pl.pallas_call(lambda *refs: reduce_kernel(plan, dims, *refs), name='redu...  297 us
    pallas_call x1, Pallas kernels, front(): pl.pallas_call(lambda *refs: front_kernel(sizes, *refs), name='front', in...  147 us
    pallas_call x1, Pallas kernels, attention(): pl.pallas_call(lambda *refs: attention_kernel(heads, head_dim, parts, bk,...  54.6 us
    pallas_call x2, Pallas kernels, widened(): pl.pallas_call(widen_kernel, name='widened', grid=(rows // block,), in_sp...  19.1 us

profile of v4, /device:TPU:11, one launch (start us, length us, event | category | flops | bytes accessed | tf_op | source)
XLA Modules:
  0.0 548.6 jit_solution(17095619408088416721)
XLA Ops:
  0.6 0.8 subtract_add_fusion
  1.4 1.9 fusion.12
  3.5 1.4 maximum_maximum_fusion
  4.9 0.6 reshape.117.refs_10_
  5.5 0.6 convert_element_type.97
  6.1 146.7 %front.1 = (bf16[1024,2048]{1,0:T(8,128)(2,1)}, bf16[1024,2048]{1,0:T(8,128)(2,1)}, bf16[2048,1536]{1,0:T(8,128)(2,1)}, bf16[1024,2048]{1,0:T(8,128)(2,1)}, bf16...) custom-call(bf16[256,2048]{1,0:T(8,128)(2,1)} %refs_0_.1, ...), custom_call_target="tpu_custom_call" | custom-call | flops 25769803776 | bytes 41943040 | tf_op jit(solution)/shard_map/front/pallas_call | solution.py:411
  152.8 1.1 copy.31.refs_3_
  154.0 0.5 and_select_fusion.refs_0_
  154.5 54.6 %attention.1 = (bf16[1024,512]{1,0:T(8,128)(2,1)}, f32[1024,512]{1,0:T(8,128)}, bf16[1024,1024]{1,0:T(8,128)(2,1)}, f32[1024,1024]{1,0:T(8,128)}, f32[1024,1024]{1,0:T(8,128)}) custom-call(s32[4]{0:T(128)} %and_select_fusion.refs_0_, bf16[1024,512]{1,0:T(8,128)(2,1)} %get-tuple-element.49.refs_1_, bf16[1024,512]{1,0:T(8,128)(2,1)} %get-tuple-element.50.refs_2_, ...), custom_call_target="tpu_custom_call" | custom-call | flops 12582912000 | bytes 12582912 | tf_op jit(solution)/shard_map/attention/pallas_call | solution.py:572
  209.3 0.6 pad.4.refs_16_
  209.9 296.7 %reduce_grads.1 = (bf16[2048,2048]{1,0:T(8,128)(2,1)}, bf16[512,2048]{1,0:T(8,128)(2,1)}, bf16[2048,2048]{1,0:T(8,128)(2,1)}, bf16[1536,2048]{1,0:T(8,128)(2,1)}...) custom-call(bf16[1024,2048]{1,0:T(8,128)(2,1)} %get-tuple-element.43, ...), custom_call_target="tpu_custom_call" | custom-call | flops 49392123904 | bytes 100663296 | tf_op jit(solution)/shard_map/reduce_grads/pallas_call | solution.py:1241
  506.6 9.5 %widened.2 = f32[2048,2048]{1,0:T(8,128)} custom-call(bf16[2048,2048]{1,0:T(8,128)(2,1)} %get-tuple-element.70.in_ref), custom_call_target="tpu_custom_call" | custom-call | bytes 25165824 | tf_op jit(solution)/shard_map/widened/pallas_call | solution.py:615
  516.2 9.5 %widened.3 = f32[2048,2048]{1,0:T(8,128)} custom-call(bf16[2048,2048]{1,0:T(8,128)(2,1)} %get-tuple-element.71.in_ref), custom_call_target="tpu_custom_call" | custom-call | bytes 25165824 | tf_op jit(solution)/shard_map/widened/pallas_call | solution.py:615
  525.7 10.3 %spread.1 = f32[2048,3,2,256]{3,2,1,0:T(2,128)} custom-call(bf16[1536,2048]{1,0:T(8,128)(2,1)} %get-tuple-element.68.refs_0_), custom_call_target="tpu_custom_call" | custom-call | bytes 18874368 | tf_op jit(solution)/shard_map/spread/pallas_call | solution.py:636
  536.0 0.2 convert_reduce_fusion
  536.3 0.4 fusion.7
  536.7 0.9 copy-done.6
  537.6 2.9 fusion.13
  540.8 0.7 copy-done.5
  541.5 2.7 fusion.8
  544.1 2.5 convert.16
  546.7 0.6 fusion.14
  547.4 0.6 reshape_squeeze.3
  548.0 0.6 copy.33
  (39 shorter events, 0.7 us)
Async XLA Ops:
  1.4 3.5 copy-start.12
  1.4 4.1 copy-start.9
  154.5 54.6 %copy-start.1 = (bf16[256,2048]{1,0:T(8,128)(2,1)S(1)}, bf16[256,2048]{1,0:T(8,128)(2,1)}, u32[]{:S(2)}) copy-start(bf16[256,2048]{1,0:T(8,128)(2,1)} %refs_1_.1) | copy-start | bytes 3145732
  525.7 10.3 %copy-start = (bf16[256,2048]{1,0:T(8,128)(2,1)S(1)}, bf16[256,2048]{1,0:T(8,128)(2,1)}, u32[]{:S(2)}) copy-start(bf16[256,2048]{1,0:T(8,128)(2,1)} %refs_0_.1) | copy-start | bytes 3145732
  536.0 1.6 copy-start.6
  537.6 2.9 copy-start.10
  537.6 3.0 copy-start.11
  537.6 3.0 copy-start.2
  537.6 3.2 copy-start.3
  537.6 3.8 copy-start.5
  541.5 2.7 copy-start.4
  544.1 2.5 copy-start.7
  547.3 1.2 copy-start.8

commit v5 on v4

--- a/solution.py
+++ b/solution.py
@@ -1,3 +1,4 @@
+import functools
 import math
 
 import jax
@@ -496,61 +497,70 @@
         for copy in copies:
             copy.wait()
 
+    def rows_of(j):
+        return pl.ds(pl.multiple_of(j * bk, bk), bk)
+
+    at = [head * head_dim for head in range(heads)]
+    head_of = lambda ref, head: ref[:, at[head] : at[head] + head_dim]
+    folded = lambda x, fold: functools.reduce(
+        fold, [x[:, c * 128 : (c + 1) * 128] for c in range(chunks)]
+    )
+
+    def scores(j, best):
+        rows = rows_of(j)
+        column = j * bk + lane
+        allowed = (column >= start) & (column <= row)
+        out = []
+        for head in range(heads):
+            key = kv_ref[rows, at[head] : at[head] + head_dim]
+            s = jnp.where(allowed, dot_cols(head_of(q_ref, head), key), -1e30)
+            s_ref[head, j] = s
+            out.append(jnp.maximum(best[head], folded(s, jnp.maximum)))
+        for head in range(heads):
+            value = kv_ref[rows, width + at[head] : width + at[head] + head_dim]
+            dp_ref[head, j] = dot_cols(head_of(do_ref, head), value)
+        return tuple(out)
+
+    low_best = jnp.full((bq, 128), -1e30, F32)
+    best = lax.fori_loop(low, high, scores, (low_best,) * heads)
+    best = [jnp.max(b, 1, keepdims=True) for b in best]
+
+    def weigh(j, carry):
+        out = []
+        for head in range(heads):
+            total, mixed = carry[head]
+            e = jnp.exp(s_ref[head, j] - best[head])
+            s_ref[head, j] = e
+            out.append(
+                (total + folded(e, jnp.add), mixed + folded(e * dp_ref[head, j], jnp.add))
+            )
+        return tuple(out)
+
+    zero = jnp.zeros((bq, 128), F32)
+    sums = lax.fori_loop(low, high, weigh, ((zero, zero),) * heads)
+    scale = [1.0 / jnp.sum(total, 1, keepdims=True) for total, _ in sums]
+    delta = [jnp.sum(mixed, 1, keepdims=True) * k for (_, mixed), k in zip(sums, scale)]
+    o_ref[...] = jnp.zeros_like(o_ref)
+
+    def spread_back(j, carry):
+        rows = rows_of(j)
+        for head in range(heads):
+            p = s_ref[head, j] * scale[head]
+            p_low = p.astype(BF16)
+            ds = (p * (dp_ref[head, j] - delta[head])).astype(BF16)
+            keys = slice(at[head], at[head] + head_dim)
+            values = slice(width + at[head], width + at[head] + head_dim)
+            o_ref[head, :, :head_dim] += dot(p_low, kv_ref[rows, values])
+            o_ref[head, :, head_dim:] += dot(ds, kv_ref[rows, keys])
+            dkv_ref[rows, keys] += dot_rows(ds, head_of(q_ref, head))
+            dkv_ref[rows, values] += dot_rows(p_low, head_of(do_ref, head))
+        return carry
+
+    lax.fori_loop(low, high, spread_back, 0)
     for head in range(heads):
-        at = head * head_dim
-        q = q_ref[:, at : at + head_dim]
-        do = do_ref[:, at : at + head_dim]
-
-        def rows_of(j):
-            return pl.ds(pl.multiple_of(j * bk, bk), bk)
-
-        def scores(j, best):
-            s = dot_cols(q, kv_ref[rows_of(j), at : at + head_dim])
-            column = j * bk + lane
-            s = jnp.where((column >= start) & (column <= row), s, -1e30)
-            s_ref[j] = s
-            for c in range(chunks):
-                best = jnp.maximum(best, s[:, c * 128 : (c + 1) * 128])
-            return best
-
-        best = lax.fori_loop(low, high, scores, jnp.full((bq, 128), -1e30, F32))
-        best = jnp.max(best, 1, keepdims=True)
-
-        def weigh(j, carry):
-            total, mixed = carry
-            e = jnp.exp(s_ref[j] - best)
-            dp = dot_cols(do, kv_ref[rows_of(j), width + at : width + at + head_dim])
-            s_ref[j] = e
-            dp_ref[j] = dp
-            both = e * dp
-            for c in range(chunks):
-                total = total + e[:, c * 128 : (c + 1) * 128]
-                mixed = mixed + both[:, c * 128 : (c + 1) * 128]
-            return total, mixed
-
-        zero = jnp.zeros((bq, 128), F32)
-        total, mixed = lax.fori_loop(low, high, weigh, (zero, zero))
-        total = jnp.sum(total, 1, keepdims=True)
-        scale = 1.0 / total
-        delta = jnp.sum(mixed, 1, keepdims=True) * scale
-        o_ref[...] = jnp.zeros_like(o_ref)
-
-        def spread(j, carry):
-            rows = rows_of(j)
-            p = s_ref[j] * scale
-            p_low = p.astype(BF16)
-            ds = (p * (dp_ref[j] - delta)).astype(BF16)
-            k = kv_ref[rows, at : at + head_dim]
-            v = kv_ref[rows, width + at : width + at + head_dim]
-            o_ref[:, :head_dim] += dot(p_low, v)
-            o_ref[:, head_dim:] += dot(ds, k)
-            dkv_ref[rows, at : at + head_dim] += dot_rows(ds, q)
-            dkv_ref[rows, width + at : width + at + head_dim] += dot_rows(p_low, do)
-            return carry
-
-        lax.fori_loop(low, high, spread, 0)
-        att_ref[:, at : at + head_dim] = o_ref[:, :head_dim].astype(BF16)
-        dq_ref[:, at : at + head_dim] = o_ref[:, head_dim:] * (1.0 / math.sqrt(head_dim))
+        keys = slice(at[head], at[head] + head_dim)
+        att_ref[:, keys] = o_ref[head, :, :head_dim].astype(BF16)
+        dq_ref[:, keys] = o_ref[head, :, head_dim:] * (1.0 / math.sqrt(head_dim))
 
     @pl.when(block == pl.num_programs(0) - 1)
     def _():
@@ -589,9 +599,9 @@
             scratch_shapes=[
                 pltpu.VMEM((total, 2 * width), BF16),
                 pltpu.VMEM((total, 2 * width), F32),
-                pltpu.VMEM((total // bk, bq, bk), F32),
-                pltpu.VMEM((total // bk, bq, bk), F32),
-                pltpu.VMEM((bq, 2 * head_dim), F32),
+                pltpu.VMEM((heads, total // bk, bq, bk), F32),
+                pltpu.VMEM((heads, total // bk, bq, bk), F32),
+                pltpu.VMEM((heads, bq, 2 * head_dim), F32),
                 pltpu.SemaphoreType.DMA((parts,)),
             ],
         ),
@@ -605,44 +615,45 @@
     )(first, q, do, start[:, None], *kv_parts)
 
 
-def widen_kernel(in_ref, out_ref):
-    out_ref[...] = in_ref[...].astype(F32)
-
-
-def widened(x):
-    rows, depth = x.shape
-    block = min(512, rows)
+def finish_kernel(heads, head_dim, natural, *refs):
+    fc2_ref, out_ref, fc1_ref, qkv_ref, fc2_to, out_to, fc1_to, qkv_to = refs
+    fc2_to[...] = fc2_ref[...].astype(F32)
+    out_to[...] = out_ref[...].astype(F32)
+    fc1_to[...] = (fc1_ref[...] if natural else fc1_ref[...].T).astype(F32)
+    for part in range(3):
+        for head in range(heads):
+            at = (part * heads + head) * head_dim
+            qkv_to[:, part, head, :] = qkv_ref[at : at + head_dim, :].T.astype(F32)
+
+
+def finish(fc2, out, fc1, qkv, heads, head_dim, natural):
+    depth = fc2.shape[1]
+    steps = 8
+    by_row = lambda i: (i, 0)
+    by_column = lambda i: (0, i)
+    rows_of = lambda x: pl.BlockSpec((x.shape[0] // steps, x.shape[1]), by_row)
+    columns_of = lambda x: pl.BlockSpec((x.shape[0], depth // steps), by_column)
+    shape = lambda *dims: jax.ShapeDtypeStruct(dims, F32)
+    fc1_shape = fc1.shape if natural else fc1.shape[::-1]
     return pl.pallas_call(
-        widen_kernel,
-        name="widened",
-        grid=(rows // block,),
-        in_specs=[pl.BlockSpec((block, depth), lambda i: (i, 0))],
-        out_specs=pl.BlockSpec((block, depth), lambda i: (i, 0)),
-        out_shape=jax.ShapeDtypeStruct(x.shape, F32),
+        lambda *refs: finish_kernel(heads, head_dim, natural, *refs),
+        name="finish",
+        grid=(steps,),
+        in_specs=[
+            rows_of(fc2), rows_of(out), rows_of(fc1) if natural else columns_of(fc1), columns_of(qkv)
+        ],
+        out_specs=[
+            rows_of(fc2),
+            rows_of(out),
+            pl.BlockSpec((fc1_shape[0] // steps, fc1_shape[1]), by_row),
+            pl.BlockSpec((depth // steps, 3, heads, head_dim), lambda i: (i, 0, 0, 0)),
+        ],
+        out_shape=[
+            shape(*fc2.shape), shape(*out.shape), shape(*fc1_shape), shape(depth, 3, heads, head_dim)
+        ],
         compiler_params=params("arbitrary"),
-        cost_estimate=cost(0, 6 * x.size),
-    )(x)
-
-
-def spread_kernel(heads, head_dim, in_ref, out_ref):
-    for head in range(heads):
-        block = in_ref[head * head_dim : (head + 1) * head_dim, :]
-        out_ref[:, 0, head, :] = block.T.astype(F32)
-
-
-def spread(stacked, heads, head_dim):
-    depth = stacked.shape[1]
-    block = min(1024, depth)
-    return pl.pallas_call(
-        lambda *refs: spread_kernel(heads, head_dim, *refs),
-        name="spread",
-        grid=(depth // block, 3),
-        in_specs=[pl.BlockSpec((heads * head_dim, block), lambda i, j: (j, i))],
-        out_specs=pl.BlockSpec((block, 1, heads, head_dim), lambda i, j: (i, j, 0, 0)),
-        out_shape=jax.ShapeDtypeStruct((depth, 3, heads, head_dim), F32),
-        compiler_params=params("arbitrary", "arbitrary"),
-        cost_estimate=cost(0, 6 * stacked.size),
-    )(stacked)
+        cost_estimate=cost(0, 6 * (fc2.size + out.size + fc1.size + qkv.size)),
+    )(fc2, out, fc1, qkv)
 
 
 def reduce_kernel(plan, dims, *refs):
@@ -830,7 +841,7 @@
     own_rows = down_own.shape[0]
     units = wide // deep
     zslots = zsend.shape[0]
-    begin = max(chunks // 2, blocks + 4)
+    begin = max(chunks // 2 + 3, blocks + 4)
 
     def z_copy(k, v, target):
         other = lax.rem(me + k, tensor)
@@ -1228,7 +1239,7 @@
     for size, right, fetched, local in shapes:
         plan.append((first, size // deep, right, fetched, local))
         first += size // deep
-    chunks, ring, slots, zslots = first, 4 * bits - 2, 4, 3
+    chunks, ring, slots, zslots = first, 2 * bits + 4, 4, 5
     blocks = 8 if chunks >= 20 else 4
     block = rows // blocks
     own_rows, units = rows // tensor, wide // deep
@@ -1346,12 +1357,12 @@
     for k in range(d_got.shape[0]):
         d_sum = d_sum + d_got[k].astype(F32)
         branch = branch + b_got[k].astype(F32)
-    fc2_grad, out_weight_grad, fc1_grad, qkv_weight_grad = stacked
     natural = hidden_width == model_width
-    fc2_grad = widened(fc2_grad)
-    out_weight_grad = out_weight_grad.astype(F32).reshape(heads, head_dim, model_width)
-    fc1_grad = widened(fc1_grad) if natural else fc1_grad.T.astype(F32)
-    qkv_weight_grad = jnp.transpose(spread(qkv_weight_grad, heads, head_dim), (0, 2, 1, 3))
+    fc2_grad, out_weight_grad, fc1_grad, qkv_weight_grad = finish(
+        *stacked, heads, head_dim, natural
+    )
+    out_weight_grad = out_weight_grad.reshape(heads, head_dim, model_width)
+    qkv_weight_grad = jnp.transpose(qkv_weight_grad, (0, 2, 1, 3))
     fc1_bias_grad = vectors[5, :hidden_width]
     qkv_bias_grad = vectors[6, : 3 * width].reshape(3, heads, head_dim)
     qkv_bias_grad = jnp.transpose(qkv_bias_grad, (1, 0, 2))

time: 546 us -> 502 us (0.919); the launches traced: 549 us -> 498 us
  Pallas kernels: 527 us -> 479 us
    pallas_call x1, Pallas kernels: 297 us -> 268 us  [reduce_grads(): pl.pallas_call(lambda *refs: reduce_kernel(plan, dims, *refs), name='redu...]
    pallas_call x1, Pallas kernels: 54.6 us -> 37.5 us  [attention(): pl.pallas_call(lambda *refs: attention_kernel(heads, head_dim, parts, bk,...]
    pallas_call x3 -> x1, Pallas kernels: 29.4 us -> 26.6 us  [finish(): pl.pallas_call(lambda *refs: finish_kernel(heads, head_dim, natural, *ref...]
where the time goes in v5:
time: 502 us; the launch traced here: 498 us
  Pallas kernels  479 us (95%)
  other arithmetic  11.6 us (2%)
  local copies, waits for them, and re-layouts  6.22 us (1%)
    pallas_call x1, Pallas kernels, reduce_grads(): pl.pallas_call(lambda *refs: reduce_kernel(plan, dims, *refs), name='redu...  268 us
    pallas_call x1, Pallas kernels, front(): pl.pallas_call(lambda *refs: front_kernel(sizes, *refs), name='front', in...  147 us
    pallas_call x1, Pallas kernels, attention(): pl.pallas_call(lambda *refs: attention_kernel(heads, head_dim, parts, bk,...  37.5 us
    pallas_call x1, Pallas kernels, finish(): pl.pallas_call(lambda *refs: finish_kernel(heads, head_dim, natural, *ref...  26.6 us

profile of v5, /device:TPU:11, one launch (start us, length us, event | category | flops | bytes accessed | tf_op | source)
XLA Modules:
  0.0 497.5 jit_solution(12575795886269209494)
XLA Ops:
  0.6 0.8 subtract_add_fusion
  1.4 1.9 fusion.12
  3.5 1.4 maximum_maximum_fusion
  4.9 0.6 reshape.113.refs_10_
  5.5 0.6 convert_element_type.96
  6.1 146.7 %front.1 = (bf16[1024,2048]{1,0:T(8,128)(2,1)}, bf16[1024,2048]{1,0:T(8,128)(2,1)}, bf16[2048,1536]{1,0:T(8,128)(2,1)}, bf16[1024,2048]{1,0:T(8,128)(2,1)}, bf16...) custom-call(bf16[256,2048]{1,0:T(8,128)(2,1)} %refs_0_.1, ...), custom_call_target="tpu_custom_call" | custom-call | flops 25769803776 | bytes 41943040 | tf_op jit(solution)/shard_map/front/pallas_call | solution.py:412
  152.8 1.1 copy.31.refs_3_
  153.9 0.1 slice.43
  154.0 0.5 and_select_fusion.refs_0_
  154.5 37.5 %attention.1 = (bf16[1024,512]{1,0:T(8,128)(2,1)}, f32[1024,512]{1,0:T(8,128)}, bf16[1024,1024]{1,0:T(8,128)(2,1)}, f32[1024,1024]{1,0:T(8,128)}, f32[1024,1024]{1,0:T(8,128)}) custom-call(s32[4]{0:T(128)} %and_select_fusion.refs_0_, bf16[1024,512]{1,0:T(8,128)(2,1)} %get-tuple-element.53.refs_1_, bf16[1024,512]{1,0:T(8,128)(2,1)} %get-tuple-element.54.refs_2_, ...), custom_call_target="tpu_custom_call" | custom-call | flops 12582912000 | bytes 12582912 | tf_op jit(solution)/shard_map/attention/pallas_call | solution.py:582
  192.0 0.2 convert_reduce_fusion.1
  192.2 0.6 pad.4.refs_16_
  192.8 268.2 %reduce_grads.1 = (bf16[2048,2048]{1,0:T(8,128)(2,1)}, bf16[512,2048]{1,0:T(8,128)(2,1)}, bf16[2048,2048]{1,0:T(8,128)(2,1)}, bf16[1536,2048]{1,0:T(8,128)(2,1)}...) custom-call(bf16[1024,2048]{1,0:T(8,128)(2,1)} %get-tuple-element.47, ...), custom_call_target="tpu_custom_call" | custom-call | flops 49392123904 | bytes 100663296 | tf_op jit(solution)/shard_map/reduce_grads/pallas_call | solution.py:1252
  461.0 26.6 %finish.1 = (f32[2048,2048]{1,0:T(8,128)}, f32[512,2048]{1,0:T(8,128)}, f32[2048,2048]{1,0:T(8,128)}, f32[2048,3,2,256]{3,2,1,0:T(2,128)}) custom-call(bf16[2048,2048]{1,0:T(8,128)(2,1)} %get-tuple-element.72.refs_0_, bf16[512,2048]{1,0:T(8,128)(2,1)} %get-tuple-element.73.refs_1_, bf16[2048,2048]{1,0:T(8,128)(2,1)} %get-tuple-element.74.refs_2_, ...), custom_call_target="tpu_custom_call" | custom-call | bytes 75497472 | tf_op jit(solution)/shard_map/finish/pallas_call | solution.py:638
  487.6 0.2 convert_reduce_fusion
  487.8 0.4 fusion.7
  488.2 0.9 copy-done.5
  489.2 2.9 fusion.13
  492.1 0.2 copy-done.3
  492.3 0.7 copy-done.4
  493.0 2.7 fusion.8
  495.7 0.6 fusion.14
  496.3 0.6 reshape_squeeze.3
  496.9 0.6 copy.33
  (34 shorter events, 0.3 us)
Async XLA Ops:
  1.4 3.5 copy-start.11
  1.4 4.1 copy-start.8
  154.5 37.5 %copy-start.1 = (bf16[256,2048]{1,0:T(8,128)(2,1)S(1)}, bf16[256,2048]{1,0:T(8,128)(2,1)}, u32[]{:S(2)}) copy-start(bf16[256,2048]{1,0:T(8,128)(2,1)} %refs_1_.1) | copy-start | bytes 3145732
  461.0 26.6 %copy-start = (bf16[256,2048]{1,0:T(8,128)(2,1)S(1)}, bf16[256,2048]{1,0:T(8,128)(2,1)}, u32[]{:S(2)}) copy-start(bf16[256,2048]{1,0:T(8,128)(2,1)} %refs_0_.1) | copy-start | bytes 3145732
  487.5 1.6 copy-start.5
  489.1 2.9 copy-start.9
  489.1 3.0 copy-start.10
  489.1 3.0 copy-start.2
  489.1 3.2 copy-start.3
  489.2 3.8 copy-start.4
  493.0 2.7 copy-start.6
  496.3 1.2 copy-start.7

commit v6 on v5

--- a/solution.py
+++ b/solution.py
@@ -616,7 +616,24 @@
 
 
 def finish_kernel(heads, head_dim, natural, *refs):
-    fc2_ref, out_ref, fc1_ref, qkv_ref, fc2_to, out_to, fc1_to, qkv_to = refs
+    fc2_ref, out_ref, fc1_ref, qkv_ref, x_ref, g_ref, d_ref, dgot_ref, b_ref, bgot_ref = refs[:10]
+    bias_ref, fc2_to, out_to, fc1_to, qkv_to, block_to, tokens_to = refs[10:]
+    x, grad, branch = x_ref[...].astype(F32), d_ref[...], b_ref[...]
+    for k in range(dgot_ref.shape[0]):
+        grad = grad + dgot_ref[k].astype(F32)
+        branch = branch + bgot_ref[k].astype(F32)
+    block_to[...] = (x + branch + bias_ref[0:1, :] + bias_ref[1:2, :]).astype(BF16)
+    average, inverse = moments(x)
+    standard = (x - average) * inverse
+    tokens_to[...] = (
+        g_ref[...].astype(F32)
+        + inverse
+        * (
+            grad
+            - jnp.mean(grad, -1, keepdims=True)
+            - standard * jnp.mean(grad * standard, -1, keepdims=True)
+        )
+    ).astype(BF16)
     fc2_to[...] = fc2_ref[...].astype(F32)
     out_to[...] = out_ref[...].astype(F32)
     fc1_to[...] = (fc1_ref[...] if natural else fc1_ref[...].T).astype(F32)
@@ -626,13 +643,14 @@
             qkv_to[:, part, head, :] = qkv_ref[at : at + head_dim, :].T.astype(F32)
 
 
-def finish(fc2, out, fc1, qkv, heads, head_dim, natural):
+def finish(fc2, out, fc1, qkv, x, g, d, d_got, b, b_got, biases, heads, head_dim, natural):
     depth = fc2.shape[1]
     steps = 8
     by_row = lambda i: (i, 0)
     by_column = lambda i: (0, i)
     rows_of = lambda x: pl.BlockSpec((x.shape[0] // steps, x.shape[1]), by_row)
     columns_of = lambda x: pl.BlockSpec((x.shape[0], depth // steps), by_column)
+    parts_of = lambda x: pl.BlockSpec((x.shape[0], x.shape[1] // steps, depth), lambda i: (0, i, 0))
     shape = lambda *dims: jax.ShapeDtypeStruct(dims, F32)
     fc1_shape = fc1.shape if natural else fc1.shape[::-1]
     return pl.pallas_call(
@@ -640,20 +658,25 @@
         name="finish",
         grid=(steps,),
         in_specs=[
-            rows_of(fc2), rows_of(out), rows_of(fc1) if natural else columns_of(fc1), columns_of(qkv)
+            rows_of(fc2), rows_of(out), rows_of(fc1) if natural else columns_of(fc1), columns_of(qkv),
+            rows_of(x), rows_of(g), rows_of(d), parts_of(d_got), rows_of(b), parts_of(b_got),
+            pl.BlockSpec(biases.shape, lambda i: (0, 0)),
         ],
         out_specs=[
             rows_of(fc2),
             rows_of(out),
             pl.BlockSpec((fc1_shape[0] // steps, fc1_shape[1]), by_row),
             pl.BlockSpec((depth // steps, 3, heads, head_dim), lambda i: (i, 0, 0, 0)),
+            rows_of(x),
+            rows_of(g),
         ],
         out_shape=[
-            shape(*fc2.shape), shape(*out.shape), shape(*fc1_shape), shape(depth, 3, heads, head_dim)
+            shape(*fc2.shape), shape(*out.shape), shape(*fc1_shape), shape(depth, 3, heads, head_dim),
+            jax.ShapeDtypeStruct(x.shape, BF16), jax.ShapeDtypeStruct(g.shape, BF16),
         ],
         compiler_params=params("arbitrary"),
         cost_estimate=cost(0, 6 * (fc2.size + out.size + fc1.size + qkv.size)),
-    )(fc2, out, fc1, qkv)
+    )(fc2, out, fc1, qkv, x, g, d, d_got, b, b_got, biases)
 
 
 def reduce_kernel(plan, dims, *refs):
@@ -1354,29 +1377,18 @@
         (fc1_weight, fc2_weight, flat_qkv, flat_out), rows_all,
         (bits, tensor, heads, head_dim),
     )
-    for k in range(d_got.shape[0]):
-        d_sum = d_sum + d_got[k].astype(F32)
-        branch = branch + b_got[k].astype(F32)
     natural = hidden_width == model_width
-    fc2_grad, out_weight_grad, fc1_grad, qkv_weight_grad = finish(
-        *stacked, heads, head_dim, natural
+    biases = jnp.stack([out_bias.astype(F32), fc2_bias.astype(F32)], 0)
+    fc2_grad, out_weight_grad, fc1_grad, qkv_weight_grad, block_out, tokens_grad = finish(
+        *stacked, tokens, out_grad, d_sum, d_got, branch, b_got, biases, heads, head_dim, natural
     )
     out_weight_grad = out_weight_grad.reshape(heads, head_dim, model_width)
     qkv_weight_grad = jnp.transpose(qkv_weight_grad, (0, 2, 1, 3))
     fc1_bias_grad = vectors[5, :hidden_width]
     qkv_bias_grad = vectors[6, : 3 * width].reshape(3, heads, head_dim)
     qkv_bias_grad = jnp.transpose(qkv_bias_grad, (1, 0, 2))
-    own_rows = tokens.astype(F32)
-    block_out = own_rows + branch + out_bias.astype(F32) + fc2_bias.astype(F32)
-    own_mean, own_inverse = moments(own_rows)
-    standard = (own_rows - own_mean) * own_inverse
-    tokens_grad = own_grad + own_inverse * (
-        d_sum
-        - jnp.mean(d_sum, -1, keepdims=True)
-        - standard * jnp.mean(d_sum * standard, -1, keepdims=True)
-    )
     return (
-        block_out.astype(BF16), tokens_grad.astype(BF16),
+        block_out, tokens_grad,
         vectors[0], vectors[1], vectors[2], vectors[3],
         qkv_weight_grad, qkv_bias_grad, out_weight_grad, vectors[4],
         fc1_grad, fc1_bias_grad, fc2_grad, vectors[4],

time: 502 us -> 498 us (level)
  other arithmetic: 11.6 us -> 5.96 us
where the time goes in v6:
time: 498 us; the launch traced here: 495 us
  Pallas kernels  484 us (97%)
  other arithmetic  5.96 us (1%)
    pallas_call x1, Pallas kernels, reduce_grads(): pl.pallas_call(lambda *refs: reduce_kernel(plan, dims, *refs), name='redu...  270 us
    pallas_call x1, Pallas kernels, front(): pl.pallas_call(lambda *refs: front_kernel(sizes, *refs), name='front', in...  147 us
    pallas_call x1, Pallas kernels, attention(): pl.pallas_call(lambda *refs: attention_kernel(heads, head_dim, parts, bk,...  37.5 us
    pallas_call x1, Pallas kernels, finish(): pl.pallas_call(lambda *refs: finish_kernel(heads, head_dim, natural, *ref...  30.3 us

profile of v6, /device:TPU:11, one launch (start us, length us, event | category | flops | bytes accessed | tf_op | source)
XLA Modules:
  0.0 495.2 jit_solution(7267352551889100831)
XLA Ops:
  0.6 0.0 copy-start.6
  0.7 0.0 copy-start.3
  0.7 0.8 subtract_add_fusion
  1.4 1.9 fusion
  3.4 0.1 pad.12.clone
  3.4 0.1 pad.9.clone
  3.5 1.4 maximum_maximum_fusion
  4.9 0.0 copy-done.6
  4.9 0.6 reshape.79.refs_10_
  5.5 0.6 convert_element_type.30
  6.1 146.7 %front.1 = (bf16[1024,2048]{1,0:T(8,128)(2,1)}, bf16[1024,2048]{1,0:T(8,128)(2,1)}, bf16[2048,1536]{1,0:T(8,128)(2,1)}, bf16[1024,2048]{1,0:T(8,128)(2,1)}, bf16...) custom-call(bf16[256,2048]{1,0:T(8,128)(2,1)} %refs_4_.5, ...), custom_call_target="tpu_custom_call" | custom-call | flops 25769803776 | bytes 41943040 | tf_op jit(solution)/shard_map/front/pallas_call | solution.py:412
  152.8 1.0 copy.31.refs_3_
  153.8 0.1 slice.25
  153.9 0.5 and_select_fusion.refs_0_
  154.5 37.5 %attention.1 = (bf16[1024,512]{1,0:T(8,128)(2,1)}, f32[1024,512]{1,0:T(8,128)}, bf16[1024,1024]{1,0:T(8,128)(2,1)}, f32[1024,1024]{1,0:T(8,128)}, f32[1024,1024]{1,0:T(8,128)}) custom-call(s32[4]{0:T(128)} %and_select_fusion.refs_0_, bf16[1024,512]{1,0:T(8,128)(2,1)} %get-tuple-element.55.refs_1_, bf16[1024,512]{1,0:T(8,128)(2,1)} %get-tuple-element.56.refs_2_, ...), custom_call_target="tpu_custom_call" | custom-call | flops 12582912000 | bytes 12582912 | tf_op jit(solution)/shard_map/attention/pallas_call | solution.py:582
  192.0 0.2 convert_reduce_fusion
  192.1 0.6 pad.4.refs_16_
  192.8 269.6 %reduce_grads.1 = (bf16[2048,2048]{1,0:T(8,128)(2,1)}, bf16[512,2048]{1,0:T(8,128)(2,1)}, bf16[2048,2048]{1,0:T(8,128)(2,1)}, bf16[1536,2048]{1,0:T(8,128)(2,1)}...) custom-call(bf16[1024,2048]{1,0:T(8,128)(2,1)} %get-tuple-element.49, ...), custom_call_target="tpu_custom_call" | custom-call | flops 49392123904 | bytes 100663296 | tf_op jit(solution)/shard_map/reduce_grads/pallas_call | solution.py:1275
  462.4 0.0 copy-done.5
  462.4 0.6 maximum_convert_fusion.refs_10_
  463.0 30.3 %finish.1 = (f32[2048,2048]{1,0:T(8,128)}, f32[512,2048]{1,0:T(8,128)}, f32[2048,2048]{1,0:T(8,128)}, f32[2048,3,2,256]{3,2,1,0:T(2,128)}, bf16[256,2048]{1,0:T(8,128)(2,1)}, /*index=5*/bf16[256,2048]{1,0:T(8,128)(2,1)}) custom-call(bf16[2048,2048]{1,0:T(8,128)(2,1)} %get-tuple-element.69.refs_0_, bf16[512,2048]{1,0:T(8,128)(2,1)} %get-tuple-element.70.refs_1_, ...), custom_call_target="tpu_custom_call" | custom-call | bytes 75497472 | tf_op jit(solution)/shard_map/finish/pallas_call | solution.py:656
  493.3 0.6 fusion.1
  494.0 0.6 reshape_squeeze.3
  494.6 0.6 copy.33
  (17 shorter events, 0.1 us)
Async XLA Ops:
  0.6 4.2 copy-start.6
  0.7 4.8 copy-start.3
  154.5 37.5 %copy-start = (bf16[256,2048]{1,0:T(8,128)(2,1)S(1)}, bf16[256,2048]{1,0:T(8,128)(2,1)}, u32[]{:S(2)}) copy-start(bf16[256,2048]{1,0:T(8,128)(2,1)} %refs_5_.1) | copy-start | bytes 3145732
  192.8 269.6 %copy-start.4 = (bf16[2048]{0:T(1024)(128)(2,1)S(1)}, bf16[2048]{0:T(1024)(128)(2,1)}, u32[]{:S(2)}) copy-start(bf16[2048]{0:T(1024)(128)(2,1)} %param.26) | copy-start | bytes 12292
  192.8 269.6 %copy-start.5 = (bf16[2048]{0:T(1024)(128)(2,1)S(1)}, bf16[2048]{0:T(1024)(128)(2,1)}, u32[]{:S(2)}) copy-start(bf16[2048]{0:T(1024)(128)(2,1)} %param.30) | copy-start | bytes 12292
  463.0 30.3 %copy-start.1 = (f32[8,2048]{1,0:T(8,128)S(1)}, f32[8,2048]{1,0:T(8,128)}, u32[]{:S(2)}) copy-start(f32[8,2048]{1,0:T(8,128)} %get-tuple-element.79) | copy-start | bytes 196612
  494.0 1.2 copy-start.2
